TPU v7x, 256 devices: a whole 4x4x8 slice. The times are simulated.
256 devices in a mesh: gx: 16 (over y, x), gy: 16 (over z, core).
Axes of the slice: x: 4, y: 4, z: 8, core: 2. Of those that a mesh axis runs over, the one named last changes fastest.
Arguments:
- right_side: float32 [9, 512, 2048], P(None, 'gx', 'gy'), may hold values from -16 to 16
- diag_blocks: float32 [9, 9, 512, 2048], P(None, None, 'gx', 'gy'), may hold values from -0.3 to 6, as said below
- couple_blocks: float32 [9, 9, 512, 2048], P(None, None, 'gx', 'gy'), may hold values from -0.15 to 1.5, as said below
- transmissibility: float32 [4, 512, 2048], P(None, 'gx', 'gy'), may hold values from 0.1 to 0.8
- pressure_weights: float32 [9, 512, 2048], P(None, 'gx', 'gy'), may hold values from 0.2 to 1
- well_mask: int32 [512, 2048], P('gx', 'gy'), may hold values 0 or 1
Outputs:
- solution: float32 [9, 512, 2048], P(None, 'gx', 'gy')
- estimate: float32 [], replicated
Inputs may be any that keep to these rules, and one draw needn't show every extreme that they name: `diag_blocks`: outside the first column, each block has diagonal entries from 4 to 6 and other entries within 0.3 in magnitude (within 0.05 in the first row); the first column is positive. `couple_blocks`: each block has first-column entries from 0.5 to 1.5, other diagonal entries from 0.6 to 1.2, and other entries within 0.15 in magnitude.
All inputs are finite; a program needn't handle non-finite values. No bound on the sum of `well_mask` on one device may be relied on, other than what follows from the above.
Results may differ from a plain program's by a relative error of at most 0.0003.
Values sent between devices are 32-bit elements; how exact they have to be, the bound alone decides.
No kernel may reach another device: no remote copies, remote signals or barrier semaphores. Data moves between devices by JAX's collectives and lax.ppermute only.
A program may use at most 64 MiB of HBM per device.

v0:
```python
import functools

import jax
import jax.numpy as jnp
from jax import lax
from jax.sharding import Mesh
from jax.sharding import PartitionSpec as P

NC = 9
GSTEPS = 2
LEVELS = 3
COARSE_SWEEPS = 6
GX_GY = ("gx_0", "gx_1", "gy_0", "gy_1")
GX = ("gx_0", "gx_1")
GY = ("gy_0", "gy_1")


relax_factor = 0.8
well_boost = 8.0


def extended(shard, sides, width):
    edges = {}
    for axis, dim in sides:
        peers, length = (lax.axis_size(axis), shard.shape[dim])
        up = [(i, (i + 1) % peers) for i in range(peers - 1)]
        last = lax.slice_in_dim(shard, length - width, length, axis=dim)
        initial = lax.slice_in_dim(shard, 0, width, axis=dim)
        edges[dim] = (
            lax.ppermute(last, axis, up),
            lax.ppermute(initial, axis, [(b, a) for a, b in up]),
        )
    done = []
    for _, dim in sides:
        low, high = edges[dim]
        around = [(width, width) if d in done else (0, 0) for d in range(shard.ndim)]
        shard = jnp.concatenate([jnp.pad(low, around), shard, jnp.pad(high, around)], axis=dim)
        done.append(dim)
    return shard


def by_axis(shard, axes):
    return functools.reduce(lax.psum, axes, shard)


def four_sides(padded):
    return (
        padded[..., 2:, 1:-1],
        padded[..., :-2, 1:-1],
        padded[..., 1:-1, 2:],
        padded[..., 1:-1, :-2],
    )


def block_padder(values):
    return extended(values, ((GX, 1), (GY, 2)), 1)


def level_padder(values):
    return extended(values, ((GX, 0), (GY, 1)), 1)


def apply_blocks(vector, eff_diag, couple_blocks, face_trans, padder):
    product = jnp.sum(couple_blocks * vector[None], axis=1)
    east_side, west_side, north_side, south_side = four_sides(padder(product))
    own_term = jnp.sum(eff_diag * vector[None], axis=1)
    return own_term - (
        face_trans[0] * east_side
        + face_trans[1] * west_side
        + face_trans[2] * north_side
        + face_trans[3] * south_side
    )


def level_apply(values, coeffs, padder):
    east_side, west_side, north_side, south_side = four_sides(padder(values))
    return coeffs[0] * values + (
        coeffs[1] * east_side
        + coeffs[2] * west_side
        + coeffs[3] * north_side
        + coeffs[4] * south_side
    )


def jacobi_sweep(iterate, source, coeffs, padder):
    return iterate + relax_factor * (source - level_apply(iterate, coeffs, padder)) / coeffs[0]


def coarse_sweeps(source, coeffs, padder):
    iterate = relax_factor * source / coeffs[0]
    for sweep_no in range(COARSE_SWEEPS - 1):
        iterate = jacobi_sweep(iterate, source, coeffs, padder)
    return iterate


def coarsen(coeffs):
    extent_x, extent_y = (coeffs.shape[1], coeffs.shape[2])
    grouped = coeffs.reshape(5, extent_x // 2, 2, extent_y // 2, 2)
    center_fine, east_fine, west_fine, north_fine, south_fine = (
        grouped[0],
        grouped[1],
        grouped[2],
        grouped[3],
        grouped[4],
    )
    center = (
        center_fine.sum(axis=(1, 3))
        + east_fine[:, 0].sum(axis=2)
        + west_fine[:, 1].sum(axis=2)
        + north_fine[:, :, :, 0].sum(axis=1)
        + south_fine[:, :, :, 1].sum(axis=1)
    )
    east_link = east_fine[:, 1].sum(axis=2)
    west_link = west_fine[:, 0].sum(axis=2)
    north_link = north_fine[:, :, :, 1].sum(axis=1)
    south_link = south_fine[:, :, :, 0].sum(axis=1)
    return jnp.stack([center, east_link, west_link, north_link, south_link])


def restrict(values):
    extent_x, extent_y = values.shape
    return values.reshape(extent_x // 2, 2, extent_y // 2, 2).sum(axis=(1, 3))


def prolong(values):
    return jnp.repeat(jnp.repeat(values, 2, axis=0), 2, axis=1)


def vcycle(source, hierarchy, padder, coarse_solve):
    if len(hierarchy) == 1:
        return coarse_solve(source, hierarchy[0])
    coeffs = hierarchy[0]
    iterate = relax_factor * source / coeffs[0]
    residue = source - level_apply(iterate, coeffs, padder)
    correction = vcycle(restrict(residue), hierarchy[1:], padder, coarse_solve)
    iterate = iterate + prolong(correction)
    return jacobi_sweep(iterate, source, coeffs, padder)


def block_inverse(matrix):
    extent = matrix.shape[0]
    identity = jnp.eye(extent, dtype=matrix.dtype)[:, :, None, None] * jnp.ones_like(matrix[0, 0])
    left_part, right_part = (matrix, identity)
    for pivot_row in range(extent):
        pivot_value = left_part[pivot_row, pivot_row]
        scaled_left = left_part[pivot_row] / pivot_value
        scaled_right = right_part[pivot_row] / pivot_value
        factor = left_part[:, pivot_row]
        left_part = left_part - factor[:, None] * scaled_left[None]
        right_part = right_part - factor[:, None] * scaled_right[None]
        left_part = left_part.at[pivot_row].set(scaled_left)
        right_part = right_part.at[pivot_row].set(scaled_right)
    return right_part


def pressure_coeffs(eff_diag, weights, face_trans, ghosts):

    def weighed(side_values):
        return jnp.sum(weights * side_values, axis=0)

    center = jnp.sum(weights * eff_diag[:, 0], axis=0)
    return jnp.stack(
        [
            center,
            -face_trans[0] * weighed(ghosts[0]),
            -face_trans[1] * weighed(ghosts[1]),
            -face_trans[2] * weighed(ghosts[2]),
            -face_trans[3] * weighed(ghosts[3]),
        ]
    )


def least_squares(start_norm, columns):
    steps_count = len(columns)
    rhs_list = [start_norm] + [jnp.zeros_like(start_norm)] * steps_count
    cosine_values, sine_values, upper_columns = ([], [], [])
    for column_no in range(steps_count):
        column = list(columns[column_no])
        for earlier in range(column_no):
            first_entry = column[earlier]
            second_entry = column[earlier + 1]
            column[earlier] = (
                cosine_values[earlier] * first_entry + sine_values[earlier] * second_entry
            )
            column[earlier + 1] = (
                -sine_values[earlier] * first_entry + cosine_values[earlier] * second_entry
            )
        radius = jnp.sqrt(
            column[column_no] * column[column_no] + column[column_no + 1] * column[column_no + 1]
        )
        cosine_value = column[column_no] / radius
        sine_value = column[column_no + 1] / radius
        column[column_no] = radius
        rhs_list[column_no + 1] = -sine_value * rhs_list[column_no]
        rhs_list[column_no] = cosine_value * rhs_list[column_no]
        cosine_values.append(cosine_value)
        sine_values.append(sine_value)
        upper_columns.append(column)
    coefficients = [None] * steps_count
    for row_no in reversed(range(steps_count)):
        running = rhs_list[row_no]
        for later_no in range(row_no + 1, steps_count):
            running = running - upper_columns[later_no][row_no] * coefficients[later_no]
        coefficients[row_no] = running / upper_columns[row_no][row_no]
    return (coefficients, jnp.abs(rhs_list[steps_count]))


def on_device(
    right_side, diag_blocks, couple_blocks, transmissibility, pressure_weights, well_mask
):
    identity = jnp.eye(NC, dtype=diag_blocks.dtype)[:, :, None, None]
    eff_diag = diag_blocks + well_boost * well_mask.astype(diag_blocks.dtype)[None, None] * identity
    inverse = block_inverse(eff_diag)
    ghost_padded = extended(couple_blocks[:, 0], ((GX, 1), (GY, 2)), 1)
    ghosts = four_sides(ghost_padded)
    hierarchy = [pressure_coeffs(eff_diag, pressure_weights, transmissibility, ghosts)]
    for level_no in range(LEVELS - 1):
        hierarchy.append(coarsen(hierarchy[-1]))

    def coarse_solve(source, coeffs):
        return coarse_sweeps(source, coeffs, level_padder)

    def apply_full(vector):
        return apply_blocks(vector, eff_diag, couple_blocks, transmissibility, block_padder)

    start_norm = jnp.sqrt(by_axis(jnp.sum(right_side * right_side), GX_GY))
    krylov_basis = [right_side / start_norm]
    directions, columns = ([], [])
    for step_no in range(GSTEPS):
        precondition_vector = krylov_basis[step_no]
        pressure_rhs = jnp.sum(pressure_weights * precondition_vector, axis=0)
        pressure = vcycle(pressure_rhs, hierarchy, level_padder, coarse_solve)
        lifted = jnp.concatenate(
            [pressure[None], jnp.zeros((NC - 1,) + pressure.shape, pressure.dtype)]
        )
        applied = apply_full(lifted)
        second = precondition_vector - applied
        direction = lifted + jnp.sum(inverse * second[None], axis=1)
        directions.append(direction)
        mapped = apply_full(direction)
        local_dots = jnp.stack(
            [jnp.sum(mapped * member) for member in krylov_basis] + [jnp.sum(mapped * mapped)]
        )
        summed = by_axis(local_dots, GX_GY)
        projections = [summed[member_no] for member_no in range(len(krylov_basis))]
        squared = summed[len(krylov_basis)]
        remainder = mapped
        for projection, member in zip(projections, krylov_basis):
            remainder = remainder - projection * member
            squared = squared - projection * projection
        length = jnp.sqrt(squared)
        krylov_basis.append(remainder / length)
        columns.append(projections + [length])
    coefficients, estimate = least_squares(start_norm, columns)
    solution = coefficients[0] * directions[0]
    step_no = 1
    solution = solution + coefficients[step_no] * directions[step_no]
    return (solution, estimate)


def solution(mesh):
    finer = Mesh(mesh.devices.reshape(4, 4, 8, 2), ("gx_0", "gx_1", "gy_0", "gy_1"))
    return jax.shard_map(
        on_device,
        mesh=finer,
        in_specs=(
            P(None, GX, GY),
            P(None, None, GX, GY),
            P(None, None, GX, GY),
            P(None, GX, GY),
            P(None, GX, GY),
            P(GX, GY),
        ),
        out_specs=(P(None, GX, GY), P()),
        check_vma=False,
    )
```

profile of v0, /device:TPU:1, one launch (start us, length us, event | category | flops | bytes accessed | tf_op | source)
XLA Modules:
  0.0 561.8 jit_solution(7733991794252343581)
XLA Ops:
  1.6 3.9 collective-permute-start.2
  7.6 4.4 collective-permute-start.6
  15.4 12.6 %psum.84 = f32[]{:T(128)} all-reduce(f32[]{:T(128)} %multiply_reduce_fusion.18), channel_id=1, replica_groups=mesh['gx_0'=4,'gx_1'=4,'gy_0'=8,'gy_1'=2] {'gx_0'}, use_global_device_ids=true, to_apply=%region_1.0 | all-reduce | flops 1 | bytes 8 | tf_op jit(solution)/shard_map/psum | solution.py:43
  28.1 7.0 %psum.85 = f32[]{:T(128)} all-reduce(f32[]{:T(128)} %psum.84), channel_id=1, replica_groups=mesh['gx_0'=4,'gx_1'=4,'gy_0'=8,'gy_1'=2] {'gx_1'}, use_global_device_ids=true, to_apply=%region_2.0 | all-reduce | flops 1 | bytes 8 | tf_op jit(solution)/shard_map/psum | solution.py:43
  37.4 15.4 %psum.86 = f32[]{:T(128)} all-reduce(f32[]{:T(128)} %psum.85), channel_id=1, replica_groups=mesh['gx_0'=4,'gx_1'=4,'gy_0'=8,'gy_1'=2] {'gy_0'}, use_global_device_ids=true, to_apply=%region_3.0 | all-reduce | flops 1 | bytes 8 | tf_op jit(solution)/shard_map/psum | solution.py:43
  53.4 12.3 %psum.87 = f32[]{:T(128)} all-reduce(f32[]{:T(128)} %psum.86), channel_id=1, replica_groups=mesh['gx_0'=4,'gx_1'=4,'gy_0'=8,'gy_1'=2] {'gy_1'}, use_global_device_ids=true, to_apply=%region_4.0 | all-reduce | flops 1 | bytes 8 | tf_op jit(solution)/shard_map/psum | solution.py:43
  70.4 2.0 neg.58
  74.4 3.0 collective-permute-start.3
  78.7 2.5 collective-permute-start.5
  81.2 3.0 collective-permute-start.7
  84.3 2.0 reduce_sum.428
  86.3 2.0 reduce_sum.426
  96.0 2.0 reduce_sum.422
  106.2 4.6 collective-permute-start.9
  113.9 3.8 collective-permute-start.11
  122.2 4.0 collective-permute-start.13
  129.4 4.5 collective-permute-start.15
  134.8 4.3 collective-permute-start.17
  142.3 4.5 collective-permute-start.19
  147.7 4.3 collective-permute-start.21
  155.2 4.5 collective-permute-start.23
  160.6 4.3 collective-permute-start.25
  168.1 4.5 collective-permute-start.27
  173.5 6.3 %collective-permute-start.29 = (f32[1,32]{1,0:T(1,128)S(1)}, f32[1,32]{1,0:T(1,128)S(1)}, u32[]{:S(2)}, u32[]{:S(2)}) collective-permute-start(f32[1,32]{1,0:T(1,128)S(1)} %get-tuple-element.385), channel_id=1, source_target_pairs={{0,16},{16,32},{32,48},{48,64},{64,80},{80,96},{96,112},{112,128},... | collective-permute-start | bytes 392 | tf_op jit(solution)/shard_map/ppermute | solution.py:30
  183.0 4.5 collective-permute-start.31
  188.5 6.4 %collective-permute-start.33 = (f32[1,64]{1,0:T(1,128)S(1)}, f32[1,64]{1,0:T(1,128)S(1)}, u32[]{:S(2)}, u32[]{:S(2)}) collective-permute-start(f32[1,64]{1,0:T(1,128)S(1)} %get-tuple-element.357), channel_id=1, source_target_pairs={{0,16},{16,32},{32,48},{48,64},{64,80},{80,96},{96,112},{112,128},... | collective-permute-start | bytes 776 | tf_op jit(solution)/shard_map/ppermute | solution.py:30
  198.2 4.5 collective-permute-start.35
  204.5 6.4 %collective-permute-start.37 = (f32[1,128]{1,0:T(1,128)S(1)}, f32[1,128]{1,0:T(1,128)S(1)}, u32[]{:S(2)}, u32[]{:S(2)}) collective-permute-start(f32[1,128]{1,0:T(1,128)S(1)} %get-tuple-element.311), channel_id=1, source_target_pairs={{0,16},{16,32},{32,48},{48,64},{64,80},{80,96},{96,112},{112,128},... | collective-permute-start | bytes 1544 | tf_op jit(solution)/shard_map/ppermute | solution.py:30
  214.1 4.5 collective-permute-start.39
  225.9 6.4 %collective-permute-start.41 = (f32[9,1,128]{2,1,0:T(1,128)S(1)}, f32[9,1,128]{2,1,0:T(1,128)S(1)}, u32[]{:S(2)}, u32[]{:S(2)}) collective-permute-start(f32[9,1,128]{2,1,0:T(1,128)S(1)} %get-tuple-element.273), channel_id=1, source_target_pairs={{0,16},{16,32},{32,48},{48,64},{64,80},{80,96},{96,112},{112,128},... | collective-permute-start | bytes 13832 | tf_op jit(solution)/shard_map/ppermute | solution.py:30
  235.5 4.5 collective-permute-start.43
  243.0 6.4 %collective-permute-start.45 = (f32[9,1,128]{2,1,0:T(1,128)S(1)}, f32[9,1,128]{2,1,0:T(1,128)S(1)}, u32[]{:S(2)}, u32[]{:S(2)}) collective-permute-start(f32[9,1,128]{2,1,0:T(1,128)S(1)} %get-tuple-element.269), channel_id=1, source_target_pairs={{0,16},{16,32},{32,48},{48,64},{64,80},{80,96},{96,112},{112,128},... | collective-permute-start | bytes 13832 | tf_op jit(solution)/shard_map/ppermute | solution.py:30
  252.8 4.7 collective-permute-start.47
  261.8 18.9 %psum.88 = f32[2]{0:T(128)S(1)} all-reduce(f32[2]{0:T(128)S(1)} %pad_maximum_fusion.138), channel_id=1, replica_groups=mesh['gx_0'=4,'gx_1'=4,'gy_0'=8,'gy_1'=2] {'gx_0'}, use_global_device_ids=true, to_apply=%region_38.39 | all-reduce | flops 2 | bytes 16 | tf_op jit(solution)/shard_map/psum | solution.py:43
  280.8 6.0 %psum.89 = f32[2]{0:T(128)S(1)} all-reduce(f32[2]{0:T(128)S(1)} %psum.88), channel_id=1, replica_groups=mesh['gx_0'=4,'gx_1'=4,'gy_0'=8,'gy_1'=2] {'gx_1'}, use_global_device_ids=true, to_apply=%region_39.40 | all-reduce | flops 2 | bytes 16 | tf_op jit(solution)/shard_map/psum | solution.py:43
  286.8 23.5 %psum.90 = f32[2]{0:T(128)S(1)} all-reduce(f32[2]{0:T(128)S(1)} %psum.89), channel_id=1, replica_groups=mesh['gx_0'=4,'gx_1'=4,'gy_0'=8,'gy_1'=2] {'gy_0'}, use_global_device_ids=true, to_apply=%region_40.41 | all-reduce | flops 2 | bytes 16 | tf_op jit(solution)/shard_map/psum | solution.py:43
  310.2 10.8 %psum.91 = f32[2]{0:T(128)S(1)} all-reduce(f32[2]{0:T(128)S(1)} %psum.90), channel_id=1, replica_groups=mesh['gx_0'=4,'gx_1'=4,'gy_0'=8,'gy_1'=2] {'gy_1'}, use_global_device_ids=true, to_apply=%region_41.42 | all-reduce | flops 2 | bytes 16 | tf_op jit(solution)/shard_map/psum | solution.py:43
  325.5 3.6 collective-permute-start.49
  330.5 2.5 collective-permute-start.50
  333.0 3.2 collective-permute-start.51
  341.5 4.3 collective-permute-start.53
  349.0 4.5 collective-permute-start.55
  356.6 4.3 collective-permute-start.57
  364.0 4.5 collective-permute-start.59
  369.5 4.3 collective-permute-start.61
  377.0 4.7 collective-permute-start.63
  382.3 4.3 collective-permute-start.65
  389.8 4.5 collective-permute-start.67
  395.2 5.0 collective-permute-start.69
  403.4 4.5 collective-permute-start.71
  408.8 6.4 %collective-permute-start.73 = (f32[1,32]{1,0:T(1,128)S(1)}, f32[1,32]{1,0:T(1,128)S(1)}, u32[]{:S(2)}, u32[]{:S(2)}) collective-permute-start(f32[1,32]{1,0:T(1,128)S(1)} %get-tuple-element.365), channel_id=1, source_target_pairs={{0,16},{16,32},{32,48},{48,64},{64,80},{80,96},{96,112},{112,128},... | collective-permute-start | bytes 392 | tf_op jit(solution)/shard_map/ppermute | solution.py:30
  418.4 4.5 collective-permute-start.75
  424.0 6.4 %collective-permute-start.77 = (f32[1,64]{1,0:T(1,128)S(1)}, f32[1,64]{1,0:T(1,128)S(1)}, u32[]{:S(2)}, u32[]{:S(2)}) collective-permute-start(f32[1,64]{1,0:T(1,128)S(1)} %get-tuple-element.349), channel_id=1, source_target_pairs={{0,16},{16,32},{32,48},{48,64},{64,80},{80,96},{96,112},{112,128},... | collective-permute-start | bytes 776 | tf_op jit(solution)/shard_map/ppermute | solution.py:30
  433.6 4.5 collective-permute-start.79
  439.2 6.4 %collective-permute-start.81 = (f32[1,128]{1,0:T(1,128)S(1)}, f32[1,128]{1,0:T(1,128)S(1)}, u32[]{:S(2)}, u32[]{:S(2)}) collective-permute-start(f32[1,128]{1,0:T(1,128)S(1)} %get-tuple-element.303), channel_id=1, source_target_pairs={{0,16},{16,32},{32,48},{48,64},{64,80},{80,96},{96,112},{112,128},... | collective-permute-start | bytes 1544 | tf_op jit(solution)/shard_map/ppermute | solution.py:30
  448.8 4.5 collective-permute-start.83
  454.8 6.5 %collective-permute-start.85 = (f32[9,1,128]{2,1,0:T(1,128)S(1)}, f32[9,1,128]{2,1,0:T(1,128)S(1)}, u32[]{:S(2)}, u32[]{:S(2)}) collective-permute-start(f32[9,1,128]{2,1,0:T(1,128)S(1)} %get-tuple-element.265), channel_id=1, source_target_pairs={{0,16},{16,32},{32,48},{48,64},{64,80},{80,96},{96,112},{112,128},... | collective-permute-start | bytes 13832 | tf_op jit(solution)/shard_map/ppermute | solution.py:30
  464.6 4.5 collective-permute-start.87
  472.4 6.4 %collective-permute-start.89 = (f32[9,1,128]{2,1,0:T(1,128)S(1)}, f32[9,1,128]{2,1,0:T(1,128)S(1)}, u32[]{:S(2)}, u32[]{:S(2)}) collective-permute-start(f32[9,1,128]{2,1,0:T(1,128)S(1)} %get-tuple-element.261), channel_id=1, source_target_pairs={{0,16},{16,32},{32,48},{48,64},{64,80},{80,96},{96,112},{112,128},... | collective-permute-start | bytes 13832 | tf_op jit(solution)/shard_map/ppermute | solution.py:30
  482.1 4.7 collective-permute-start.91
  493.1 18.8 %psum.92 = f32[3]{0:T(128)S(1)} all-reduce(f32[3]{0:T(128)S(1)} %pad_maximum_fusion.139), channel_id=1, replica_groups=mesh['gx_0'=4,'gx_1'=4,'gy_0'=8,'gy_1'=2] {'gx_0'}, use_global_device_ids=true, to_apply=%region_53.54 | all-reduce | flops 3 | bytes 24 | tf_op jit(solution)/shard_map/psum | solution.py:43
  511.9 6.0 %psum.93 = f32[3]{0:T(128)S(1)} all-reduce(f32[3]{0:T(128)S(1)} %psum.92), channel_id=1, replica_groups=mesh['gx_0'=4,'gx_1'=4,'gy_0'=8,'gy_1'=2] {'gx_1'}, use_global_device_ids=true, to_apply=%region_54.55 | all-reduce | flops 3 | bytes 24 | tf_op jit(solution)/shard_map/psum | solution.py:43
  517.9 24.9 %psum.94 = f32[3]{0:T(128)S(1)} all-reduce(f32[3]{0:T(128)S(1)} %psum.93), channel_id=1, replica_groups=mesh['gx_0'=4,'gx_1'=4,'gy_0'=8,'gy_1'=2] {'gy_0'}, use_global_device_ids=true, to_apply=%region_55.56 | all-reduce | flops 3 | bytes 24 | tf_op jit(solution)/shard_map/psum | solution.py:43
  542.8 10.8 %psum.95 = f32[3]{0:T(128)S(1)} all-reduce(f32[3]{0:T(128)S(1)} %psum.94), channel_id=1, replica_groups=mesh['gx_0'=4,'gx_1'=4,'gy_0'=8,'gy_1'=2] {'gy_1'}, use_global_device_ids=true, to_apply=%region_56.57 | all-reduce | flops 3 | bytes 24 | tf_op jit(solution)/shard_map/psum | solution.py:43
  (443 shorter events, 150.7 us)
Async XLA Ops:
  1.6 70.8 %collective-permute-start.2 = (f32[9,1,128]{2,1,0:T(1,128)S(1)}, f32[9,1,128]{2,1,0:T(1,128)S(1)}, u32[]{:S(2)}, u32[]{:S(2)}) collective-permute-start(f32[9,1,128]{2,1,0:T(1,128)S(1)} %get-tuple-element.277), channel_id=1, source_target_pairs={{0,16},{16,32},{32,48},{48,64},{64,80},{80,96},{96,112},{112,128},... | collective-permute-start | bytes 13832 | tf_op jit(solution)/shard_map/ppermute | solution.py:30
  5.5 67.6 %collective-permute-start = (f32[9,1,128]{2,1,0:T(1,128)S(1)}, f32[9,1,128]{2,1,0:T(1,128)S(1)}, u32[]{:S(2)}, u32[]{:S(2)}) collective-permute-start(f32[9,1,128]{2,1,0:T(1,128)S(1)} %get-tuple-element.278), channel_id=1, source_target_pairs={{16,0},{32,16},{48,32},{64,48},{80,64},{96,80},{112,96},{128,112},... | collective-permute-start | bytes 13832 | tf_op jit(solution)/shard_map/ppermute | solution.py:31
  7.6 64.8 %collective-permute-start.6 = (f32[9,32,1]{2,1,0:T(8,128)}, f32[9,32,1]{2,1,0:T(8,128)S(1)}, u32[]{:S(2)}, u32[]{:S(2)}) collective-permute-start(f32[9,32,1]{2,1,0:T(8,128)} %get-tuple-element.275), channel_id=1, source_target_pairs={{0,1},{1,2},{2,3},{3,4},{4,5},{5,6},{6,7},{7,8},{8,9},{9,10},{10,1... | collective-permute-start | bytes 3464 | tf_op jit(solution)/shard_map/ppermute | solution.py:30
  13.5 58.9 %collective-permute-start.4 = (f32[9,32,1]{2,1,0:T(8,128)}, f32[9,32,1]{2,1,0:T(8,128)S(1)}, u32[]{:S(2)}, u32[]{:S(2)}) collective-permute-start(f32[9,32,1]{2,1,0:T(8,128)} %get-tuple-element.276), channel_id=1, source_target_pairs={{1,0},{2,1},{3,2},{4,3},{5,4},{6,5},{7,6},{8,7},{9,8},{10,9},{11,1... | collective-permute-start | bytes 3464 | tf_op jit(solution)/shard_map/ppermute | solution.py:31
  74.4 29.2 %collective-permute-start.3 = (f32[1,128]{1,0:T(1,128)S(1)}, f32[1,128]{1,0:T(1,128)S(1)}, u32[]{:S(2)}, u32[]{:S(2)}) collective-permute-start(f32[1,128]{1,0:T(1,128)S(1)} %get-tuple-element.315), channel_id=1, source_target_pairs={{0,16},{16,32},{32,48},{48,64},{64,80},{80,96},{96,112},{112,128},... | collective-permute-start | bytes 1544 | tf_op jit(solution)/shard_map/ppermute | solution.py:30
  77.4 26.2 %collective-permute-start.1 = (f32[1,128]{1,0:T(1,128)S(1)}, f32[1,128]{1,0:T(1,128)S(1)}, u32[]{:S(2)}, u32[]{:S(2)}) collective-permute-start(f32[1,128]{1,0:T(1,128)S(1)} %get-tuple-element.316), channel_id=1, source_target_pairs={{16,0},{32,16},{48,32},{64,48},{80,64},{96,80},{112,96},{128,112},... | collective-permute-start | bytes 1544 | tf_op jit(solution)/shard_map/ppermute | solution.py:31
  78.7 24.8 %collective-permute-start.5 = (f32[32,1]{1,0:T(8,128)S(1)}, f32[32,1]{1,0:T(8,128)S(1)}, u32[]{:S(2)}, u32[]{:S(2)}) collective-permute-start(f32[32,1]{1,0:T(8,128)S(1)} %get-tuple-element.313), channel_id=1, source_target_pairs={{1,0},{2,1},{3,2},{4,3},{5,4},{6,5},{7,6},{8,7},{9,8},{10,9},{11,1... | collective-permute-start | bytes 392 | tf_op jit(solution)/shard_map/ppermute | solution.py:31
  81.2 22.3 %collective-permute-start.7 = (f32[32,1]{1,0:T(8,128)S(1)}, f32[32,1]{1,0:T(8,128)S(1)}, u32[]{:S(2)}, u32[]{:S(2)}) collective-permute-start(f32[32,1]{1,0:T(8,128)S(1)} %get-tuple-element.314), channel_id=1, source_target_pairs={{0,1},{1,2},{2,3},{3,4},{4,5},{5,6},{6,7},{7,8},{8,9},{9,10},{10,1... | collective-permute-start | bytes 392 | tf_op jit(solution)/shard_map/ppermute | solution.py:30
  106.2 12.6 %collective-permute-start.9 = (f32[1,64]{1,0:T(1,128)S(1)}, f32[1,64]{1,0:T(1,128)}, u32[]{:S(2)}, u32[]{:S(2)}) collective-permute-start(f32[1,64]{1,0:T(1,128)S(1)} %get-tuple-element.361), channel_id=1, source_target_pairs={{0,16},{16,32},{32,48},{48,64},{64,80},{80,96},{96,112},{112,128},... | collective-permute-start | bytes 776 | tf_op jit(solution)/shard_map/ppermute | solution.py:30
  110.7 8.1 %collective-permute-start.8 = (f32[1,64]{1,0:T(1,128)S(1)}, f32[1,64]{1,0:T(1,128)}, u32[]{:S(2)}, u32[]{:S(2)}) collective-permute-start(f32[1,64]{1,0:T(1,128)S(1)} %get-tuple-element.362), channel_id=1, source_target_pairs={{16,0},{32,16},{48,32},{64,48},{80,64},{96,80},{112,96},{128,112},... | collective-permute-start | bytes 776 | tf_op jit(solution)/shard_map/ppermute | solution.py:31
  112.0 6.8 %collective-permute-start.10 = (f32[16,1]{1,0:T(8,128)}, f32[16,1]{1,0:T(8,128)}, u32[]{:S(2)}, u32[]{:S(2)}) collective-permute-start(f32[16,1]{1,0:T(8,128)} %get-tuple-element.359), channel_id=1, source_target_pairs={{1,0},{2,1},{3,2},{4,3},{5,4},{6,5},{7,6},{8,7},{9,8},{10,9},{11,1... | collective-permute-start | bytes 200 | tf_op jit(solution)/shard_map/ppermute | solution.py:31
  122.2 12.5 %collective-permute-start.13 = (f32[1,32]{1,0:T(1,128)S(1)}, f32[1,32]{1,0:T(1,128)S(1)}, u32[]{:S(2)}, u32[]{:S(2)}) collective-permute-start(f32[1,32]{1,0:T(1,128)S(1)} %get-tuple-element.401), channel_id=1, source_target_pairs={{0,16},{16,32},{32,48},{48,64},{64,80},{80,96},{96,112},{112,128},... | collective-permute-start | bytes 392 | tf_op jit(solution)/shard_map/ppermute | solution.py:30
  126.2 8.5 %collective-permute-start.12 = (f32[1,32]{1,0:T(1,128)S(1)}, f32[1,32]{1,0:T(1,128)S(1)}, u32[]{:S(2)}, u32[]{:S(2)}) collective-permute-start(f32[1,32]{1,0:T(1,128)S(1)} %get-tuple-element.402), channel_id=1, source_target_pairs={{16,0},{32,16},{48,32},{64,48},{80,64},{96,80},{112,96},{128,112},... | collective-permute-start | bytes 392 | tf_op jit(solution)/shard_map/ppermute | solution.py:31
  127.5 6.5 %collective-permute-start.14 = (f32[8,1]{1,0:T(8,128)S(1)}, f32[8,1]{1,0:T(8,128)S(1)}, u32[]{:S(2)}, u32[]{:S(2)}) collective-permute-start(f32[8,1]{1,0:T(8,128)S(1)} %get-tuple-element.399), channel_id=1, source_target_pairs={{1,0},{2,1},{3,2},{4,3},{5,4},{6,5},{7,6},{8,7},{9,8},{10,9},{11,1... | collective-permute-start | bytes 104 | tf_op jit(solution)/shard_map/ppermute | solution.py:31
  134.8 12.7 %collective-permute-start.17 = (f32[1,32]{1,0:T(1,128)S(1)}, f32[1,32]{1,0:T(1,128)S(1)}, u32[]{:S(2)}, u32[]{:S(2)}) collective-permute-start(f32[1,32]{1,0:T(1,128)S(1)} %get-tuple-element.397), channel_id=1, source_target_pairs={{0,16},{16,32},{32,48},{48,64},{64,80},{80,96},{96,112},{112,128},... | collective-permute-start | bytes 392 | tf_op jit(solution)/shard_map/ppermute | solution.py:30
  139.1 8.4 %collective-permute-start.16 = (f32[1,32]{1,0:T(1,128)S(1)}, f32[1,32]{1,0:T(1,128)S(1)}, u32[]{:S(2)}, u32[]{:S(2)}) collective-permute-start(f32[1,32]{1,0:T(1,128)S(1)} %get-tuple-element.398), channel_id=1, source_target_pairs={{16,0},{32,16},{48,32},{64,48},{80,64},{96,80},{112,96},{128,112},... | collective-permute-start | bytes 392 | tf_op jit(solution)/shard_map/ppermute | solution.py:31
  147.7 12.7 %collective-permute-start.21 = (f32[1,32]{1,0:T(1,128)S(1)}, f32[1,32]{1,0:T(1,128)S(1)}, u32[]{:S(2)}, u32[]{:S(2)}) collective-permute-start(f32[1,32]{1,0:T(1,128)S(1)} %get-tuple-element.393), channel_id=1, source_target_pairs={{0,16},{16,32},{32,48},{48,64},{64,80},{80,96},{96,112},{112,128},... | collective-permute-start | bytes 392 | tf_op jit(solution)/shard_map/ppermute | solution.py:30
  152.0 8.4 %collective-permute-start.20 = (f32[1,32]{1,0:T(1,128)S(1)}, f32[1,32]{1,0:T(1,128)S(1)}, u32[]{:S(2)}, u32[]{:S(2)}) collective-permute-start(f32[1,32]{1,0:T(1,128)S(1)} %get-tuple-element.394), channel_id=1, source_target_pairs={{16,0},{32,16},{48,32},{64,48},{80,64},{96,80},{112,96},{128,112},... | collective-permute-start | bytes 392 | tf_op jit(solution)/shard_map/ppermute | solution.py:31
  160.6 12.7 %collective-permute-start.25 = (f32[1,32]{1,0:T(1,128)S(1)}, f32[1,32]{1,0:T(1,128)S(1)}, u32[]{:S(2)}, u32[]{:S(2)}) collective-permute-start(f32[1,32]{1,0:T(1,128)S(1)} %get-tuple-element.389), channel_id=1, source_target_pairs={{0,16},{16,32},{32,48},{48,64},{64,80},{80,96},{96,112},{112,128},... | collective-permute-start | bytes 392 | tf_op jit(solution)/shard_map/ppermute | solution.py:30
  164.9 8.4 %collective-permute-start.24 = (f32[1,32]{1,0:T(1,128)S(1)}, f32[1,32]{1,0:T(1,128)S(1)}, u32[]{:S(2)}, u32[]{:S(2)}) collective-permute-start(f32[1,32]{1,0:T(1,128)S(1)} %get-tuple-element.390), channel_id=1, source_target_pairs={{16,0},{32,16},{48,32},{64,48},{80,64},{96,80},{112,96},{128,112},... | collective-permute-start | bytes 392 | tf_op jit(solution)/shard_map/ppermute | solution.py:31
  173.5 14.7 %collective-permute-start.29 = (f32[1,32]{1,0:T(1,128)S(1)}, f32[1,32]{1,0:T(1,128)S(1)}, u32[]{:S(2)}, u32[]{:S(2)}) collective-permute-start(f32[1,32]{1,0:T(1,128)S(1)} %get-tuple-element.385), channel_id=1, source_target_pairs={{0,16},{16,32},{32,48},{48,64},{64,80},{80,96},{96,112},{112,128},... | collective-permute-start | bytes 392 | tf_op jit(solution)/shard_map/ppermute | solution.py:30
  179.7 8.4 %collective-permute-start.28 = (f32[1,32]{1,0:T(1,128)S(1)}, f32[1,32]{1,0:T(1,128)S(1)}, u32[]{:S(2)}, u32[]{:S(2)}) collective-permute-start(f32[1,32]{1,0:T(1,128)S(1)} %get-tuple-element.386), channel_id=1, source_target_pairs={{16,0},{32,16},{48,32},{64,48},{80,64},{96,80},{112,96},{128,112},... | collective-permute-start | bytes 392 | tf_op jit(solution)/shard_map/ppermute | solution.py:31
  188.5 14.9 %collective-permute-start.33 = (f32[1,64]{1,0:T(1,128)S(1)}, f32[1,64]{1,0:T(1,128)S(1)}, u32[]{:S(2)}, u32[]{:S(2)}) collective-permute-start(f32[1,64]{1,0:T(1,128)S(1)} %get-tuple-element.357), channel_id=1, source_target_pairs={{0,16},{16,32},{32,48},{48,64},{64,80},{80,96},{96,112},{112,128},... | collective-permute-start | bytes 776 | tf_op jit(solution)/shard_map/ppermute | solution.py:30
  194.9 8.5 %collective-permute-start.32 = (f32[1,64]{1,0:T(1,128)S(1)}, f32[1,64]{1,0:T(1,128)S(1)}, u32[]{:S(2)}, u32[]{:S(2)}) collective-permute-start(f32[1,64]{1,0:T(1,128)S(1)} %get-tuple-element.358), channel_id=1, source_target_pairs={{16,0},{32,16},{48,32},{64,48},{80,64},{96,80},{112,96},{128,112},... | collective-permute-start | bytes 776 | tf_op jit(solution)/shard_map/ppermute | solution.py:31
  204.5 14.9 %collective-permute-start.37 = (f32[1,128]{1,0:T(1,128)S(1)}, f32[1,128]{1,0:T(1,128)S(1)}, u32[]{:S(2)}, u32[]{:S(2)}) collective-permute-start(f32[1,128]{1,0:T(1,128)S(1)} %get-tuple-element.311), channel_id=1, source_target_pairs={{0,16},{16,32},{32,48},{48,64},{64,80},{80,96},{96,112},{112,128},... | collective-permute-start | bytes 1544 | tf_op jit(solution)/shard_map/ppermute | solution.py:30
  210.9 8.6 %collective-permute-start.36 = (f32[1,128]{1,0:T(1,128)S(1)}, f32[1,128]{1,0:T(1,128)S(1)}, u32[]{:S(2)}, u32[]{:S(2)}) collective-permute-start(f32[1,128]{1,0:T(1,128)S(1)} %get-tuple-element.312), channel_id=1, source_target_pairs={{16,0},{32,16},{48,32},{64,48},{80,64},{96,80},{112,96},{128,112},... | collective-permute-start | bytes 1544 | tf_op jit(solution)/shard_map/ppermute | solution.py:31
  212.2 7.2 %collective-permute-start.38 = (f32[32,1]{1,0:T(8,128)S(1)}, f32[32,1]{1,0:T(8,128)S(1)}, u32[]{:S(2)}, u32[]{:S(2)}) collective-permute-start(f32[32,1]{1,0:T(8,128)S(1)} %get-tuple-element.309), channel_id=1, source_target_pairs={{1,0},{2,1},{3,2},{4,3},{5,4},{6,5},{7,6},{8,7},{9,8},{10,9},{11,1... | collective-permute-start | bytes 392 | tf_op jit(solution)/shard_map/ppermute | solution.py:31
  225.9 16.2 %collective-permute-start.41 = (f32[9,1,128]{2,1,0:T(1,128)S(1)}, f32[9,1,128]{2,1,0:T(1,128)S(1)}, u32[]{:S(2)}, u32[]{:S(2)}) collective-permute-start(f32[9,1,128]{2,1,0:T(1,128)S(1)} %get-tuple-element.273), channel_id=1, source_target_pairs={{0,16},{16,32},{32,48},{48,64},{64,80},{80,96},{96,112},{112,128},... | collective-permute-start | bytes 13832 | tf_op jit(solution)/shard_map/ppermute | solution.py:30
  232.3 9.8 %collective-permute-start.40 = (f32[9,1,128]{2,1,0:T(1,128)S(1)}, f32[9,1,128]{2,1,0:T(1,128)S(1)}, u32[]{:S(2)}, u32[]{:S(2)}) collective-permute-start(f32[9,1,128]{2,1,0:T(1,128)S(1)} %get-tuple-element.274), channel_id=1, source_target_pairs={{16,0},{32,16},{48,32},{64,48},{80,64},{96,80},{112,96},{128,112},... | collective-permute-start | bytes 13832 | tf_op jit(solution)/shard_map/ppermute | solution.py:31
  233.6 7.3 %collective-permute-start.42 = (f32[9,32,1]{2,1,0:T(8,128)S(1)}, f32[9,32,1]{2,1,0:T(8,128)S(1)}, u32[]{:S(2)}, u32[]{:S(2)}) collective-permute-start(f32[9,32,1]{2,1,0:T(8,128)S(1)} %get-tuple-element.271), channel_id=1, source_target_pairs={{1,0},{2,1},{3,2},{4,3},{5,4},{6,5},{7,6},{8,7},{9,8},{10,9},{11,1... | collective-permute-start | bytes 3464 | tf_op jit(solution)/shard_map/ppermute | solution.py:31
  235.5 6.6 %collective-permute-start.43 = (f32[9,32,1]{2,1,0:T(8,128)S(1)}, f32[9,32,1]{2,1,0:T(8,128)S(1)}, u32[]{:S(2)}, u32[]{:S(2)}) collective-permute-start(f32[9,32,1]{2,1,0:T(8,128)S(1)} %get-tuple-element.272), channel_id=1, source_target_pairs={{0,1},{1,2},{2,3},{3,4},{4,5},{5,6},{6,7},{7,8},{8,9},{9,10},{10,1... | collective-permute-start | bytes 3464 | tf_op jit(solution)/shard_map/ppermute | solution.py:30
  243.0 16.5 %collective-permute-start.45 = (f32[9,1,128]{2,1,0:T(1,128)S(1)}, f32[9,1,128]{2,1,0:T(1,128)S(1)}, u32[]{:S(2)}, u32[]{:S(2)}) collective-permute-start(f32[9,1,128]{2,1,0:T(1,128)S(1)} %get-tuple-element.269), channel_id=1, source_target_pairs={{0,16},{16,32},{32,48},{48,64},{64,80},{80,96},{96,112},{112,128},... | collective-permute-start | bytes 13832 | tf_op jit(solution)/shard_map/ppermute | solution.py:30
  249.4 10.1 %collective-permute-start.44 = (f32[9,1,128]{2,1,0:T(1,128)S(1)}, f32[9,1,128]{2,1,0:T(1,128)S(1)}, u32[]{:S(2)}, u32[]{:S(2)}) collective-permute-start(f32[9,1,128]{2,1,0:T(1,128)S(1)} %get-tuple-element.270), channel_id=1, source_target_pairs={{16,0},{32,16},{48,32},{64,48},{80,64},{96,80},{112,96},{128,112},... | collective-permute-start | bytes 13832 | tf_op jit(solution)/shard_map/ppermute | solution.py:31
  250.8 7.5 %collective-permute-start.46 = (f32[9,32,1]{2,1,0:T(8,128)S(1)}, f32[9,32,1]{2,1,0:T(8,128)S(1)}, u32[]{:S(2)}, u32[]{:S(2)}) collective-permute-start(f32[9,32,1]{2,1,0:T(8,128)S(1)} %get-tuple-element.267), channel_id=1, source_target_pairs={{1,0},{2,1},{3,2},{4,3},{5,4},{6,5},{7,6},{8,7},{9,8},{10,9},{11,1... | collective-permute-start | bytes 3464 | tf_op jit(solution)/shard_map/ppermute | solution.py:31
  252.8 6.7 %collective-permute-start.47 = (f32[9,32,1]{2,1,0:T(8,128)S(1)}, f32[9,32,1]{2,1,0:T(8,128)S(1)}, u32[]{:S(2)}, u32[]{:S(2)}) collective-permute-start(f32[9,32,1]{2,1,0:T(8,128)S(1)} %get-tuple-element.268), channel_id=1, source_target_pairs={{0,1},{1,2},{2,3},{3,4},{4,5},{5,6},{6,7},{7,8},{8,9},{9,10},{10,1... | collective-permute-start | bytes 3464 | tf_op jit(solution)/shard_map/ppermute | solution.py:30
  325.5 11.6 %collective-permute-start.49 = (f32[1,128]{1,0:T(1,128)S(1)}, f32[1,128]{1,0:T(1,128)S(1)}, u32[]{:S(2)}, u32[]{:S(2)}) collective-permute-start(f32[1,128]{1,0:T(1,128)S(1)} %get-tuple-element.307), channel_id=1, source_target_pairs={{0,16},{16,32},{32,48},{48,64},{64,80},{80,96},{96,112},{112,128},... | collective-permute-start | bytes 1544 | tf_op jit(solution)/shard_map/ppermute | solution.py:30
  329.1 7.9 %collective-permute-start.48 = (f32[1,128]{1,0:T(1,128)S(1)}, f32[1,128]{1,0:T(1,128)S(1)}, u32[]{:S(2)}, u32[]{:S(2)}) collective-permute-start(f32[1,128]{1,0:T(1,128)S(1)} %get-tuple-element.308), channel_id=1, source_target_pairs={{16,0},{32,16},{48,32},{64,48},{80,64},{96,80},{112,96},{128,112},... | collective-permute-start | bytes 1544 | tf_op jit(solution)/shard_map/ppermute | solution.py:31
  341.5 12.8 %collective-permute-start.53 = (f32[1,64]{1,0:T(1,128)S(1)}, f32[1,64]{1,0:T(1,128)S(1)}, u32[]{:S(2)}, u32[]{:S(2)}) collective-permute-start(f32[1,64]{1,0:T(1,128)S(1)} %get-tuple-element.353), channel_id=1, source_target_pairs={{0,16},{16,32},{32,48},{48,64},{64,80},{80,96},{96,112},{112,128},... | collective-permute-start | bytes 776 | tf_op jit(solution)/shard_map/ppermute | solution.py:30
  345.8 8.5 %collective-permute-start.52 = (f32[1,64]{1,0:T(1,128)S(1)}, f32[1,64]{1,0:T(1,128)S(1)}, u32[]{:S(2)}, u32[]{:S(2)}) collective-permute-start(f32[1,64]{1,0:T(1,128)S(1)} %get-tuple-element.354), channel_id=1, source_target_pairs={{16,0},{32,16},{48,32},{64,48},{80,64},{96,80},{112,96},{128,112},... | collective-permute-start | bytes 776 | tf_op jit(solution)/shard_map/ppermute | solution.py:31
  347.1 6.4 %collective-permute-start.54 = (f32[16,1]{1,0:T(8,128)S(1)}, f32[16,1]{1,0:T(8,128)S(1)}, u32[]{:S(2)}, u32[]{:S(2)}) collective-permute-start(f32[16,1]{1,0:T(8,128)S(1)} %get-tuple-element.351), channel_id=1, source_target_pairs={{1,0},{2,1},{3,2},{4,3},{5,4},{6,5},{7,6},{8,7},{9,8},{10,9},{11,1... | collective-permute-start | bytes 200 | tf_op jit(solution)/shard_map/ppermute | solution.py:31
  356.6 12.7 %collective-permute-start.57 = (f32[1,32]{1,0:T(1,128)S(1)}, f32[1,32]{1,0:T(1,128)S(1)}, u32[]{:S(2)}, u32[]{:S(2)}) collective-permute-start(f32[1,32]{1,0:T(1,128)S(1)} %get-tuple-element.381), channel_id=1, source_target_pairs={{0,16},{16,32},{32,48},{48,64},{64,80},{80,96},{96,112},{112,128},... | collective-permute-start | bytes 392 | tf_op jit(solution)/shard_map/ppermute | solution.py:30
  360.8 8.4 %collective-permute-start.56 = (f32[1,32]{1,0:T(1,128)S(1)}, f32[1,32]{1,0:T(1,128)S(1)}, u32[]{:S(2)}, u32[]{:S(2)}) collective-permute-start(f32[1,32]{1,0:T(1,128)S(1)} %get-tuple-element.382), channel_id=1, source_target_pairs={{16,0},{32,16},{48,32},{64,48},{80,64},{96,80},{112,96},{128,112},... | collective-permute-start | bytes 392 | tf_op jit(solution)/shard_map/ppermute | solution.py:31
  362.1 6.4 %collective-permute-start.58 = (f32[8,1]{1,0:T(8,128)S(1)}, f32[8,1]{1,0:T(8,128)S(1)}, u32[]{:S(2)}, u32[]{:S(2)}) collective-permute-start(f32[8,1]{1,0:T(8,128)S(1)} %get-tuple-element.379), channel_id=1, source_target_pairs={{1,0},{2,1},{3,2},{4,3},{5,4},{6,5},{7,6},{8,7},{9,8},{10,9},{11,1... | collective-permute-start | bytes 104 | tf_op jit(solution)/shard_map/ppermute | solution.py:31
  369.5 12.7 %collective-permute-start.61 = (f32[1,32]{1,0:T(1,128)S(1)}, f32[1,32]{1,0:T(1,128)S(1)}, u32[]{:S(2)}, u32[]{:S(2)}) collective-permute-start(f32[1,32]{1,0:T(1,128)S(1)} %get-tuple-element.377), channel_id=1, source_target_pairs={{0,16},{16,32},{32,48},{48,64},{64,80},{80,96},{96,112},{112,128},... | collective-permute-start | bytes 392 | tf_op jit(solution)/shard_map/ppermute | solution.py:30
  373.7 8.4 %collective-permute-start.60 = (f32[1,32]{1,0:T(1,128)S(1)}, f32[1,32]{1,0:T(1,128)S(1)}, u32[]{:S(2)}, u32[]{:S(2)}) collective-permute-start(f32[1,32]{1,0:T(1,128)S(1)} %get-tuple-element.378), channel_id=1, source_target_pairs={{16,0},{32,16},{48,32},{64,48},{80,64},{96,80},{112,96},{128,112},... | collective-permute-start | bytes 392 | tf_op jit(solution)/shard_map/ppermute | solution.py:31
  375.0 6.6 %collective-permute-start.62 = (f32[8,1]{1,0:T(8,128)S(1)}, f32[8,1]{1,0:T(8,128)S(1)}, u32[]{:S(2)}, u32[]{:S(2)}) collective-permute-start(f32[8,1]{1,0:T(8,128)S(1)} %get-tuple-element.375), channel_id=1, source_target_pairs={{1,0},{2,1},{3,2},{4,3},{5,4},{6,5},{7,6},{8,7},{9,8},{10,9},{11,1... | collective-permute-start | bytes 104 | tf_op jit(solution)/shard_map/ppermute | solution.py:31
  382.3 12.7 %collective-permute-start.65 = (f32[1,32]{1,0:T(1,128)S(1)}, f32[1,32]{1,0:T(1,128)S(1)}, u32[]{:S(2)}, u32[]{:S(2)}) collective-permute-start(f32[1,32]{1,0:T(1,128)S(1)} %get-tuple-element.373), channel_id=1, source_target_pairs={{0,16},{16,32},{32,48},{48,64},{64,80},{80,96},{96,112},{112,128},... | collective-permute-start | bytes 392 | tf_op jit(solution)/shard_map/ppermute | solution.py:30
  386.6 8.4 %collective-permute-start.64 = (f32[1,32]{1,0:T(1,128)S(1)}, f32[1,32]{1,0:T(1,128)S(1)}, u32[]{:S(2)}, u32[]{:S(2)}) collective-permute-start(f32[1,32]{1,0:T(1,128)S(1)} %get-tuple-element.374), channel_id=1, source_target_pairs={{16,0},{32,16},{48,32},{64,48},{80,64},{96,80},{112,96},{128,112},... | collective-permute-start | bytes 392 | tf_op jit(solution)/shard_map/ppermute | solution.py:31
  395.2 13.4 %collective-permute-start.69 = (f32[1,32]{1,0:T(1,128)S(1)}, f32[1,32]{1,0:T(1,128)S(1)}, u32[]{:S(2)}, u32[]{:S(2)}) collective-permute-start(f32[1,32]{1,0:T(1,128)S(1)} %get-tuple-element.369), channel_id=1, source_target_pairs={{0,16},{16,32},{32,48},{48,64},{64,80},{80,96},{96,112},{112,128},... | collective-permute-start | bytes 392 | tf_op jit(solution)/shard_map/ppermute | solution.py:30
  400.2 8.4 %collective-permute-start.68 = (f32[1,32]{1,0:T(1,128)S(1)}, f32[1,32]{1,0:T(1,128)S(1)}, u32[]{:S(2)}, u32[]{:S(2)}) collective-permute-start(f32[1,32]{1,0:T(1,128)S(1)} %get-tuple-element.370), channel_id=1, source_target_pairs={{16,0},{32,16},{48,32},{64,48},{80,64},{96,80},{112,96},{128,112},... | collective-permute-start | bytes 392 | tf_op jit(solution)/shard_map/ppermute | solution.py:31
  408.8 14.8 %collective-permute-start.73 = (f32[1,32]{1,0:T(1,128)S(1)}, f32[1,32]{1,0:T(1,128)S(1)}, u32[]{:S(2)}, u32[]{:S(2)}) collective-permute-start(f32[1,32]{1,0:T(1,128)S(1)} %get-tuple-element.365), channel_id=1, source_target_pairs={{0,16},{16,32},{32,48},{48,64},{64,80},{80,96},{96,112},{112,128},... | collective-permute-start | bytes 392 | tf_op jit(solution)/shard_map/ppermute | solution.py:30
  415.2 8.4 %collective-permute-start.72 = (f32[1,32]{1,0:T(1,128)S(1)}, f32[1,32]{1,0:T(1,128)S(1)}, u32[]{:S(2)}, u32[]{:S(2)}) collective-permute-start(f32[1,32]{1,0:T(1,128)S(1)} %get-tuple-element.366), channel_id=1, source_target_pairs={{16,0},{32,16},{48,32},{64,48},{80,64},{96,80},{112,96},{128,112},... | collective-permute-start | bytes 392 | tf_op jit(solution)/shard_map/ppermute | solution.py:31
  424.0 14.9 %collective-permute-start.77 = (f32[1,64]{1,0:T(1,128)S(1)}, f32[1,64]{1,0:T(1,128)S(1)}, u32[]{:S(2)}, u32[]{:S(2)}) collective-permute-start(f32[1,64]{1,0:T(1,128)S(1)} %get-tuple-element.349), channel_id=1, source_target_pairs={{0,16},{16,32},{32,48},{48,64},{64,80},{80,96},{96,112},{112,128},... | collective-permute-start | bytes 776 | tf_op jit(solution)/shard_map/ppermute | solution.py:30
  430.4 8.5 %collective-permute-start.76 = (f32[1,64]{1,0:T(1,128)S(1)}, f32[1,64]{1,0:T(1,128)S(1)}, u32[]{:S(2)}, u32[]{:S(2)}) collective-permute-start(f32[1,64]{1,0:T(1,128)S(1)} %get-tuple-element.350), channel_id=1, source_target_pairs={{16,0},{32,16},{48,32},{64,48},{80,64},{96,80},{112,96},{128,112},... | collective-permute-start | bytes 776 | tf_op jit(solution)/shard_map/ppermute | solution.py:31
  439.2 15.0 %collective-permute-start.81 = (f32[1,128]{1,0:T(1,128)S(1)}, f32[1,128]{1,0:T(1,128)S(1)}, u32[]{:S(2)}, u32[]{:S(2)}) collective-permute-start(f32[1,128]{1,0:T(1,128)S(1)} %get-tuple-element.303), channel_id=1, source_target_pairs={{0,16},{16,32},{32,48},{48,64},{64,80},{80,96},{96,112},{112,128},... | collective-permute-start | bytes 1544 | tf_op jit(solution)/shard_map/ppermute | solution.py:30
  445.6 8.6 %collective-permute-start.80 = (f32[1,128]{1,0:T(1,128)S(1)}, f32[1,128]{1,0:T(1,128)S(1)}, u32[]{:S(2)}, u32[]{:S(2)}) collective-permute-start(f32[1,128]{1,0:T(1,128)S(1)} %get-tuple-element.304), channel_id=1, source_target_pairs={{16,0},{32,16},{48,32},{64,48},{80,64},{96,80},{112,96},{128,112},... | collective-permute-start | bytes 1544 | tf_op jit(solution)/shard_map/ppermute | solution.py:31
  454.8 16.4 %collective-permute-start.85 = (f32[9,1,128]{2,1,0:T(1,128)S(1)}, f32[9,1,128]{2,1,0:T(1,128)S(1)}, u32[]{:S(2)}, u32[]{:S(2)}) collective-permute-start(f32[9,1,128]{2,1,0:T(1,128)S(1)} %get-tuple-element.265), channel_id=1, source_target_pairs={{0,16},{16,32},{32,48},{48,64},{64,80},{80,96},{96,112},{112,128},... | collective-permute-start | bytes 13832 | tf_op jit(solution)/shard_map/ppermute | solution.py:30
  461.3 9.9 %collective-permute-start.84 = (f32[9,1,128]{2,1,0:T(1,128)S(1)}, f32[9,1,128]{2,1,0:T(1,128)S(1)}, u32[]{:S(2)}, u32[]{:S(2)}) collective-permute-start(f32[9,1,128]{2,1,0:T(1,128)S(1)} %get-tuple-element.266), channel_id=1, source_target_pairs={{16,0},{32,16},{48,32},{64,48},{80,64},{96,80},{112,96},{128,112},... | collective-permute-start | bytes 13832 | tf_op jit(solution)/shard_map/ppermute | solution.py:31
  462.7 7.3 %collective-permute-start.86 = (f32[9,32,1]{2,1,0:T(8,128)S(1)}, f32[9,32,1]{2,1,0:T(8,128)S(1)}, u32[]{:S(2)}, u32[]{:S(2)}) collective-permute-start(f32[9,32,1]{2,1,0:T(8,128)S(1)} %get-tuple-element.263), channel_id=1, source_target_pairs={{1,0},{2,1},{3,2},{4,3},{5,4},{6,5},{7,6},{8,7},{9,8},{10,9},{11,1... | collective-permute-start | bytes 3464 | tf_op jit(solution)/shard_map/ppermute | solution.py:31
  464.6 6.6 %collective-permute-start.87 = (f32[9,32,1]{2,1,0:T(8,128)S(1)}, f32[9,32,1]{2,1,0:T(8,128)S(1)}, u32[]{:S(2)}, u32[]{:S(2)}) collective-permute-start(f32[9,32,1]{2,1,0:T(8,128)S(1)} %get-tuple-element.264), channel_id=1, source_target_pairs={{0,1},{1,2},{2,3},{3,4},{4,5},{5,6},{6,7},{7,8},{8,9},{9,10},{10,1... | collective-permute-start | bytes 3464 | tf_op jit(solution)/shard_map/ppermute | solution.py:30
  472.4 16.5 %collective-permute-start.89 = (f32[9,1,128]{2,1,0:T(1,128)S(1)}, f32[9,1,128]{2,1,0:T(1,128)S(1)}, u32[]{:S(2)}, u32[]{:S(2)}) collective-permute-start(f32[9,1,128]{2,1,0:T(1,128)S(1)} %get-tuple-element.261), channel_id=1, source_target_pairs={{0,16},{16,32},{32,48},{48,64},{64,80},{80,96},{96,112},{112,128},... | collective-permute-start | bytes 13832 | tf_op jit(solution)/shard_map/ppermute | solution.py:30
  478.8 10.1 %collective-permute-start.88 = (f32[9,1,128]{2,1,0:T(1,128)S(1)}, f32[9,1,128]{2,1,0:T(1,128)S(1)}, u32[]{:S(2)}, u32[]{:S(2)}) collective-permute-start(f32[9,1,128]{2,1,0:T(1,128)S(1)} %get-tuple-element.262), channel_id=1, source_target_pairs={{16,0},{32,16},{48,32},{64,48},{80,64},{96,80},{112,96},{128,112},... | collective-permute-start | bytes 13832 | tf_op jit(solution)/shard_map/ppermute | solution.py:31
  480.2 7.5 %collective-permute-start.90 = (f32[9,32,1]{2,1,0:T(8,128)S(1)}, f32[9,32,1]{2,1,0:T(8,128)S(1)}, u32[]{:S(2)}, u32[]{:S(2)}) collective-permute-start(f32[9,32,1]{2,1,0:T(8,128)S(1)} %get-tuple-element.259), channel_id=1, source_target_pairs={{1,0},{2,1},{3,2},{4,3},{5,4},{6,5},{7,6},{8,7},{9,8},{10,9},{11,1... | collective-permute-start | bytes 3464 | tf_op jit(solution)/shard_map/ppermute | solution.py:31
  482.1 6.7 %collective-permute-start.91 = (f32[9,32,1]{2,1,0:T(8,128)S(1)}, f32[9,32,1]{2,1,0:T(8,128)S(1)}, u32[]{:S(2)}, u32[]{:S(2)}) collective-permute-start(f32[9,32,1]{2,1,0:T(8,128)S(1)} %get-tuple-element.260), channel_id=1, source_target_pairs={{0,1},{1,2},{2,3},{3,4},{4,5},{5,6},{6,7},{7,8},{8,9},{9,10},{10,1... | collective-permute-start | bytes 3464 | tf_op jit(solution)/shard_map/ppermute | solution.py:30
  (85 other events, 3721.0 us)
where the time goes:
time: 566 us; the launch traced here: 562 us
  starting transfers between devices  293 us (52%)
  blocking collectives  167 us (30%)
  other arithmetic  40.5 us (7%)
  local copies, waits for them, and re-layouts  29 us (5%)
  waiting for transfers between devices  19.2 us (3%)
  between operations  13.4 us (2%)
    ppermute x46, starting transfers between devices, extended(): lax.ppermute(last, axis, up)  218 us
    psum x12, blocking collectives, by_axis(): return functools.reduce(lax.psum, axes, shard)  167 us
    ppermute x46, starting transfers between devices, extended(): lax.ppermute(initial, axis, [(b, a) for a, b in up])  75.1 us
    ppermute x46, waiting for transfers between devices, extended(): lax.ppermute(last, axis, up)  15.8 us
  transfers between devices with their start and end apart: 92, of which 23 were waited for; matrix products, arithmetic and copies ran while one was open for 6% of the time, Pallas kernels for 0%

commit v1 on v0

v1 whole, which is shorter than its diff:
```python
import functools

import jax
import jax.numpy as jnp
from jax import lax
from jax.experimental import pallas as pl
from jax.experimental.pallas import tpu as pltpu
from jax.sharding import PartitionSpec as P

NC = 9
COARSE_SWEEPS = 6
RELAX = 0.8
WELL_BOOST = 8.0

R, L = 32, 128
HALO = 32
EX, EY = 3 * R, 2 * L

AX_EDGE = 6 * R
AX_COL = AX_EDGE + 24
AX_ROWS = AX_COL + R
AY_ROWS = 2 * EX
BX_EDGE = R
BX_COL = BX_EDGE + 16
BX_ROWS = BX_COL + R

CENTER, EAST, WEST, NORTH, SOUTH, SCALE = range(6)


def iotas(shape):
    return (lax.broadcasted_iota(jnp.int32, shape, 0), lax.broadcasted_iota(jnp.int32, shape, 1))


def shifted(values, axis, step):
    return pltpu.roll(values, (-step) % values.shape[axis], axis)


def lane_roll(values, shift):
    shift = shift % values.shape[1]
    return values if shift == 0 else pltpu.roll(values, shift, 1)


def even_mask(par_ref, which, shape):
    return jnp.full(shape, par_ref[which], jnp.int32) == 0


def put(par_ref, which, first, second, rows, up, down):
    even = even_mask(par_ref, which, up.shape)
    first[rows, :] = jnp.where(even, up, down)
    second[rows, :] = jnp.where(even, down, up)


def take(par_ref, which, first, second, rows):
    one, two = (first[rows, :], second[rows, :])
    even = even_mask(par_ref, which, one.shape)
    return (jnp.where(even, one, two), jnp.where(even, two, one))


def pack_columns(parts):
    shape = parts[0][0].shape
    lanes = iotas(shape)[1]
    packed = jnp.zeros(shape, jnp.float32)
    for values, lane, target in parts:
        packed = jnp.where(lanes == target, lane_roll(values, target - lane), packed)
    return packed


def setup_kernel(par, rhs, diag0, couple0, trans, weights, wells, msg1, msg2, own, cols):
    rows, lanes = iotas((R, L))
    center = WELL_BOOST * wells[...].astype(jnp.float32) * weights[0]
    pressure = jnp.zeros((R, L), jnp.float32)
    links = [jnp.zeros((R, L), jnp.float32) for _ in range(4)]
    for c in range(NC):
        w, col = (weights[c], couple0[c, 0])
        center = center + w * diag0[c, 0]
        pressure = pressure + w * rhs[c]
        for d, (axis, step) in enumerate(((0, 1), (0, -1), (1, 1), (1, -1))):
            links[d] = links[d] + w * shifted(col, axis, step)
    inside = (rows != R - 1, rows != 0, lanes != L - 1, lanes != 0)
    fields = [center]
    for d in range(4):
        fields.append(jnp.where(inside[d], -trans[d] * links[d], 0.0))
    fields.append(pressure)
    for k, field in enumerate(fields):
        span = pl.ds(k * R, R)
        own[span, :] = field
        msg1[span, :] = field
        msg2[span, :] = field
    t_up, t_down = (trans[0, R - 1 : R, :], trans[1, 0:1, :])
    t_right, t_left = (trans[2], trans[3])
    for c in range(NC):
        put(par, 0, msg1, msg2, pl.ds(AX_EDGE + c, 1), couple0[c, 0, R - 1 : R, :], couple0[c, 0, 0:1, :])
        put(par, 0, msg1, msg2, pl.ds(AX_EDGE + NC + c, 1), t_up * weights[c, R - 1 : R, :], t_down * weights[c, 0:1, :])
    blank = jnp.zeros((24 - 2 * NC, L), jnp.float32)
    msg1[pl.ds(AX_EDGE + 2 * NC, 24 - 2 * NC), :] = blank
    msg2[pl.ds(AX_EDGE + 2 * NC, 24 - 2 * NC), :] = blank
    parts = []
    for c in range(NC):
        col, w = (couple0[c, 0], weights[c])
        parts += [(col, 0, c), (t_left * w, 0, NC + c), (col, L - 1, 2 * NC + c), (t_right * w, L - 1, 3 * NC + c)]
    packed = pack_columns(parts)
    cols[...] = packed
    msg1[pl.ds(AX_COL, R), :] = packed
    msg2[pl.ds(AX_COL, R), :] = packed


def inverse_kernel(diag, wells, out):
    boost = WELL_BOOST * wells[...].astype(jnp.float32)
    a = [[diag[i, j] + boost if i == j else diag[i, j] for j in range(NC)] for i in range(NC)]
    for k in range(NC):
        inv = 1.0 / a[k][k]
        a[k] = [inv if j == k else a[k][j] * inv for j in range(NC)]
        for i in range(NC):
            if i != k:
                factor = a[i][k]
                a[i] = [-factor * inv if j == k else a[i][j] - factor * a[k][j] for j in range(NC)]
    for i in range(NC):
        for j in range(NC):
            out[i, j] = a[i][j]


def setup_middle_kernel(par, got1, got2, own, cols, couple0, trans, weights, msg1, msg2, ext, ext_cols, edges):
    rows, lanes = iotas((EX, L))

    def dots(span_of):
        total = jnp.zeros((1, L), jnp.float32)
        for c in range(NC):
            total = total + span_of(c)
        return -total

    ups, downs, tw_ups, tw_downs = ([], [], [], [])
    for c in range(NC):
        up, down = take(par, 0, got1, got2, pl.ds(AX_EDGE + c, 1))
        ups.append(up)
        downs.append(down)
        up, down = take(par, 0, got1, got2, pl.ds(AX_EDGE + NC + c, 1))
        tw_ups.append(up)
        tw_downs.append(down)
        edges[pl.ds(c, 1), :] = ups[c]
        edges[pl.ds(NC + c, 1), :] = downs[c]
        edges[pl.ds(2 * NC + c, 1), :] = tw_ups[c]
        edges[pl.ds(3 * NC + c, 1), :] = tw_downs[c]
    t_up, t_down = (trans[0, R - 1 : R, :], trans[1, 0:1, :])
    east_own = dots(lambda c: t_up * weights[c, R - 1 : R, :] * ups[c])
    west_own = dots(lambda c: t_down * weights[c, 0:1, :] * downs[c])
    west_up = dots(lambda c: tw_ups[c] * couple0[c, 0, R - 1 : R, :])
    east_down = dots(lambda c: tw_downs[c] * couple0[c, 0, 0:1, :])
    fields = []
    for k in range(6):
        up, down = take(par, 0, got1, got2, pl.ds(k * R, R))
        field = jnp.concatenate([own[pl.ds(k * R, R), :], up, down], axis=0)
        if k == CENTER:
            field = jnp.where(field == 0.0, 1.0, field)
        if k == EAST:
            field = jnp.where(rows == R - 1, east_own, jnp.where(rows == EX - 1, east_down, field))
        if k == WEST:
            field = jnp.where(rows == 0, west_own, jnp.where(rows == R, west_up, field))
        ext[k] = field
        fields.append(field)
    up, down = take(par, 0, got1, got2, pl.ds(AX_COL, R))
    packed = jnp.concatenate([cols[...], up, down], axis=0)
    ext_cols[...] = packed
    to_right = [lane_roll(f, HALO * (k % 4) + HALO) for k, f in enumerate(fields)]
    to_left = [lane_roll(f, HALO * (k % 4)) for k, f in enumerate(fields)]
    group = lanes // HALO

    def quad(parts):
        result = parts[-1]
        for g in range(len(parts) - 2, -1, -1):
            result = jnp.where(group == g, parts[g], result)
        return result

    put(par, 1, msg1, msg2, pl.ds(0, EX), quad(to_right[:4]), quad(to_left[:4]))
    put(
        par,
        1,
        msg1,
        msg2,
        pl.ds(EX, EX),
        quad(to_right[4:] + [lane_roll(packed, 64 - 2 * NC)]),
        quad(to_left[4:] + [lane_roll(packed, 64)]),
    )


def lane_sum(product, start):
    lanes = iotas(product.shape)[1]
    keep = jnp.logical_and(lanes >= start, lanes < start + NC)
    return jnp.sum(jnp.where(keep, product, 0.0), axis=1, keepdims=True)


def pair_sums(values, step):
    rows, lanes = iotas(values.shape)
    values = values + jnp.where((rows // step) % 2 == 0, shifted(values, 0, step), shifted(values, 0, -step))
    return values + jnp.where((lanes // step) % 2 == 0, shifted(values, 1, step), shifted(values, 1, -step))


def coarsen_into(coeffs, level):
    step = 2**level
    base, out = (6 * level, 6 * level + 6)
    rows, lanes = iotas((EX, EY))
    row_even = (rows // step) % 2 == 0
    lane_even = (lanes // step) % 2 == 0
    east, west, north, south = (coeffs[base + d] for d in (EAST, WEST, NORTH, SOUTH))
    center = coeffs[base] + (jnp.where(row_even, east, west) + jnp.where(lane_even, north, south))
    center = pair_sums(center, step)
    coeffs[out + CENTER] = center
    coeffs[out + SCALE] = RELAX / center
    coeffs[out + EAST] = pair_sums(jnp.where(row_even, 0.0, east), step)
    coeffs[out + WEST] = pair_sums(jnp.where(row_even, west, 0.0), step)
    coeffs[out + NORTH] = pair_sums(jnp.where(lane_even, 0.0, north), step)
    coeffs[out + SOUTH] = pair_sums(jnp.where(lane_even, south, 0.0), step)


def level_apply(values, coeffs, level):
    step = 2**level
    base = 6 * level
    return coeffs[base + CENTER] * values + (
        coeffs[base + EAST] * shifted(values, 0, step)
        + coeffs[base + WEST] * shifted(values, 0, -step)
        + coeffs[base + NORTH] * shifted(values, 1, step)
        + coeffs[base + SOUTH] * shifted(values, 1, -step)
    )


def sweep(values, source, coeffs, level):
    return values + coeffs[6 * level + SCALE] * (source - level_apply(values, coeffs, level))


def vcycle(source, coeffs):
    values0 = coeffs[SCALE] * source
    source1 = pair_sums(source - level_apply(values0, coeffs, 0), 1)
    values1 = coeffs[6 + SCALE] * source1
    source2 = pair_sums(source1 - level_apply(values1, coeffs, 1), 2)
    values2 = coeffs[12 + SCALE] * source2
    for _ in range(COARSE_SWEEPS - 1):
        values2 = sweep(values2, source2, coeffs, 2)
    values1 = sweep(values1 + values2, source1, coeffs, 1)
    return sweep(values0 + values1, source, coeffs, 0)


def ghost_column(packed, start, to_lane, lane):
    return lane_roll(packed, to_lane - (start + lane))


def neighbour_sum(values, trans, up_row, down_row, right_col, left_col):
    rows, lanes = iotas((R, L))
    east = jnp.where(rows == R - 1, up_row, shifted(values, 0, 1))
    west = jnp.where(rows == 0, down_row, shifted(values, 0, -1))
    north = jnp.where(lanes == L - 1, right_col, shifted(values, 1, 1))
    south = jnp.where(lanes == 0, left_col, shifted(values, 1, -1))
    return trans[0] * east + trans[1] * west + trans[2] * north + trans[3] * south


def ghost_sum(trans, up_row, down_row, right_col, left_col):
    rows, lanes = iotas((R, L))
    return (
        jnp.where(rows == R - 1, trans[0] * up_row, 0.0)
        + jnp.where(rows == 0, trans[1] * down_row, 0.0)
        + jnp.where(lanes == L - 1, trans[2] * right_col, 0.0)
        + jnp.where(lanes == 0, trans[3] * left_col, 0.0)
    )


def one_step(pressure, vector, edges, col_right, col_left, diag, inverse, couple, trans, boost, z_out, product_out):
    p = pressure[0:R, 0:L]
    up_row, down_row = (pressure[R : R + 1, 0:L], pressure[EX - 1 : EX, 0:L])
    far = pressure[0:R, L:EY]
    right_p, left_p = (lane_roll(far, L - 1), lane_roll(far, 1))
    second = []
    for c in range(NC):
        own = diag[c, 0] * p
        if c == 0:
            own = own + boost * p
        around = neighbour_sum(
            couple[c, 0] * p,
            trans,
            edges[pl.ds(c, 1), :] * up_row,
            edges[pl.ds(NC + c, 1), :] * down_row,
            ghost_column(col_right, 64, L - 1, c) * right_p,
            ghost_column(col_left, 64, 0, c) * left_p,
        )
        second.append(vector[c] - (own - around))
    z = []
    for c in range(NC):
        total = inverse[c, 0] * second[0]
        for k in range(1, NC):
            total = total + inverse[c, k] * second[k]
        if c == 0:
            total = total + p
        z_out[c] = total
        z.append(total)
    result = []
    for c in range(NC):
        product = couple[c, 0] * z[0]
        own = diag[c, 0] * z[0]
        for k in range(1, NC):
            product = product + couple[c, k] * z[k]
            own = own + diag[c, k] * z[k]
        product_out[c] = product
        own = own + boost * z[c]
        zero = jnp.zeros((1, L), jnp.float32)
        around = neighbour_sum(product, trans, zero, zero, 0.0, 0.0)
        result.append(own - around - vector[c])
    return result


def load_blocks(sources, targets, sems):
    copies = [pltpu.make_async_copy(s, t, sems.at[i]) for i, (s, t) in enumerate(zip(sources, targets))]
    for copy in copies:
        copy.start()
    return copies


def first_step_kernel(
    par, got1, got2, ext, ext_cols, edges, rhs, trans, weights, wells, diag_hbm, inverse_hbm, couple_hbm,
    msg1, msg2, z_out, partial, product, coeffs, cols_right, cols_left, pressure_part, product_cols,
    diag, inverse, couple, sems,
):
    copies = load_blocks((diag_hbm, inverse_hbm, couple_hbm), (diag, inverse, couple), sems)
    rows, lanes = iotas((EX, L))
    right, left = take(par, 1, got1, got2, pl.ds(EX, EX))
    cols_right[...] = right
    cols_left[...] = left
    packed = ext_cols[...]
    north_own = -lane_sum(lane_roll(packed, 64 - 3 * NC) * right, 64)
    south_right = -lane_sum(lane_roll(packed, 64 - NC) * right, 64 + NC)
    south_own = -lane_sum(lane_roll(packed, 64 - NC) * left, 64)
    north_left = -lane_sum(lane_roll(packed, 64 + NC) * left, 64 + NC)
    right_four, left_four = take(par, 1, got1, got2, pl.ds(0, EX))
    source = None
    for k in range(6):
        from_right = lane_roll(right_four if k < 4 else right, -HALO * (k % 4))
        from_left = lane_roll(left_four if k < 4 else left, L - HALO - HALO * (k % 4))
        near = ext[k]
        far = jnp.where(lanes < HALO, from_right, jnp.where(lanes >= L - HALO, from_left, 0.0))
        if k == CENTER:
            far = jnp.where(far == 0.0, 1.0, far)
        if k == NORTH:
            near = jnp.where(lanes == L - 1, north_own, near)
            far = jnp.where(lanes == L - 1, north_left, far)
        if k == SOUTH:
            near = jnp.where(lanes == 0, south_own, near)
            far = jnp.where(lanes == 0, south_right, far)
        field = jnp.concatenate([near, far], axis=1)
        if k == 5:
            source = field
        else:
            coeffs[k] = field
    coeffs[SCALE] = RELAX / coeffs[CENTER]
    coarsen_into(coeffs, 0)
    coarsen_into(coeffs, 1)
    pressure = vcycle(source, coeffs)
    for copy in copies:
        copy.wait()
    boost = WELL_BOOST * wells[...].astype(jnp.float32)
    vector = [rhs[c] for c in range(NC)]
    result = one_step(
        pressure, vector, edges, right[0:R], left[0:R], diag, inverse, couple, trans, boost, z_out, product
    )
    weighed = jnp.zeros((R, L), jnp.float32)
    parts = []
    for c in range(NC):
        partial[c] = result[c]
        weighed = weighed + weights[c] * result[c]
        put(par, 0, msg1, msg2, pl.ds(BX_EDGE + c, 1), product[c, R - 1 : R, :], product[c, 0:1, :])
        parts += [(product[c], 0, c), (product[c], L - 1, NC + c)]
    blank = jnp.zeros((16 - NC, L), jnp.float32)
    columns = pack_columns(parts)
    pressure_part[...] = weighed
    product_cols[...] = columns
    for msg in (msg1, msg2):
        msg[pl.ds(0, R), :] = weighed
        msg[pl.ds(BX_EDGE + NC, 16 - NC), :] = blank
        msg[pl.ds(BX_COL, R), :] = columns


def between_kernel(par, got1, got2, pressure_part, product_cols, product, edges, trans, weights, msg1, msg2, ext, ext_cols, rows_out):
    rows, lanes = iotas((EX, L))
    t_up, t_down = (trans[0, R - 1 : R, :], trans[1, 0:1, :])
    own_up, own_down, far_up, far_down = (jnp.zeros((1, L), jnp.float32) for _ in range(4))
    for c in range(NC):
        up, down = take(par, 0, got1, got2, pl.ds(BX_EDGE + c, 1))
        rows_out[pl.ds(c, 1), :] = up
        rows_out[pl.ds(NC + c, 1), :] = down
        own_up = own_up + t_up * weights[c, R - 1 : R, :] * up
        own_down = own_down + t_down * weights[c, 0:1, :] * down
        far_up = far_up + edges[pl.ds(2 * NC + c, 1), :] * product[c, R - 1 : R, :]
        far_down = far_down + edges[pl.ds(3 * NC + c, 1), :] * product[c, 0:1, :]
    up, down = take(par, 0, got1, got2, pl.ds(0, R))
    field = jnp.concatenate([pressure_part[...], up, down], axis=0)
    edge = jnp.where(rows == R - 1, own_up, 0.0) + jnp.where(rows == 0, own_down, 0.0)
    edge = edge + jnp.where(rows == R, far_up, 0.0) + jnp.where(rows == EX - 1, far_down, 0.0)
    field = field - edge
    ext[...] = field
    up, down = take(par, 0, got1, got2, pl.ds(BX_COL, R))
    packed = jnp.concatenate([product_cols[...], up, down], axis=0)
    ext_cols[...] = packed
    near = lanes < HALO
    put(
        par, 1, msg1, msg2, pl.ds(0, EX),
        jnp.where(near, lane_roll(field, HALO), lane_roll(packed, HALO - NC)),
        jnp.where(near, field, lane_roll(packed, HALO)),
    )


def second_step_kernel(
    par, got1, got2, ext, ext_cols, rows_in, setup_cols, cols_right, cols_left, edges, coeffs, partial, trans, wells,
    diag_hbm, inverse_hbm, couple_hbm,
    msgx1, msgx2, msgy1, msgy2, z_out, vector_out, remainder, product,
    diag, inverse, couple, sems,
):
    copies = load_blocks((diag_hbm, inverse_hbm, couple_hbm), (diag, inverse, couple), sems)
    rows, lanes = iotas((EX, L))
    right, left = take(par, 1, got1, got2, pl.ds(0, EX))
    packed, tw = (ext_cols[...], setup_cols[...])
    old_right, old_left = (cols_right[...], cols_left[...])
    own_right = lane_sum(lane_roll(tw, HALO - 3 * NC) * right, HALO)
    own_left = lane_sum(lane_roll(tw, HALO - NC) * left, HALO)
    far_right = lane_sum(old_right * lane_roll(packed, 64), 64 + NC)
    far_left = lane_sum(old_left * lane_roll(packed, 64 + NC), 64 + NC)
    near = ext[...] - jnp.where(lanes == L - 1, own_right, 0.0) - jnp.where(lanes == 0, own_left, 0.0)
    far = jnp.where(
        lanes < HALO, right, jnp.where(lanes >= L - HALO, lane_roll(left, L - HALO), 0.0)
    )
    far = far - jnp.where(lanes == 0, far_right, 0.0) - jnp.where(lanes == L - 1, far_left, 0.0)
    pressure = vcycle(jnp.concatenate([near, far], axis=1), coeffs)
    vector = []
    for c in range(NC):
        ghosts = ghost_sum(
            trans,
            rows_in[pl.ds(c, 1), :],
            rows_in[pl.ds(NC + c, 1), :],
            ghost_column(right[0:R], HALO, L - 1, c),
            ghost_column(left[0:R], HALO, 0, c),
        )
        value = partial[c] - ghosts
        vector_out[c] = value
        vector.append(value)
    for copy in copies:
        copy.wait()
    boost = WELL_BOOST * wells[...].astype(jnp.float32)
    result = one_step(
        pressure, vector, edges, old_right[0:R], old_left[0:R], diag, inverse, couple, trans, boost, z_out, product
    )
    to_right, to_left = ([], [])
    for c in range(NC):
        remainder[c] = result[c]
        put(par, 0, msgx1, msgx2, pl.ds(c, 1), product[c, R - 1 : R, :], product[c, 0:1, :])
        to_right.append((product[c], L - 1, c))
        to_left.append((product[c], 0, c))
    blank = jnp.zeros((16 - NC, L), jnp.float32)
    msgx1[pl.ds(NC, 16 - NC), :] = blank
    msgx2[pl.ds(NC, 16 - NC), :] = blank
    put(par, 1, msgy1, msgy2, pl.ds(0, R), pack_columns(to_right), pack_columns(to_left))


def dots_kernel(par, gotx1, gotx2, goty1, goty2, rhs, vector, remainder, trans, out):
    right, left = take(par, 1, goty1, goty2, pl.ds(0, R))
    sums = [jnp.zeros((R, L), jnp.float32) for _ in range(6)]
    for c in range(NC):
        up, down = take(par, 0, gotx1, gotx2, pl.ds(c, 1))
        ghosts = ghost_sum(trans, up, down, ghost_column(right, 0, L - 1, c), ghost_column(left, 0, 0, c))
        two = remainder[c] - ghosts
        zero, one = (rhs[c], vector[c])
        for k, (a, b) in enumerate(((zero, zero), (zero, one), (one, one), (zero, two), (one, two), (two, two))):
            sums[k] = sums[k] + a * b
    lanes = iotas((1, L))[1]
    row = jnp.zeros((1, L), jnp.float32)
    for k, total in enumerate(sums):
        row = jnp.where(lanes == k, jnp.sum(total, keepdims=True), row)
    out[...] = jnp.broadcast_to(row, out.shape)


def finish_kernel(gathered, z_one, z_two, out, estimate):
    row = jnp.sum(gathered[...], axis=0, keepdims=True)
    lanes = iotas((1, L))[1]
    g00, g01, g11, g02, g12, g22 = (
        jnp.sum(jnp.where(lanes == k, row, 0.0), axis=1, keepdims=True) for k in range(6)
    )
    beta = jnp.sqrt(g00)
    shift = g01 / g00
    h00 = 1.0 + shift
    length2 = g11 - shift * g01
    length = jnp.sqrt(length2)
    h10 = length / beta
    h01 = (g02 - shift * g01) / (beta * length)
    above = (g12 - shift * g02 - shift * (g11 - shift * g01)) / length2
    h11 = 1.0 + above
    h21 = jnp.sqrt((g22 - 2.0 * shift * g12 + shift * shift * g11) / length2 - h01 * h01 - above * above)
    radius0 = jnp.sqrt(h00 * h00 + h10 * h10)
    cos0, sin0 = (h00 / radius0, h10 / radius0)
    r01 = cos0 * h01 + sin0 * h11
    mid = cos0 * h11 - sin0 * h01
    radius1 = jnp.sqrt(mid * mid + h21 * h21)
    cos1, sin1 = (mid / radius1, h21 / radius1)
    rhs0, rhs1 = (cos0 * beta, -sin0 * beta)
    estimate[...] = jnp.abs(sin1 * rhs1)
    y1 = cos1 * rhs1 / radius1
    y0 = (rhs0 - r01 * y1) / radius0
    weight1 = y1 / length
    weight0 = y0 / beta - weight1 * shift
    for c in range(NC):
        out[c] = weight0 * z_one[c] + weight1 * z_two[c]


VMEM = functools.partial(pl.BlockSpec, memory_space=pltpu.VMEM)
SMEM = functools.partial(pl.BlockSpec, memory_space=pltpu.SMEM)
ANY = functools.partial(pl.BlockSpec, memory_space=pl.ANY)


def shape(*dims):
    return jax.ShapeDtypeStruct(dims, jnp.float32)


def call(kernel, in_specs, outs, scratch=(), cost=20_000_000):
    return pl.pallas_call(
        kernel,
        in_specs=list(in_specs),
        out_specs=[VMEM()] * len(outs),
        out_shape=list(outs),
        scratch_shapes=list(scratch),
        cost_estimate=pl.CostEstimate(flops=cost, bytes_accessed=1_000_000, transcendentals=0),
        compiler_params=pltpu.CompilerParams(vmem_limit_bytes=30 * 1024 * 1024),
    )


def swap(first, second, axis):
    peers = lax.axis_size(axis)
    pairs = [(i, i ^ 1) for i in range(peers) if i ^ 1 < peers]
    others = [(i, ((i + 1) ^ 1) - 1) for i in range(1, peers) if ((i + 1) ^ 1) - 1 < peers]
    return (lax.ppermute(first, axis, pairs), lax.ppermute(second, axis, others))


def on_device(right_side, diag_blocks, couple_blocks, transmissibility, pressure_weights, well_mask):
    par = jnp.stack([lax.axis_index("gx") % 2, lax.axis_index("gy") % 2]).astype(jnp.int32)
    column = pl.BlockSpec((NC, 1, R, L), lambda i: (0, 0, 0, 0))

    def whole(*dims):
        return pl.BlockSpec(dims, lambda i: (0,) * len(dims))

    msg_a1, msg_a2, own, cols = pl.pallas_call(
        setup_kernel,
        grid=(1,),
        in_specs=[
            SMEM(), whole(NC, R, L), column, column, whole(4, R, L), whole(NC, R, L), whole(R, L),
        ],
        out_specs=[whole(AX_ROWS, L), whole(AX_ROWS, L), whole(6 * R, L), whole(R, L)],
        out_shape=[shape(AX_ROWS, L), shape(AX_ROWS, L), shape(6 * R, L), shape(R, L)],
        compiler_params=pltpu.CompilerParams(vmem_limit_bytes=30 * 1024 * 1024),
    )(par, right_side, diag_blocks, couple_blocks, transmissibility, pressure_weights, well_mask)

    got_a1, got_a2 = swap(msg_a1, msg_a2, "gx")

    slab = pl.BlockSpec((NC, NC, 8, L), lambda i: (0, 0, i, 0))
    inverse = pl.pallas_call(
        inverse_kernel,
        grid=(R // 8,),
        in_specs=[slab, pl.BlockSpec((8, L), lambda i: (i, 0))],
        out_specs=slab,
        out_shape=shape(NC, NC, R, L),
        cost_estimate=pl.CostEstimate(flops=20_000_000, bytes_accessed=2_700_000, transcendentals=0),
        compiler_params=pltpu.CompilerParams(vmem_limit_bytes=30 * 1024 * 1024),
    )(diag_blocks, well_mask)

    msg_y1, msg_y2, ext, ext_cols, edges = pl.pallas_call(
        setup_middle_kernel,
        grid=(1,),
        in_specs=[
            SMEM(), whole(AX_ROWS, L), whole(AX_ROWS, L), whole(6 * R, L), whole(R, L), column,
            whole(4, R, L), whole(NC, R, L),
        ],
        out_specs=[whole(AY_ROWS, L), whole(AY_ROWS, L), whole(6, EX, L), whole(EX, L), whole(4 * NC, L)],
        out_shape=[shape(AY_ROWS, L), shape(AY_ROWS, L), shape(6, EX, L), shape(EX, L), shape(4 * NC, L)],
        compiler_params=pltpu.CompilerParams(vmem_limit_bytes=30 * 1024 * 1024),
    )(par, got_a1, got_a2, own, cols, couple_blocks, transmissibility, pressure_weights)

    got_y1, got_y2 = swap(msg_y1, msg_y2, "gy")

    blocks = [pltpu.VMEM((NC, NC, R, L), jnp.float32)] * 3 + [pltpu.SemaphoreType.DMA((3,))]
    fields = shape(NC, R, L)
    msg_b1, msg_b2, z_one, partial, product, coeffs, cols_right, cols_left, pressure_part, product_cols = call(
        first_step_kernel,
        [SMEM()] + [VMEM()] * 9 + [ANY()] * 3,
        [
            shape(BX_ROWS, L), shape(BX_ROWS, L), fields, fields, fields, shape(18, EX, EY),
            shape(EX, L), shape(EX, L), shape(R, L), shape(R, L),
        ],
        blocks,
    )(
        par, got_y1, got_y2, ext, ext_cols, edges, right_side, transmissibility, pressure_weights, well_mask,
        diag_blocks, inverse, couple_blocks,
    )

    got_b1, got_b2 = swap(msg_b1, msg_b2, "gx")
    msg_c1, msg_c2, ext_b, ext_cols_b, rows_b = call(
        between_kernel,
        [SMEM()] + [VMEM()] * 8,
        [shape(EX, L), shape(EX, L), shape(EX, L), shape(EX, L), shape(2 * NC, L)],
    )(par, got_b1, got_b2, pressure_part, product_cols, product, edges, transmissibility, pressure_weights)
    got_c1, got_c2 = swap(msg_c1, msg_c2, "gy")

    msg_x1, msg_x2, msg_z1, msg_z2, z_two, vector, remainder, _ = call(
        second_step_kernel,
        [SMEM()] + [VMEM()] * 13 + [ANY()] * 3,
        [shape(16, L), shape(16, L), shape(R, L), shape(R, L), fields, fields, fields, fields],
        blocks,
    )(
        par, got_c1, got_c2, ext_b, ext_cols_b, rows_b, ext_cols, cols_right, cols_left, edges, coeffs, partial,
        transmissibility, well_mask, diag_blocks, inverse, couple_blocks,
    )
    got_x1, got_x2 = swap(msg_x1, msg_x2, "gx")
    got_z1, got_z2 = swap(msg_z1, msg_z2, "gy")
    devices = lax.axis_size("gx") * lax.axis_size("gy")
    (local,) = call(dots_kernel, [SMEM()] + [VMEM()] * 8, [shape(devices, L)])(
        par, got_x1, got_x2, got_z1, got_z2, right_side, vector, remainder, transmissibility
    )
    gathered = lax.all_to_all(local, ("gx", "gy"), 0, 0, tiled=True)
    answer, estimate = call(finish_kernel, [VMEM()] * 3, [fields, shape(1, 1)])(gathered, z_one, z_two)
    return (answer, estimate.reshape(()))


def solution(mesh):
    return jax.shard_map(
        on_device,
        mesh=mesh,
        in_specs=(
            P(None, "gx", "gy"),
            P(None, None, "gx", "gy"),
            P(None, None, "gx", "gy"),
            P(None, "gx", "gy"),
            P(None, "gx", "gy"),
            P("gx", "gy"),
        ),
        out_specs=(P(None, "gx", "gy"), P()),
        check_vma=False,
    )
```

time: 566 us -> 89.2 us (0.16)
  starting transfers between devices: 293 us -> 26.9 us
  blocking collectives: 167 us -> 34.5 us
  other arithmetic: 40.5 us -> 0.08 us
  local copies, waits for them, and re-layouts: 29 us -> 6.03 us
  Pallas kernels: 0 us -> 12.8 us
  between operations: 13.4 us -> 0.81 us
  waiting for transfers between devices: 19.2 us -> 7.62 us
    ppermute x92 -> x12, starting transfers between devices: 293 us -> 26.9 us  [the longest x6 16.1 us: swap(): lax.ppermute(first, axis, pairs)]
    psum x12 -> x0, blocking collectives: 167 us -> none  [by_axis(): return functools.reduce(lax.psum, axes, shard)]
    all_to_all x0 -> x1, blocking collectives: none -> 34.5 us  [on_device(): gathered = lax.all_to_all(local, ('gx', 'gy'), 0, 0, tiled=True)]
    reduce_sum x23 -> x0, other arithmetic: 17.8 us -> none  [the longest x4 2.87 us: restrict(): return values.reshape(extent_x // 2, 2, extent_y // 2, 2).sum(axis=(1, 3))]
    pallas_call x0 -> x8, Pallas kernels: none -> 12.8 us  [the longest x1 3.85 us: on_device(): call(first_step_kernel, [SMEM()] + [VMEM()] * 9 + [ANY()] * 3, [shape(BX_...]
    ppermute x92 -> x12, waiting for transfers between devices: 19.2 us -> 7.62 us  [the longest x6 4.84 us: swap(): lax.ppermute(second, axis, others)]
    reduce_sum x4 -> x0, local copies, waits for them, and re-layouts: 7.98 us -> none  [weighed(): return jnp.sum(weights * side_values, axis=0)]
    sub x14 -> x0, other arithmetic: 6.48 us -> none  [the longest x4 3.05 us: vcycle(): residue = source - level_apply(iterate, coeffs, padder)]
  transfers between devices with their start and end apart: 92 -> 12, of which waited for: 23 -> 5; matrix products, arithmetic and copies ran while one was open for 6% -> 0% of each run, Pallas kernels for 0% -> 1%
where the time goes in v1:
time: 89.2 us; the launch traced here: 88.8 us
  blocking collectives  34.5 us (39%)
  starting transfers between devices  26.9 us (30%)
  Pallas kernels  12.8 us (14%)
  waiting for transfers between devices  7.62 us (9%)
  local copies, waits for them, and re-layouts  6.03 us (7%)
    all_to_all x1, blocking collectives, on_device(): gathered = lax.all_to_all(local, ('gx', 'gy'), 0, 0, tiled=True)  34.5 us
    ppermute x6, starting transfers between devices, swap(): lax.ppermute(first, axis, pairs)  16.1 us
    ppermute x6, starting transfers between devices, swap(): lax.ppermute(second, axis, others)  10.8 us
    unnamed x18, local copies, waits for them, and re-layouts  6.03 us
    ppermute x6, waiting for transfers between devices, swap(): lax.ppermute(second, axis, others)  4.84 us
    pallas_call x1, Pallas kernels, on_device(): call(first_step_kernel, [SMEM()] + [VMEM()] * 9 + [ANY()] * 3, [shape(BX_...  3.85 us
    pallas_call x1, Pallas kernels, on_device(): call(second_step_kernel, [SMEM()] + [VMEM()] * 13 + [ANY()] * 3, [shape(1...  3.72 us
    ppermute x6, waiting for transfers between devices, swap(): lax.ppermute(first, axis, pairs)  2.77 us
  transfers between devices with their start and end apart: 12, of which 5 were waited for; matrix products, arithmetic and copies ran while one was open for 0% of the time, Pallas kernels for 1%

profile of v1, /device:TPU:1, one launch (start us, length us, event | category | flops | bytes accessed | tf_op | source)
XLA Modules:
  0.0 88.8 jit_solution(16138145054848947511)
XLA Ops:
  0.6 0.1 pad_add_fusion.par
  0.7 0.0 copy-start
  0.7 1.3 %copy-done = f32[9,9,32,128]{3,2,1,0:T(8,128)S(1)} copy-done((f32[9,9,32,128]{3,2,1,0:T(8,128)S(1)}, f32[9,9,32,128]{3,2,1,0:T(8,128)}, u32[]{:S(2)}) %copy-start) | copy-done | bytes 1327128
  2.0 0.0 copy-start.2
  2.0 1.3 %copy-done.2 = f32[9,9,32,128]{3,2,1,0:T(8,128)S(1)} copy-done((f32[9,9,32,128]{3,2,1,0:T(8,128)S(1)}, f32[9,9,32,128]{3,2,1,0:T(8,128)}, u32[]{:S(2)}) %copy-start.2) | copy-done | bytes 1327128
  3.4 0.0 copy-start.4
  3.4 0.8 copy-done.4
  4.2 0.0 copy-start.6
  4.2 0.9 %copy-done.6 = f32[9,32,128]{2,1,0:T(8,128)S(1)} copy-done((f32[9,32,128]{2,1,0:T(8,128)S(1)}, f32[9,32,128]{2,1,0:T(8,128)}, u32[]{:S(2)}) %copy-start.6) | copy-done | bytes 147480
  5.1 0.0 copy-start.7
  5.1 0.9 %copy-done.7 = f32[9,32,128]{2,1,0:T(8,128)S(1)} copy-done((f32[9,32,128]{2,1,0:T(8,128)S(1)}, f32[9,32,128]{2,1,0:T(8,128)}, u32[]{:S(2)}) %copy-start.7) | copy-done | bytes 147480
  6.0 0.0 copy-start.8
  6.0 0.7 copy-done.8
  6.7 0.0 copy-start.3
  6.7 0.8 shard_map.77
  7.6 0.0 copy-start.1
  7.6 2.1 %collective-permute-start = (f32[248,128]{1,0:T(8,128)S(1)}, f32[248,128]{1,0:T(8,128)S(1)}, u32[]{:S(2)}, u32[]{:S(2)}) collective-permute-start(f32[248,128]{1,0:T(8,128)S(1)} %get-tuple-element.35), channel_id=1, source_target_pairs={{0,16},{16,0},{32,48},{48,32},{64,80},{80,64},{96,112},{112,96},{1... | collective-permute-start | bytes 380936 | tf_op jit(solution)/shard_map/ppermute | solution.py:531
  9.7 0.7 collective-permute-start.1
  10.4 1.6 %collective-permute-done.got1 = f32[248,128]{1,0:T(8,128)S(1)} collective-permute-done((f32[248,128]{1,0:T(8,128)S(1)}, f32[248,128]{1,0:T(8,128)S(1)}, u32[]{:S(2)}, u32[]{:S(2)}) %collective-permute-start) | collective-permute-done | bytes 127008 | tf_op jit(solution)/shard_map/ppermute | solution.py:531
  12.0 0.0 collective-permute-done.1.got2
  12.0 0.0 copy-done.3
  12.0 0.8 shard_map.78
  12.8 3.9 %collective-permute-start.2 = (f32[192,128]{1,0:T(8,128)S(1)}, f32[192,128]{1,0:T(8,128)S(1)}, u32[]{:S(2)}, u32[]{:S(2)}) collective-permute-start(f32[192,128]{1,0:T(8,128)S(1)} %get-tuple-element.39), channel_id=1, source_target_pairs={{0,1},{1,0},{2,3},{3,2},{4,5},{5,4},{6,7},{7,6},{8,9},{9,8},{10,11... | collective-permute-start | bytes 294920 | tf_op jit(solution)/shard_map/ppermute | solution.py:531
  16.7 2.0 %collective-permute-start.3 = (f32[192,128]{1,0:T(8,128)S(1)}, f32[192,128]{1,0:T(8,128)S(1)}, u32[]{:S(2)}, u32[]{:S(2)}) collective-permute-start(f32[192,128]{1,0:T(8,128)S(1)} %get-tuple-element.40), channel_id=1, source_target_pairs={{1,2},{2,1},{3,4},{4,3},{5,6},{6,5},{7,8},{8,7},{9,10},{10,9},{11,... | collective-permute-start | bytes 294920 | tf_op jit(solution)/shard_map/ppermute | solution.py:531
  18.7 0.0 copy-done.1
  18.7 1.3 %shard_map.79.inverse_hbm = f32[9,9,32,128]{3,2,1,0:T(8,128)S(1)} custom-call(f32[9,9,32,128]{3,2,1,0:T(8,128)S(1)} %copy-done.1, s32[32,128]{1,0:T(8,128)S(1)} %copy-done.8), custom_call_target="tpu_custom_call" | custom-call | flops 20000000 | bytes 2700000 | tf_op jit(solution)/shard_map/pallas_call | solution.py:555
  19.9 0.0 collective-permute-done.2.got1
  20.0 2.7 %collective-permute-done.3.got2 = f32[192,128]{1,0:T(8,128)S(1)} collective-permute-done((f32[192,128]{1,0:T(8,128)S(1)}, f32[192,128]{1,0:T(8,128)S(1)}, u32[]{:S(2)}, u32[]{:S(2)}) %collective-permute-start.3) | collective-permute-done | bytes 98336 | tf_op jit(solution)/shard_map/ppermute | solution.py:531
  22.6 0.0 copy-start.5
  22.6 3.9 %shard_map.80 = (f32[80,128]{1,0:T(8,128)S(1)}, f32[80,128]{1,0:T(8,128)S(1)}, f32[9,32,128]{2,1,0:T(8,128)S(1)}, f32[9,32,128]{2,1,0:T(8,128)S(1)}, f32[9,32,12...) custom-call(s32[2]{0:T(128)S(1)} %pad_add_fusion.par, ...), custom_call_target="tpu_custom_call" | custom-call | flops 20000000 | bytes 1000000 | tf_op jit(solution)/shard_map/pallas_call | solution.py:581
  26.5 3.7 %collective-permute-start.4 = (f32[80,128]{1,0:T(8,128)S(1)}, f32[80,128]{1,0:T(8,128)S(1)}, u32[]{:S(2)}, u32[]{:S(2)}) collective-permute-start(f32[80,128]{1,0:T(8,128)S(1)} %get-tuple-element.44), channel_id=1, source_target_pairs={{0,16},{16,0},{32,48},{48,32},{64,80},{80,64},{96,112},{112,96},{1... | collective-permute-start | bytes 122888 | tf_op jit(solution)/shard_map/ppermute | solution.py:531
  30.2 0.7 collective-permute-start.5
  30.8 0.7 collective-permute-done.4.got1
  31.6 0.0 collective-permute-done.5.got2
  31.6 0.7 shard_map.81
  32.2 0.1 collective-permute-start.6
  32.3 3.2 %collective-permute-start.7 = (f32[96,128]{1,0:T(8,128)S(1)}, f32[96,128]{1,0:T(8,128)S(1)}, u32[]{:S(2)}, u32[]{:S(2)}) collective-permute-start(f32[96,128]{1,0:T(8,128)S(1)} %get-tuple-element.50), channel_id=1, source_target_pairs={{1,2},{2,1},{3,4},{4,3},{5,6},{6,5},{7,8},{8,7},{9,10},{10,9},{11,... | collective-permute-start | bytes 147464 | tf_op jit(solution)/shard_map/ppermute | solution.py:531
  35.6 0.0 collective-permute-done.6.got1
  35.6 2.2 %collective-permute-done.7.got2 = f32[96,128]{1,0:T(8,128)S(1)} collective-permute-done((f32[96,128]{1,0:T(8,128)S(1)}, f32[96,128]{1,0:T(8,128)S(1)}, u32[]{:S(2)}, u32[]{:S(2)}) %collective-permute-start.7) | collective-permute-done | bytes 49184 | tf_op jit(solution)/shard_map/ppermute | solution.py:531
  37.8 0.0 copy-done.5
  37.8 3.7 %shard_map.82 = (f32[16,128]{1,0:T(8,128)S(1)}, f32[16,128]{1,0:T(8,128)S(1)}, f32[32,128]{1,0:T(8,128)S(1)}, f32[32,128]{1,0:T(8,128)S(1)}, f32[9,32,128]{2,1,0...) custom-call(s32[2]{0:T(128)S(1)} %pad_add_fusion.par, ...), custom_call_target="tpu_custom_call" | custom-call | flops 20000000 | bytes 1000000 | tf_op jit(solution)/shard_map/pallas_call | solution.py:602
  41.5 0.1 collective-permute-start.10
  41.6 3.7 %collective-permute-start.11 = (f32[32,128]{1,0:T(8,128)S(1)}, f32[32,128]{1,0:T(8,128)S(1)}, u32[]{:S(2)}, u32[]{:S(2)}) collective-permute-start(f32[32,128]{1,0:T(8,128)S(1)} %get-tuple-element.61), channel_id=1, source_target_pairs={{1,2},{2,1},{3,4},{4,3},{5,6},{6,5},{7,8},{8,7},{9,10},{10,9},{11,... | collective-permute-start | bytes 49160 | tf_op jit(solution)/shard_map/ppermute | solution.py:531
  45.3 6.2 %collective-permute-start.8 = (f32[16,128]{1,0:T(8,128)S(1)}, f32[16,128]{1,0:T(8,128)S(1)}, u32[]{:S(2)}, u32[]{:S(2)}) collective-permute-start(f32[16,128]{1,0:T(8,128)S(1)} %get-tuple-element.58), channel_id=1, source_target_pairs={{0,16},{16,0},{32,48},{48,32},{64,80},{80,64},{96,112},{112,96},{1... | collective-permute-start | bytes 24584 | tf_op jit(solution)/shard_map/ppermute | solution.py:531
  51.5 0.6 collective-permute-start.9
  52.1 0.4 collective-permute-done.8.gotx1
  52.5 0.0 collective-permute-done.9.gotx2
  52.5 0.0 collective-permute-done.10.goty1
  52.5 0.0 collective-permute-done.11.goty2
  52.5 0.8 shard_map.83
  53.4 34.5 %all_to_all.11 = f32[256,1,128]{2,1,0:T(1,128)S(1)} all-to-all(f32[256,1,128]{2,1,0:T(1,128)S(1)} %bitcast.8), channel_id=1, replica_groups=mesh['gx'=16,'gy'=16] {'gx','gy'}, dimensions={0} | all-to-all | bytes 262144 | tf_op jit(solution)/shard_map/all_to_all | solution.py:617
  87.9 0.9 shard_map.84
Async XLA Ops:
  0.7 1.3 %copy-start = (f32[9,9,32,128]{3,2,1,0:T(8,128)S(1)}, f32[9,9,32,128]{3,2,1,0:T(8,128)}, u32[]{:S(2)}) copy-start(f32[9,9,32,128]{3,2,1,0:T(8,128)} %diag_hbm.3) | copy-start | bytes 3981316
  2.0 1.3 %copy-start.2 = (f32[9,9,32,128]{3,2,1,0:T(8,128)S(1)}, f32[9,9,32,128]{3,2,1,0:T(8,128)}, u32[]{:S(2)}) copy-start(f32[9,9,32,128]{3,2,1,0:T(8,128)} %couple_hbm.3) | copy-start | bytes 3981316
  3.4 0.8 copy-start.4
  4.2 0.9 %copy-start.6 = (f32[9,32,128]{2,1,0:T(8,128)S(1)}, f32[9,32,128]{2,1,0:T(8,128)}, u32[]{:S(2)}) copy-start(f32[9,32,128]{2,1,0:T(8,128)} %weights.7) | copy-start | bytes 442372
  5.1 0.9 %copy-start.7 = (f32[9,32,128]{2,1,0:T(8,128)S(1)}, f32[9,32,128]{2,1,0:T(8,128)}, u32[]{:S(2)}) copy-start(f32[9,32,128]{2,1,0:T(8,128)} %rhs.5) | copy-start | bytes 442372
  6.0 0.7 copy-start.8
  6.7 5.3 %copy-start.3 = (f32[9,9,32,128]{3,2,1,0:T(8,128)S(1)}, f32[9,9,32,128]{3,2,1,0:T(8,128)}, u32[]{:S(2)}) copy-start(f32[9,9,32,128]{3,2,1,0:T(8,128)} %couple_hbm.3) | copy-start | bytes 3981316
  7.6 11.1 %copy-start.1 = (f32[9,9,32,128]{3,2,1,0:T(8,128)S(1)}, f32[9,9,32,128]{3,2,1,0:T(8,128)}, u32[]{:S(2)}) copy-start(f32[9,9,32,128]{3,2,1,0:T(8,128)} %diag_hbm.3) | copy-start | bytes 3981316
  7.6 4.4 %collective-permute-start = (f32[248,128]{1,0:T(8,128)S(1)}, f32[248,128]{1,0:T(8,128)S(1)}, u32[]{:S(2)}, u32[]{:S(2)}) collective-permute-start(f32[248,128]{1,0:T(8,128)S(1)} %get-tuple-element.35), channel_id=1, source_target_pairs={{0,16},{16,0},{32,48},{48,32},{64,80},{80,64},{96,112},{112,96},{1... | collective-permute-start | bytes 380936 | tf_op jit(solution)/shard_map/ppermute | solution.py:531
  9.7 2.3 %collective-permute-start.1 = (f32[248,128]{1,0:T(8,128)S(1)}, f32[248,128]{1,0:T(8,128)S(1)}, u32[]{:S(2)}, u32[]{:S(2)}) collective-permute-start(f32[248,128]{1,0:T(8,128)S(1)} %get-tuple-element.36), channel_id=1, source_target_pairs={{16,32},{32,16},{48,64},{64,48},{80,96},{96,80},{112,128},{128,112... | collective-permute-start | bytes 380936 | tf_op jit(solution)/shard_map/ppermute | solution.py:531
  12.8 7.1 %collective-permute-start.2 = (f32[192,128]{1,0:T(8,128)S(1)}, f32[192,128]{1,0:T(8,128)S(1)}, u32[]{:S(2)}, u32[]{:S(2)}) collective-permute-start(f32[192,128]{1,0:T(8,128)S(1)} %get-tuple-element.39), channel_id=1, source_target_pairs={{0,1},{1,0},{2,3},{3,2},{4,5},{5,4},{6,7},{7,6},{8,9},{9,8},{10,11... | collective-permute-start | bytes 294920 | tf_op jit(solution)/shard_map/ppermute | solution.py:531
  16.7 5.9 %collective-permute-start.3 = (f32[192,128]{1,0:T(8,128)S(1)}, f32[192,128]{1,0:T(8,128)S(1)}, u32[]{:S(2)}, u32[]{:S(2)}) collective-permute-start(f32[192,128]{1,0:T(8,128)S(1)} %get-tuple-element.40), channel_id=1, source_target_pairs={{1,2},{2,1},{3,4},{4,3},{5,6},{6,5},{7,8},{8,7},{9,10},{10,9},{11,... | collective-permute-start | bytes 294920 | tf_op jit(solution)/shard_map/ppermute | solution.py:531
  22.6 15.1 %copy-start.5 = (f32[4,32,128]{2,1,0:T(8,128)S(1)}, f32[4,32,128]{2,1,0:T(8,128)}, u32[]{:S(2)}) copy-start(f32[4,32,128]{2,1,0:T(8,128)} %trans.11) | copy-start | bytes 196612
  26.5 5.1 %collective-permute-start.4 = (f32[80,128]{1,0:T(8,128)S(1)}, f32[80,128]{1,0:T(8,128)S(1)}, u32[]{:S(2)}, u32[]{:S(2)}) collective-permute-start(f32[80,128]{1,0:T(8,128)S(1)} %get-tuple-element.44), channel_id=1, source_target_pairs={{0,16},{16,0},{32,48},{48,32},{64,80},{80,64},{96,112},{112,96},{1... | collective-permute-start | bytes 122888 | tf_op jit(solution)/shard_map/ppermute | solution.py:531
  30.2 1.4 %collective-permute-start.5 = (f32[80,128]{1,0:T(8,128)S(1)}, f32[80,128]{1,0:T(8,128)S(1)}, u32[]{:S(2)}, u32[]{:S(2)}) collective-permute-start(f32[80,128]{1,0:T(8,128)S(1)} %get-tuple-element.45), channel_id=1, source_target_pairs={{16,32},{32,16},{48,64},{64,48},{80,96},{96,80},{112,128},{128,112... | collective-permute-start | bytes 122888 | tf_op jit(solution)/shard_map/ppermute | solution.py:531
  32.2 3.3 %collective-permute-start.6 = (f32[96,128]{1,0:T(8,128)S(1)}, f32[96,128]{1,0:T(8,128)S(1)}, u32[]{:S(2)}, u32[]{:S(2)}) collective-permute-start(f32[96,128]{1,0:T(8,128)S(1)} %get-tuple-element.49), channel_id=1, source_target_pairs={{0,1},{1,0},{2,3},{3,2},{4,5},{5,4},{6,7},{7,6},{8,9},{9,8},{10,11... | collective-permute-start | bytes 147464 | tf_op jit(solution)/shard_map/ppermute | solution.py:531
  32.3 5.4 %collective-permute-start.7 = (f32[96,128]{1,0:T(8,128)S(1)}, f32[96,128]{1,0:T(8,128)S(1)}, u32[]{:S(2)}, u32[]{:S(2)}) collective-permute-start(f32[96,128]{1,0:T(8,128)S(1)} %get-tuple-element.50), channel_id=1, source_target_pairs={{1,2},{2,1},{3,4},{4,3},{5,6},{6,5},{7,8},{8,7},{9,10},{10,9},{11,... | collective-permute-start | bytes 147464 | tf_op jit(solution)/shard_map/ppermute | solution.py:531
  41.5 11.0 %collective-permute-start.10 = (f32[32,128]{1,0:T(8,128)S(1)}, f32[32,128]{1,0:T(8,128)S(1)}, u32[]{:S(2)}, u32[]{:S(2)}) collective-permute-start(f32[32,128]{1,0:T(8,128)S(1)} %get-tuple-element.60), channel_id=1, source_target_pairs={{0,1},{1,0},{2,3},{3,2},{4,5},{5,4},{6,7},{7,6},{8,9},{9,8},{10,11... | collective-permute-start | bytes 49160 | tf_op jit(solution)/shard_map/ppermute | solution.py:531
  41.6 10.9 %collective-permute-start.11 = (f32[32,128]{1,0:T(8,128)S(1)}, f32[32,128]{1,0:T(8,128)S(1)}, u32[]{:S(2)}, u32[]{:S(2)}) collective-permute-start(f32[32,128]{1,0:T(8,128)S(1)} %get-tuple-element.61), channel_id=1, source_target_pairs={{1,2},{2,1},{3,4},{4,3},{5,6},{6,5},{7,8},{8,7},{9,10},{10,9},{11,... | collective-permute-start | bytes 49160 | tf_op jit(solution)/shard_map/ppermute | solution.py:531
  45.3 7.2 %collective-permute-start.8 = (f32[16,128]{1,0:T(8,128)S(1)}, f32[16,128]{1,0:T(8,128)S(1)}, u32[]{:S(2)}, u32[]{:S(2)}) collective-permute-start(f32[16,128]{1,0:T(8,128)S(1)} %get-tuple-element.58), channel_id=1, source_target_pairs={{0,16},{16,0},{32,48},{48,32},{64,80},{80,64},{96,112},{112,96},{1... | collective-permute-start | bytes 24584 | tf_op jit(solution)/shard_map/ppermute | solution.py:531
  51.5 1.0 %collective-permute-start.9 = (f32[16,128]{1,0:T(8,128)S(1)}, f32[16,128]{1,0:T(8,128)S(1)}, u32[]{:S(2)}, u32[]{:S(2)}) collective-permute-start(f32[16,128]{1,0:T(8,128)S(1)} %get-tuple-element.59), channel_id=1, source_target_pairs={{16,32},{32,16},{48,64},{64,48},{80,96},{96,80},{112,128},{128,112... | collective-permute-start | bytes 24584 | tf_op jit(solution)/shard_map/ppermute | solution.py:531

commit v2 on v1

--- a/solution.py
+++ b/solution.py
@@ -65,7 +65,23 @@
     return packed
 
 
-def setup_kernel(par, rhs, diag0, couple0, trans, weights, wells, msg1, msg2, own, cols):
+def setup_kernel(
+    par, rhs_hbm, diag_hbm, couple_hbm, trans_hbm, weights_hbm, wells_hbm, msg1, msg2, own, cols,
+    rhs, diag0, couple0, trans, weights, wells, sems,
+):
+    pairs = (
+        (weights_hbm, weights),
+        (couple_hbm.at[:, 0:1], couple0),
+        (diag_hbm.at[:, 0:1], diag0),
+        (trans_hbm, trans),
+        (rhs_hbm, rhs),
+        (wells_hbm, wells),
+    )
+    copies = [pltpu.make_async_copy(a, b, sems.at[i]) for i, (a, b) in enumerate(pairs)]
+    for copy in copies:
+        copy.start()
+    for copy in copies:
+        copy.wait()
     rows, lanes = iotas((R, L))
     center = WELL_BOOST * wells[...].astype(jnp.float32) * weights[0]
     pressure = jnp.zeros((R, L), jnp.float32)
@@ -304,19 +320,10 @@
     return result
 
 
-def load_blocks(sources, targets, sems):
-    copies = [pltpu.make_async_copy(s, t, sems.at[i]) for i, (s, t) in enumerate(zip(sources, targets))]
-    for copy in copies:
-        copy.start()
-    return copies
-
-
 def first_step_kernel(
-    par, got1, got2, ext, ext_cols, edges, rhs, trans, weights, wells, diag_hbm, inverse_hbm, couple_hbm,
+    par, got1, got2, ext, ext_cols, edges, rhs, trans, weights, wells, diag, inverse, couple,
     msg1, msg2, z_out, partial, product, coeffs, cols_right, cols_left, pressure_part, product_cols,
-    diag, inverse, couple, sems,
 ):
-    copies = load_blocks((diag_hbm, inverse_hbm, couple_hbm), (diag, inverse, couple), sems)
     rows, lanes = iotas((EX, L))
     right, left = take(par, 1, got1, got2, pl.ds(EX, EX))
     cols_right[...] = right
@@ -350,8 +357,6 @@
     coarsen_into(coeffs, 0)
     coarsen_into(coeffs, 1)
     pressure = vcycle(source, coeffs)
-    for copy in copies:
-        copy.wait()
     boost = WELL_BOOST * wells[...].astype(jnp.float32)
     vector = [rhs[c] for c in range(NC)]
     result = one_step(
@@ -405,11 +410,9 @@
 
 def second_step_kernel(
     par, got1, got2, ext, ext_cols, rows_in, setup_cols, cols_right, cols_left, edges, coeffs, partial, trans, wells,
-    diag_hbm, inverse_hbm, couple_hbm,
+    diag, inverse, couple,
     msgx1, msgx2, msgy1, msgy2, z_out, vector_out, remainder, product,
-    diag, inverse, couple, sems,
 ):
-    copies = load_blocks((diag_hbm, inverse_hbm, couple_hbm), (diag, inverse, couple), sems)
     rows, lanes = iotas((EX, L))
     right, left = take(par, 1, got1, got2, pl.ds(0, EX))
     packed, tw = (ext_cols[...], setup_cols[...])
@@ -436,8 +439,6 @@
         value = partial[c] - ghosts
         vector_out[c] = value
         vector.append(value)
-    for copy in copies:
-        copy.wait()
     boost = WELL_BOOST * wells[...].astype(jnp.float32)
     result = one_step(
         pressure, vector, edges, old_right[0:R], old_left[0:R], diag, inverse, couple, trans, boost, z_out, product
@@ -505,7 +506,7 @@
 
 VMEM = functools.partial(pl.BlockSpec, memory_space=pltpu.VMEM)
 SMEM = functools.partial(pl.BlockSpec, memory_space=pltpu.SMEM)
-ANY = functools.partial(pl.BlockSpec, memory_space=pl.ANY)
+HBM = functools.partial(pl.BlockSpec, memory_space=pltpu.HBM)
 
 
 def shape(*dims):
@@ -532,22 +533,32 @@
 
 
 def on_device(right_side, diag_blocks, couple_blocks, transmissibility, pressure_weights, well_mask):
-    par = jnp.stack([lax.axis_index("gx") % 2, lax.axis_index("gy") % 2]).astype(jnp.int32)
+    par = jnp.stack([lax.axis_index("gx") & 1, lax.axis_index("gy") & 1]).astype(jnp.int32)
     column = pl.BlockSpec((NC, 1, R, L), lambda i: (0, 0, 0, 0))
 
     def whole(*dims):
         return pl.BlockSpec(dims, lambda i: (0,) * len(dims))
 
-    msg_a1, msg_a2, own, cols = pl.pallas_call(
+    msg_a1, msg_a2, own, cols = call(
         setup_kernel,
-        grid=(1,),
-        in_specs=[
-            SMEM(), whole(NC, R, L), column, column, whole(4, R, L), whole(NC, R, L), whole(R, L),
+        [SMEM()] + [HBM()] * 6,
+        [shape(AX_ROWS, L), shape(AX_ROWS, L), shape(6 * R, L), shape(R, L)],
+        [
+            pltpu.VMEM((NC, R, L), jnp.float32),
+            pltpu.VMEM((NC, 1, R, L), jnp.float32),
+            pltpu.VMEM((NC, 1, R, L), jnp.float32),
+            pltpu.VMEM((4, R, L), jnp.float32),
+            pltpu.VMEM((NC, R, L), jnp.float32),
+            pltpu.VMEM((R, L), jnp.int32),
+            pltpu.SemaphoreType.DMA((6,)),
         ],
-        out_specs=[whole(AX_ROWS, L), whole(AX_ROWS, L), whole(6 * R, L), whole(R, L)],
-        out_shape=[shape(AX_ROWS, L), shape(AX_ROWS, L), shape(6 * R, L), shape(R, L)],
-        compiler_params=pltpu.CompilerParams(vmem_limit_bytes=30 * 1024 * 1024),
-    )(par, right_side, diag_blocks, couple_blocks, transmissibility, pressure_weights, well_mask)
+    )(
+        par,
+        *(
+            pltpu.with_memory_space_constraint(x, pltpu.HBM)
+            for x in (right_side, diag_blocks, couple_blocks, transmissibility, pressure_weights, well_mask)
+        ),
+    )
 
     got_a1, got_a2 = swap(msg_a1, msg_a2, "gx")
 
@@ -576,16 +587,14 @@
 
     got_y1, got_y2 = swap(msg_y1, msg_y2, "gy")
 
-    blocks = [pltpu.VMEM((NC, NC, R, L), jnp.float32)] * 3 + [pltpu.SemaphoreType.DMA((3,))]
     fields = shape(NC, R, L)
     msg_b1, msg_b2, z_one, partial, product, coeffs, cols_right, cols_left, pressure_part, product_cols = call(
         first_step_kernel,
-        [SMEM()] + [VMEM()] * 9 + [ANY()] * 3,
+        [SMEM()] + [VMEM()] * 12,
         [
             shape(BX_ROWS, L), shape(BX_ROWS, L), fields, fields, fields, shape(18, EX, EY),
             shape(EX, L), shape(EX, L), shape(R, L), shape(R, L),
         ],
-        blocks,
     )(
         par, got_y1, got_y2, ext, ext_cols, edges, right_side, transmissibility, pressure_weights, well_mask,
         diag_blocks, inverse, couple_blocks,
@@ -601,9 +610,8 @@
 
     msg_x1, msg_x2, msg_z1, msg_z2, z_two, vector, remainder, _ = call(
         second_step_kernel,
-        [SMEM()] + [VMEM()] * 13 + [ANY()] * 3,
+        [SMEM()] + [VMEM()] * 16,
         [shape(16, L), shape(16, L), shape(R, L), shape(R, L), fields, fields, fields, fields],
-        blocks,
     )(
         par, got_c1, got_c2, ext_b, ext_cols_b, rows_b, ext_cols, cols_right, cols_left, edges, coeffs, partial,
         transmissibility, well_mask, diag_blocks, inverse, couple_blocks,

time: 89.2 us -> 83.8 us (0.939)
  local copies, waits for them, and re-layouts: 6.03 us -> 0.03 us
    unnamed x18 -> x12, local copies, waits for them, and re-layouts: 6.03 us -> 0.03 us
  transfers between devices with their start and end apart: 12 -> 12, of which waited for: 5 -> 5; matrix products, arithmetic and copies ran while one was open for 0% -> 0% of each run, Pallas kernels for 1% -> 2%
where the time goes in v2:
time: 83.8 us; the launch traced here: 83.5 us
  blocking collectives  34.5 us (41%)
  starting transfers between devices  26.9 us (32%)
  Pallas kernels  13.5 us (16%)
  waiting for transfers between devices  7.6 us (9%)
    all_to_all x1, blocking collectives, on_device(): gathered = lax.all_to_all(local, ('gx', 'gy'), 0, 0, tiled=True)  34.5 us
    ppermute x6, starting transfers between devices, swap(): lax.ppermute(first, axis, pairs)  16 us
    ppermute x6, starting transfers between devices, swap(): lax.ppermute(second, axis, others)  11 us
    ppermute x6, waiting for transfers between devices, swap(): lax.ppermute(second, axis, others)  4.82 us
    pallas_call x1, Pallas kernels, on_device(): call(first_step_kernel, [SMEM()] + [VMEM()] * 12, [shape(BX_ROWS, L), sha...  3.66 us
    pallas_call x1, Pallas kernels, on_device(): call(second_step_kernel, [SMEM()] + [VMEM()] * 16, [shape(16, L), shape(1...  3.38 us
    ppermute x6, waiting for transfers between devices, swap(): lax.ppermute(first, axis, pairs)  2.77 us
    pallas_call x1, Pallas kernels, on_device(): call(setup_kernel, [SMEM()] + [HBM()] * 6, [shape(AX_ROWS, L), shape(AX_R...  2.06 us
  transfers between devices with their start and end apart: 12, of which 5 were waited for; matrix products, arithmetic and copies ran while one was open for 0% of the time, Pallas kernels for 2%

profile of v2, /device:TPU:1, one launch (start us, length us, event | category | flops | bytes accessed | tf_op | source)
XLA Modules:
  0.0 83.5 jit_solution(8474626630431168750)
XLA Ops:
  0.6 0.1 pad_add_fusion.par
  0.7 0.0 copy-start.1
  0.7 0.0 copy-start.2
  0.7 0.0 copy-start.3
  0.7 2.1 %shard_map.77 = (f32[248,128]{1,0:T(8,128)S(1)}, f32[248,128]{1,0:T(8,128)S(1)}, f32[192,128]{1,0:T(8,128)S(1)}, f32[32,128]{1,0:T(8,128)S(1)}) custom-call(s32[2]{0:T(128)S(1)} %pad_add_fusion.par, f32[9,32,128]{2,1,0:T(8,128)} %rhs.3, f32[9,9,32,128]{3,2,1,0:T(8,128)} %diag.5, f32[9,9,32,128]{3,2,1,0:T(8,128)} %couple.3, f32[4,32,128]{2,1,0:T(8,128)} %trans.9, ...), custom_call_target="tpu_custom_call" | custom-call | flops 20000000 | bytes 1000000 | tf_op jit(solution)/shard_map/pallas_call | solution.py:542
  2.8 0.0 copy-start
  2.8 0.0 copy-start.5
  2.8 2.1 %collective-permute-start = (f32[248,128]{1,0:T(8,128)S(1)}, f32[248,128]{1,0:T(8,128)S(1)}, u32[]{:S(2)}, u32[]{:S(2)}) collective-permute-start(f32[248,128]{1,0:T(8,128)S(1)} %get-tuple-element.35), channel_id=1, source_target_pairs={{0,16},{16,0},{32,48},{48,32},{64,80},{80,64},{96,112},{112,96},{1... | collective-permute-start | bytes 380936 | tf_op jit(solution)/shard_map/ppermute | solution.py:532
  4.9 0.7 collective-permute-start.1
  5.6 1.6 %collective-permute-done.got1 = f32[248,128]{1,0:T(8,128)S(1)} collective-permute-done((f32[248,128]{1,0:T(8,128)S(1)}, f32[248,128]{1,0:T(8,128)S(1)}, u32[]{:S(2)}, u32[]{:S(2)}) %collective-permute-start) | collective-permute-done | bytes 127008 | tf_op jit(solution)/shard_map/ppermute | solution.py:532
  7.2 0.0 collective-permute-done.1.got2
  7.2 0.0 copy-done.1
  7.2 0.0 copy-done.2
  7.2 0.0 copy-done.3
  7.3 0.8 shard_map.78
  8.0 3.9 %collective-permute-start.2 = (f32[192,128]{1,0:T(8,128)S(1)}, f32[192,128]{1,0:T(8,128)S(1)}, u32[]{:S(2)}, u32[]{:S(2)}) collective-permute-start(f32[192,128]{1,0:T(8,128)S(1)} %get-tuple-element.39), channel_id=1, source_target_pairs={{0,1},{1,0},{2,3},{3,2},{4,5},{5,4},{6,7},{7,6},{8,9},{9,8},{10,11... | collective-permute-start | bytes 294920 | tf_op jit(solution)/shard_map/ppermute | solution.py:532
  11.9 0.0 copy-start.4
  11.9 2.1 %collective-permute-start.3 = (f32[192,128]{1,0:T(8,128)S(1)}, f32[192,128]{1,0:T(8,128)S(1)}, u32[]{:S(2)}, u32[]{:S(2)}) collective-permute-start(f32[192,128]{1,0:T(8,128)S(1)} %get-tuple-element.40), channel_id=1, source_target_pairs={{1,2},{2,1},{3,4},{4,3},{5,6},{6,5},{7,8},{8,7},{9,10},{10,9},{11,... | collective-permute-start | bytes 294920 | tf_op jit(solution)/shard_map/ppermute | solution.py:532
  14.0 0.0 copy-done
  14.0 0.0 copy-done.5
  14.0 1.3 %shard_map.79.inverse = f32[9,9,32,128]{3,2,1,0:T(8,128)S(1)} custom-call(f32[9,9,32,128]{3,2,1,0:T(8,128)S(1)} %copy-done, s32[32,128]{1,0:T(8,128)S(1)} %copy-done.5), custom_call_target="tpu_custom_call" | custom-call | flops 20000000 | bytes 2700000 | tf_op jit(solution)/shard_map/pallas_call | solution.py:566
  15.3 0.0 collective-permute-done.2.got1
  15.3 2.6 %collective-permute-done.3.got2 = f32[192,128]{1,0:T(8,128)S(1)} collective-permute-done((f32[192,128]{1,0:T(8,128)S(1)}, f32[192,128]{1,0:T(8,128)S(1)}, u32[]{:S(2)}, u32[]{:S(2)}) %collective-permute-start.3) | collective-permute-done | bytes 98336 | tf_op jit(solution)/shard_map/ppermute | solution.py:532
  18.0 0.0 copy-done.4
  18.0 3.7 %shard_map.80 = (f32[80,128]{1,0:T(8,128)S(1)}, f32[80,128]{1,0:T(8,128)S(1)}, f32[9,32,128]{2,1,0:T(8,128)S(1)}, f32[9,32,128]{2,1,0:T(8,128)S(1)}, f32[9,32,12...) custom-call(s32[2]{0:T(128)S(1)} %pad_add_fusion.par, ...), custom_call_target="tpu_custom_call" | custom-call | flops 20000000 | bytes 1000000 | tf_op jit(solution)/shard_map/pallas_call | solution.py:591
  21.6 3.7 %collective-permute-start.4 = (f32[80,128]{1,0:T(8,128)S(1)}, f32[80,128]{1,0:T(8,128)S(1)}, u32[]{:S(2)}, u32[]{:S(2)}) collective-permute-start(f32[80,128]{1,0:T(8,128)S(1)} %get-tuple-element.44), channel_id=1, source_target_pairs={{0,16},{16,0},{32,48},{48,32},{64,80},{80,64},{96,112},{112,96},{1... | collective-permute-start | bytes 122888 | tf_op jit(solution)/shard_map/ppermute | solution.py:532
  25.3 0.7 collective-permute-start.5
  26.0 0.7 collective-permute-done.4.got1
  26.7 0.0 collective-permute-done.5.got2
  26.7 0.7 shard_map.81
  27.4 0.1 collective-permute-start.6
  27.5 3.2 %collective-permute-start.7 = (f32[96,128]{1,0:T(8,128)S(1)}, f32[96,128]{1,0:T(8,128)S(1)}, u32[]{:S(2)}, u32[]{:S(2)}) collective-permute-start(f32[96,128]{1,0:T(8,128)S(1)} %get-tuple-element.50), channel_id=1, source_target_pairs={{1,2},{2,1},{3,4},{4,3},{5,6},{6,5},{7,8},{8,7},{9,10},{10,9},{11,... | collective-permute-start | bytes 147464 | tf_op jit(solution)/shard_map/ppermute | solution.py:532
  30.7 0.0 collective-permute-done.6.got1
  30.7 2.2 %collective-permute-done.7.got2 = f32[96,128]{1,0:T(8,128)S(1)} collective-permute-done((f32[96,128]{1,0:T(8,128)S(1)}, f32[96,128]{1,0:T(8,128)S(1)}, u32[]{:S(2)}, u32[]{:S(2)}) %collective-permute-start.7) | collective-permute-done | bytes 49184 | tf_op jit(solution)/shard_map/ppermute | solution.py:532
  32.9 3.4 %shard_map.82 = (f32[16,128]{1,0:T(8,128)S(1)}, f32[16,128]{1,0:T(8,128)S(1)}, f32[32,128]{1,0:T(8,128)S(1)}, f32[32,128]{1,0:T(8,128)S(1)}, f32[9,32,128]{2,1,0...) custom-call(s32[2]{0:T(128)S(1)} %pad_add_fusion.par, ...), custom_call_target="tpu_custom_call" | custom-call | flops 20000000 | bytes 1000000 | tf_op jit(solution)/shard_map/pallas_call | solution.py:611
  36.3 0.0 collective-permute-start.10
  36.3 3.7 %collective-permute-start.11 = (f32[32,128]{1,0:T(8,128)S(1)}, f32[32,128]{1,0:T(8,128)S(1)}, u32[]{:S(2)}, u32[]{:S(2)}) collective-permute-start(f32[32,128]{1,0:T(8,128)S(1)} %get-tuple-element.61), channel_id=1, source_target_pairs={{1,2},{2,1},{3,4},{4,3},{5,6},{6,5},{7,8},{8,7},{9,10},{10,9},{11,... | collective-permute-start | bytes 49160 | tf_op jit(solution)/shard_map/ppermute | solution.py:532
  40.0 6.2 %collective-permute-start.8 = (f32[16,128]{1,0:T(8,128)S(1)}, f32[16,128]{1,0:T(8,128)S(1)}, u32[]{:S(2)}, u32[]{:S(2)}) collective-permute-start(f32[16,128]{1,0:T(8,128)S(1)} %get-tuple-element.58), channel_id=1, source_target_pairs={{0,16},{16,0},{32,48},{48,32},{64,80},{80,64},{96,112},{112,96},{1... | collective-permute-start | bytes 24584 | tf_op jit(solution)/shard_map/ppermute | solution.py:532
  46.2 0.6 collective-permute-start.9
  46.8 0.4 collective-permute-done.8.gotx1
  47.2 0.0 collective-permute-done.9.gotx2
  47.2 0.0 collective-permute-done.10.goty1
  47.2 0.0 collective-permute-done.11.goty2
  47.2 0.8 %shard_map.83 = f32[256,128]{1,0:T(8,128)S(1)} custom-call(s32[2]{0:T(128)S(1)} %pad_add_fusion.par, f32[16,128]{1,0:T(8,128)S(1)} %collective-permute-done.8.gotx1, f32[16,128]{1,0:T(8,128)S(1)} %collective-permute-done.9.gotx2, f32[32,128]{1,0:T(8,128)S(1)} %collective-permute-done.10.goty1, f32[32,128]{1,0:T(8,128)S(1)} %collective-permute-done.11.goty2, ...), custom_call_target="tpu_custom_call" | custom-call | flops 20000000 | bytes 1000000 | tf_op jit(solution)/shard_map/pallas_call | solution.py:622
  48.1 34.5 %all_to_all.11 = f32[256,1,128]{2,1,0:T(1,128)S(1)} all-to-all(f32[256,1,128]{2,1,0:T(1,128)S(1)} %bitcast.8), channel_id=1, replica_groups=mesh['gx'=16,'gy'=16] {'gx','gy'}, dimensions={0} | all-to-all | bytes 262144 | tf_op jit(solution)/shard_map/all_to_all | solution.py:625
  82.6 0.9 %shard_map.84 = (f32[9,32,128]{2,1,0:T(8,128)}, f32[1,1]{1,0:T(1,128)}) custom-call(f32[256,128]{1,0:T(8,128)S(1)} %bitcast.7, f32[9,32,128]{2,1,0:T(8,128)S(1)} %get-tuple-element.64.z_one, f32[9,32,128]{2,1,0:T(8,128)S(1)} %get-tuple-element.65.z_two), custom_call_target="tpu_custom_call" | custom-call | flops 20000000 | bytes 1000000 | tf_op jit(solution)/shard_map/pallas_call | solution.py:626
Async XLA Ops:
  0.7 6.5 %copy-start.1 = (f32[9,9,32,128]{3,2,1,0:T(8,128)S(1)}, f32[9,9,32,128]{3,2,1,0:T(8,128)}, u32[]{:S(2)}) copy-start(f32[9,9,32,128]{3,2,1,0:T(8,128)} %couple.3) | copy-start | bytes 3981316
  0.7 6.5 %copy-start.2 = (f32[4,32,128]{2,1,0:T(8,128)S(1)}, f32[4,32,128]{2,1,0:T(8,128)}, u32[]{:S(2)}) copy-start(f32[4,32,128]{2,1,0:T(8,128)} %trans.9) | copy-start | bytes 196612
  0.7 6.5 %copy-start.3 = (f32[9,32,128]{2,1,0:T(8,128)S(1)}, f32[9,32,128]{2,1,0:T(8,128)}, u32[]{:S(2)}) copy-start(f32[9,32,128]{2,1,0:T(8,128)} %weights.5) | copy-start | bytes 442372
  2.8 11.2 %copy-start = (f32[9,9,32,128]{3,2,1,0:T(8,128)S(1)}, f32[9,9,32,128]{3,2,1,0:T(8,128)}, u32[]{:S(2)}) copy-start(f32[9,9,32,128]{3,2,1,0:T(8,128)} %diag.5) | copy-start | bytes 3981316
  2.8 11.2 %copy-start.5 = (s32[32,128]{1,0:T(8,128)S(1)}, s32[32,128]{1,0:T(8,128)}, u32[]{:S(2)}) copy-start(s32[32,128]{1,0:T(8,128)} %wells.5) | copy-start | bytes 49156
  2.8 4.4 %collective-permute-start = (f32[248,128]{1,0:T(8,128)S(1)}, f32[248,128]{1,0:T(8,128)S(1)}, u32[]{:S(2)}, u32[]{:S(2)}) collective-permute-start(f32[248,128]{1,0:T(8,128)S(1)} %get-tuple-element.35), channel_id=1, source_target_pairs={{0,16},{16,0},{32,48},{48,32},{64,80},{80,64},{96,112},{112,96},{1... | collective-permute-start | bytes 380936 | tf_op jit(solution)/shard_map/ppermute | solution.py:532
  4.9 2.3 %collective-permute-start.1 = (f32[248,128]{1,0:T(8,128)S(1)}, f32[248,128]{1,0:T(8,128)S(1)}, u32[]{:S(2)}, u32[]{:S(2)}) collective-permute-start(f32[248,128]{1,0:T(8,128)S(1)} %get-tuple-element.36), channel_id=1, source_target_pairs={{16,32},{32,16},{48,64},{64,48},{80,96},{96,80},{112,128},{128,112... | collective-permute-start | bytes 380936 | tf_op jit(solution)/shard_map/ppermute | solution.py:532
  8.0 7.3 %collective-permute-start.2 = (f32[192,128]{1,0:T(8,128)S(1)}, f32[192,128]{1,0:T(8,128)S(1)}, u32[]{:S(2)}, u32[]{:S(2)}) collective-permute-start(f32[192,128]{1,0:T(8,128)S(1)} %get-tuple-element.39), channel_id=1, source_target_pairs={{0,1},{1,0},{2,3},{3,2},{4,5},{5,4},{6,7},{7,6},{8,9},{9,8},{10,11... | collective-permute-start | bytes 294920 | tf_op jit(solution)/shard_map/ppermute | solution.py:532
  11.9 6.1 %copy-start.4 = (f32[9,32,128]{2,1,0:T(8,128)S(1)}, f32[9,32,128]{2,1,0:T(8,128)}, u32[]{:S(2)}) copy-start(f32[9,32,128]{2,1,0:T(8,128)} %rhs.3) | copy-start | bytes 442372
  11.9 6.1 %collective-permute-start.3 = (f32[192,128]{1,0:T(8,128)S(1)}, f32[192,128]{1,0:T(8,128)S(1)}, u32[]{:S(2)}, u32[]{:S(2)}) collective-permute-start(f32[192,128]{1,0:T(8,128)S(1)} %get-tuple-element.40), channel_id=1, source_target_pairs={{1,2},{2,1},{3,4},{4,3},{5,6},{6,5},{7,8},{8,7},{9,10},{10,9},{11,... | collective-permute-start | bytes 294920 | tf_op jit(solution)/shard_map/ppermute | solution.py:532
  21.6 5.1 %collective-permute-start.4 = (f32[80,128]{1,0:T(8,128)S(1)}, f32[80,128]{1,0:T(8,128)S(1)}, u32[]{:S(2)}, u32[]{:S(2)}) collective-permute-start(f32[80,128]{1,0:T(8,128)S(1)} %get-tuple-element.44), channel_id=1, source_target_pairs={{0,16},{16,0},{32,48},{48,32},{64,80},{80,64},{96,112},{112,96},{1... | collective-permute-start | bytes 122888 | tf_op jit(solution)/shard_map/ppermute | solution.py:532
  25.3 1.4 %collective-permute-start.5 = (f32[80,128]{1,0:T(8,128)S(1)}, f32[80,128]{1,0:T(8,128)S(1)}, u32[]{:S(2)}, u32[]{:S(2)}) collective-permute-start(f32[80,128]{1,0:T(8,128)S(1)} %get-tuple-element.45), channel_id=1, source_target_pairs={{16,32},{32,16},{48,64},{64,48},{80,96},{96,80},{112,128},{128,112... | collective-permute-start | bytes 122888 | tf_op jit(solution)/shard_map/ppermute | solution.py:532
  27.4 3.3 %collective-permute-start.6 = (f32[96,128]{1,0:T(8,128)S(1)}, f32[96,128]{1,0:T(8,128)S(1)}, u32[]{:S(2)}, u32[]{:S(2)}) collective-permute-start(f32[96,128]{1,0:T(8,128)S(1)} %get-tuple-element.49), channel_id=1, source_target_pairs={{0,1},{1,0},{2,3},{3,2},{4,5},{5,4},{6,7},{7,6},{8,9},{9,8},{10,11... | collective-permute-start | bytes 147464 | tf_op jit(solution)/shard_map/ppermute | solution.py:532
  27.5 5.4 %collective-permute-start.7 = (f32[96,128]{1,0:T(8,128)S(1)}, f32[96,128]{1,0:T(8,128)S(1)}, u32[]{:S(2)}, u32[]{:S(2)}) collective-permute-start(f32[96,128]{1,0:T(8,128)S(1)} %get-tuple-element.50), channel_id=1, source_target_pairs={{1,2},{2,1},{3,4},{4,3},{5,6},{6,5},{7,8},{8,7},{9,10},{10,9},{11,... | collective-permute-start | bytes 147464 | tf_op jit(solution)/shard_map/ppermute | solution.py:532
  36.3 10.9 %collective-permute-start.10 = (f32[32,128]{1,0:T(8,128)S(1)}, f32[32,128]{1,0:T(8,128)S(1)}, u32[]{:S(2)}, u32[]{:S(2)}) collective-permute-start(f32[32,128]{1,0:T(8,128)S(1)} %get-tuple-element.60), channel_id=1, source_target_pairs={{0,1},{1,0},{2,3},{3,2},{4,5},{5,4},{6,7},{7,6},{8,9},{9,8},{10,11... | collective-permute-start | bytes 49160 | tf_op jit(solution)/shard_map/ppermute | solution.py:532
  36.3 10.9 %collective-permute-start.11 = (f32[32,128]{1,0:T(8,128)S(1)}, f32[32,128]{1,0:T(8,128)S(1)}, u32[]{:S(2)}, u32[]{:S(2)}) collective-permute-start(f32[32,128]{1,0:T(8,128)S(1)} %get-tuple-element.61), channel_id=1, source_target_pairs={{1,2},{2,1},{3,4},{4,3},{5,6},{6,5},{7,8},{8,7},{9,10},{10,9},{11,... | collective-permute-start | bytes 49160 | tf_op jit(solution)/shard_map/ppermute | solution.py:532
  40.0 7.2 %collective-permute-start.8 = (f32[16,128]{1,0:T(8,128)S(1)}, f32[16,128]{1,0:T(8,128)S(1)}, u32[]{:S(2)}, u32[]{:S(2)}) collective-permute-start(f32[16,128]{1,0:T(8,128)S(1)} %get-tuple-element.58), channel_id=1, source_target_pairs={{0,16},{16,0},{32,48},{48,32},{64,80},{80,64},{96,112},{112,96},{1... | collective-permute-start | bytes 24584 | tf_op jit(solution)/shard_map/ppermute | solution.py:532
  46.2 1.0 %collective-permute-start.9 = (f32[16,128]{1,0:T(8,128)S(1)}, f32[16,128]{1,0:T(8,128)S(1)}, u32[]{:S(2)}, u32[]{:S(2)}) collective-permute-start(f32[16,128]{1,0:T(8,128)S(1)} %get-tuple-element.59), channel_id=1, source_target_pairs={{16,32},{32,16},{48,64},{64,48},{80,96},{96,80},{112,128},{128,112... | collective-permute-start | bytes 24584 | tf_op jit(solution)/shard_map/ppermute | solution.py:532

commit v3 on v2

--- a/solution.py
+++ b/solution.py
@@ -22,7 +22,9 @@
 AY_ROWS = 2 * EX
 BX_EDGE = R
 BX_COL = BX_EDGE + 16
-BX_ROWS = BX_COL + R
+BX_RING = BX_COL + R
+BX_ROWS = BX_RING + 112
+RING_EFF, RING_NEXT, RING_TRANS, RING_VECTOR, RING_STATIC = 81, 90, 99, 103, 104
 
 CENTER, EAST, WEST, NORTH, SOUTH, SCALE = range(6)
 
@@ -120,7 +122,7 @@
     msg2[pl.ds(AX_COL, R), :] = packed
 
 
-def inverse_kernel(diag, wells, out):
+def inverse_kernel(diag, couple, trans, wells, out, pack_left, pack_right, rows_up, rows_down):
     boost = WELL_BOOST * wells[...].astype(jnp.float32)
     a = [[diag[i, j] + boost if i == j else diag[i, j] for j in range(NC)] for i in range(NC)]
     for k in range(NC):
@@ -133,6 +135,33 @@
     for i in range(NC):
         for j in range(NC):
             out[i, j] = a[i][j]
+    entries = []
+    for k in range(NC):
+        for c in range(NC):
+            total = couple[c, 0] * a[0][k]
+            for m in range(1, NC):
+                total = total + couple[c, m] * a[m][k]
+            entries.append((total, 0, NC * k + c))
+    for c in range(NC):
+        entries.append((diag[c, 0] + boost if c == 0 else diag[c, 0], 0, RING_EFF + c))
+        entries.append((couple[c, 0], 1, RING_NEXT + c))
+    for d in range(4):
+        entries.append((trans[d], 0, RING_TRANS + d))
+    pack_left[...] = pack_columns([(v, inward, place) for v, inward, place in entries])
+    pack_right[...] = pack_columns([(v, L - 1 - inward, place) for v, inward, place in entries])
+    zero = jnp.zeros((1, L), jnp.float32)
+
+    @pl.when(pl.program_id(0) == 0)
+    def _():
+        rows_down[pl.ds(RING_STATIC - 1, 1), :] = zero
+        for v, inward, place in entries:
+            rows_down[pl.ds(place, 1), :] = v[inward : inward + 1, :]
+
+    @pl.when(pl.program_id(0) == R // 8 - 1)
+    def _():
+        rows_up[pl.ds(RING_STATIC - 1, 1), :] = zero
+        for v, inward, place in entries:
+            rows_up[pl.ds(place, 1), :] = v[7 - inward : 8 - inward, :]
 
 
 def setup_middle_kernel(par, got1, got2, own, cols, couple0, trans, weights, msg1, msg2, ext, ext_cols, edges):
@@ -267,17 +296,17 @@
     return trans[0] * east + trans[1] * west + trans[2] * north + trans[3] * south
 
 
-def ghost_sum(trans, up_row, down_row, right_col, left_col):
-    rows, lanes = iotas((R, L))
-    return (
-        jnp.where(rows == R - 1, trans[0] * up_row, 0.0)
-        + jnp.where(rows == 0, trans[1] * down_row, 0.0)
-        + jnp.where(lanes == L - 1, trans[2] * right_col, 0.0)
-        + jnp.where(lanes == 0, trans[3] * left_col, 0.0)
-    )
-
-
-def one_step(pressure, vector, edges, col_right, col_left, diag, inverse, couple, trans, boost, z_out, product_out):
+def ghost_rows(trans, up_row, down_row):
+    rows, _ = iotas((R, L))
+    return jnp.where(rows == R - 1, trans[0] * up_row, 0.0) + jnp.where(rows == 0, trans[1] * down_row, 0.0)
+
+
+def ghost_columns(trans, right_col, left_col):
+    _, lanes = iotas((R, L))
+    return jnp.where(lanes == L - 1, trans[2] * right_col, 0.0) + jnp.where(lanes == 0, trans[3] * left_col, 0.0)
+
+
+def one_step(pressure, vector, edges, col_right, col_left, diag, inverse, couple, trans, boost, z_out):
     p = pressure[0:R, 0:L]
     up_row, down_row = (pressure[R : R + 1, 0:L], pressure[EX - 1 : EX, 0:L])
     far = pressure[0:R, L:EY]
@@ -296,32 +325,24 @@
             ghost_column(col_left, 64, 0, c) * left_p,
         )
         second.append(vector[c] - (own - around))
-    z = []
+    rest = []
     for c in range(NC):
         total = inverse[c, 0] * second[0]
         for k in range(1, NC):
             total = total + inverse[c, k] * second[k]
-        if c == 0:
-            total = total + p
-        z_out[c] = total
-        z.append(total)
-    result = []
-    for c in range(NC):
-        product = couple[c, 0] * z[0]
-        own = diag[c, 0] * z[0]
+        rest.append(total)
+        z_out[c] = total + p if c == 0 else total
+    products = []
+    for c in range(NC):
+        product = couple[c, 0] * rest[0]
         for k in range(1, NC):
-            product = product + couple[c, k] * z[k]
-            own = own + diag[c, k] * z[k]
-        product_out[c] = product
-        own = own + boost * z[c]
-        zero = jnp.zeros((1, L), jnp.float32)
-        around = neighbour_sum(product, trans, zero, zero, 0.0, 0.0)
-        result.append(own - around - vector[c])
-    return result
+            product = product + couple[c, k] * rest[k]
+        products.append(product)
+    return products
 
 
 def first_step_kernel(
-    par, got1, got2, ext, ext_cols, edges, rhs, trans, weights, wells, diag, inverse, couple,
+    par, got1, got2, ext, ext_cols, edges, rhs, trans, weights, wells, diag, inverse, couple, rows_up, rows_down,
     msg1, msg2, z_out, partial, product, coeffs, cols_right, cols_left, pressure_part, product_cols,
 ):
     rows, lanes = iotas((EX, L))
@@ -359,16 +380,22 @@
     pressure = vcycle(source, coeffs)
     boost = WELL_BOOST * wells[...].astype(jnp.float32)
     vector = [rhs[c] for c in range(NC)]
-    result = one_step(
-        pressure, vector, edges, right[0:R], left[0:R], diag, inverse, couple, trans, boost, z_out, product
-    )
+    products = one_step(
+        pressure, vector, edges, right[0:R], left[0:R], diag, inverse, couple, trans, boost, z_out
+    )
+    put(par, 0, msg1, msg2, pl.ds(BX_RING, RING_STATIC), rows_up[...], rows_down[...])
     weighed = jnp.zeros((R, L), jnp.float32)
+    zero = jnp.zeros((1, L), jnp.float32)
     parts = []
     for c in range(NC):
-        partial[c] = result[c]
-        weighed = weighed + weights[c] * result[c]
-        put(par, 0, msg1, msg2, pl.ds(BX_EDGE + c, 1), product[c, R - 1 : R, :], product[c, 0:1, :])
-        parts += [(product[c], 0, c), (product[c], L - 1, NC + c)]
+        product[c] = products[c]
+        value = -neighbour_sum(products[c], trans, zero, zero, 0.0, 0.0)
+        partial[c] = value
+        weighed = weighed + weights[c] * value
+        last, first = (slice(R - 1, R), slice(0, 1))
+        put(par, 0, msg1, msg2, pl.ds(BX_EDGE + c, 1), products[c][last], products[c][first])
+        put(par, 0, msg1, msg2, pl.ds(BX_RING + RING_VECTOR + c, 1), value[last], value[first])
+        parts += [(products[c], 0, c), (products[c], L - 1, NC + c)]
     blank = jnp.zeros((16 - NC, L), jnp.float32)
     columns = pack_columns(parts)
     pressure_part[...] = weighed
@@ -379,10 +406,14 @@
         msg[pl.ds(BX_COL, R), :] = columns
 
 
-def between_kernel(par, got1, got2, pressure_part, product_cols, product, edges, trans, weights, msg1, msg2, ext, ext_cols, rows_out):
+def between_kernel(
+    par, got1, got2, pressure_part, product_cols, product, edges, trans, weights, partial, pack_left, pack_right,
+    msg1, msg2, ext, ext_cols, rows_out, vector_out,
+):
     rows, lanes = iotas((EX, L))
     t_up, t_down = (trans[0, R - 1 : R, :], trans[1, 0:1, :])
     own_up, own_down, far_up, far_down = (jnp.zeros((1, L), jnp.float32) for _ in range(4))
+    to_right, to_left = ([], [])
     for c in range(NC):
         up, down = take(par, 0, got1, got2, pl.ds(BX_EDGE + c, 1))
         rows_out[pl.ds(c, 1), :] = up
@@ -391,6 +422,10 @@
         own_down = own_down + t_down * weights[c, 0:1, :] * down
         far_up = far_up + edges[pl.ds(2 * NC + c, 1), :] * product[c, R - 1 : R, :]
         far_down = far_down + edges[pl.ds(3 * NC + c, 1), :] * product[c, 0:1, :]
+        value = partial[c] - ghost_rows(trans, up, down)
+        vector_out[c] = value
+        to_right.append((value, L - 1, RING_VECTOR + c))
+        to_left.append((value, 0, RING_VECTOR + c))
     up, down = take(par, 0, got1, got2, pl.ds(0, R))
     field = jnp.concatenate([pressure_part[...], up, down], axis=0)
     edge = jnp.where(rows == R - 1, own_up, 0.0) + jnp.where(rows == 0, own_down, 0.0)
@@ -406,12 +441,73 @@
         jnp.where(near, lane_roll(field, HALO), lane_roll(packed, HALO - NC)),
         jnp.where(near, field, lane_roll(packed, HALO)),
     )
+    fixed = iotas((R, L))[1] < RING_VECTOR
+    put(
+        par, 1, msg1, msg2, pl.ds(EX, R),
+        jnp.where(fixed, pack_right[...], pack_columns(to_right)),
+        jnp.where(fixed, pack_left[...], pack_columns(to_left)),
+    )
+
+
+def row_ring(ring, outward, inward, pressure, row, out_row, own_row, edge_cols, product_row, couple_row, corners, old_corners):
+    lanes = iotas((1, L))[1]
+    line = pressure[row : row + 1, :]
+    p = line[:, 0:L]
+    p_right, p_left = (line[:, L : L + 1], line[:, EY - 1 : EY])
+    p_out, p_own = (pressure[out_row : out_row + 1, 0:L], pressure[own_row : own_row + 1, 0:L])
+    t_out, t_in = (ring(RING_TRANS + outward), ring(RING_TRANS + inward))
+    t_right, t_left = (ring(RING_TRANS + 2), ring(RING_TRANS + 3))
+    second = []
+    for c in range(NC):
+        beside = edge_cols(c) * p
+        old_right, old_left = (ghost_column(old_corners[0], 64, L - 1, c), ghost_column(old_corners[1], 64, 0, c))
+        new_right, new_left = (ghost_column(corners[0], HALO, L - 1, c), ghost_column(corners[1], HALO, 0, c))
+        north = jnp.where(lanes == L - 1, old_right * p_right, shifted(beside, 1, 1))
+        south = jnp.where(lanes == 0, old_left * p_left, shifted(beside, 1, -1))
+        value = ring(RING_VECTOR + c) - t_in * product_row(c)
+        value = value - jnp.where(lanes == L - 1, t_right * new_right, 0.0)
+        value = value - jnp.where(lanes == 0, t_left * new_left, 0.0)
+        second.append(
+            value
+            - ring(RING_EFF + c) * p
+            + t_out * (ring(RING_NEXT + c) * p_out)
+            + t_in * (couple_row(c) * p_own)
+            + t_right * north
+            + t_left * south
+        )
+    return second
+
+
+def column_ring(pack, outward, inward, p, p_out, p_own, p_up, p_down, own_couple, own_product, beside_up, beside_down):
+    lanes = iotas((R, L))[1]
+
+    def trans(d):
+        return pack[:, RING_TRANS + d : RING_TRANS + d + 1]
+
+    second = (
+        lane_roll(pack, -RING_VECTOR)
+        - trans(inward) * own_product
+        - lane_roll(pack, -RING_EFF) * p
+        + trans(outward) * (lane_roll(pack, -RING_NEXT) * p_out)
+        + trans(inward) * (own_couple * p_own)
+        + trans(0) * (beside_up * p_up)
+        + trans(1) * (beside_down * p_down)
+    )
+    spread = jnp.zeros((R, L), jnp.float32)
+    for k in range(NC):
+        within = jnp.logical_and(lanes >= NC * k, lanes < NC * k + NC)
+        spread = jnp.where(within, second[:, k : k + 1], spread)
+    terms = pack * spread
+    total = terms
+    for k in range(1, NC):
+        total = total + lane_roll(terms, -NC * k)
+    return total
 
 
 def second_step_kernel(
-    par, got1, got2, ext, ext_cols, rows_in, setup_cols, cols_right, cols_left, edges, coeffs, partial, trans, wells,
-    diag, inverse, couple,
-    msgx1, msgx2, msgy1, msgy2, z_out, vector_out, remainder, product,
+    par, got1, got2, gotx1, gotx2, ext, ext_cols, rows_in, setup_cols, cols_right, cols_left, edges, coeffs, partial,
+    product, rhs, trans, wells, diag, inverse, couple,
+    z_out, dots, ring_up, ring_down,
 ):
     rows, lanes = iotas((EX, L))
     right, left = take(par, 1, got1, got2, pl.ds(0, EX))
@@ -429,47 +525,60 @@
     pressure = vcycle(jnp.concatenate([near, far], axis=1), coeffs)
     vector = []
     for c in range(NC):
-        ghosts = ghost_sum(
-            trans,
-            rows_in[pl.ds(c, 1), :],
-            rows_in[pl.ds(NC + c, 1), :],
-            ghost_column(right[0:R], HALO, L - 1, c),
-            ghost_column(left[0:R], HALO, 0, c),
+        columns = ghost_columns(
+            trans, ghost_column(right[0:R], HALO, L - 1, c), ghost_column(left[0:R], HALO, 0, c)
         )
-        value = partial[c] - ghosts
-        vector_out[c] = value
-        vector.append(value)
+        vector.append(partial[c] - columns)
     boost = WELL_BOOST * wells[...].astype(jnp.float32)
-    result = one_step(
-        pressure, vector, edges, old_right[0:R], old_left[0:R], diag, inverse, couple, trans, boost, z_out, product
-    )
-    to_right, to_left = ([], [])
-    for c in range(NC):
-        remainder[c] = result[c]
-        put(par, 0, msgx1, msgx2, pl.ds(c, 1), product[c, R - 1 : R, :], product[c, 0:1, :])
-        to_right.append((product[c], L - 1, c))
-        to_left.append((product[c], 0, c))
-    blank = jnp.zeros((16 - NC, L), jnp.float32)
-    msgx1[pl.ds(NC, 16 - NC), :] = blank
-    msgx2[pl.ds(NC, 16 - NC), :] = blank
-    put(par, 1, msgy1, msgy2, pl.ds(0, R), pack_columns(to_right), pack_columns(to_left))
-
-
-def dots_kernel(par, gotx1, gotx2, goty1, goty2, rhs, vector, remainder, trans, out):
-    right, left = take(par, 1, goty1, goty2, pl.ds(0, R))
+    products = one_step(
+        pressure, vector, edges, old_right[0:R], old_left[0:R], diag, inverse, couple, trans, boost, z_out
+    )
+    up, down = take(par, 0, gotx1, gotx2, pl.ds(BX_RING, 112))
+    ring_up[...] = up
+    ring_down[...] = down
+    second_up = row_ring(
+        lambda i: ring_up[pl.ds(i, 1), :], 0, 1, pressure, R, R + 1, R - 1,
+        lambda c: edges[pl.ds(c, 1), :], lambda c: product[c, R - 1 : R, :], lambda c: couple[c, 0, R - 1 : R, :],
+        (right[R : R + 1], left[R : R + 1]), (old_right[R : R + 1], old_left[R : R + 1]),
+    )
+    second_down = row_ring(
+        lambda i: ring_down[pl.ds(i, 1), :], 1, 0, pressure, EX - 1, EX - 2, 0,
+        lambda c: edges[pl.ds(NC + c, 1), :], lambda c: product[c, 0:1, :], lambda c: couple[c, 0, 0:1, :],
+        (right[EX - 1 : EX], left[EX - 1 : EX]), (old_right[EX - 1 : EX], old_left[EX - 1 : EX]),
+    )
+    product_up = ring_up[pl.ds(0, NC), :] * second_up[0]
+    product_down = ring_down[pl.ds(0, NC), :] * second_down[0]
+    for k in range(1, NC):
+        product_up = product_up + ring_up[pl.ds(NC * k, NC), :] * second_up[k]
+        product_down = product_down + ring_down[pl.ds(NC * k, NC), :] * second_down[k]
+    pack_right, pack_left = take(par, 1, got1, got2, pl.ds(EX, R))
+    far_p = pressure[:, L:EY]
+    far_up, far_down = (shifted(far_p, 0, 1)[0:R], shifted(far_p, 0, -1)[0:R])
+    far_p, near_p = (far_p[0:R], pressure[0:R, 0:L])
+    right_cols = column_ring(
+        pack_right, 2, 3, far_p[:, 0:1], far_p[:, 1:2], near_p[:, L - 1 : L], far_up[:, 0:1], far_down[:, 0:1],
+        lane_roll(tw[0:R], -2 * NC), lane_roll(packed[0:R], -NC),
+        lane_roll(shifted(old_right, 0, 1)[0:R], -64), lane_roll(shifted(old_right, 0, -1)[0:R], -64),
+    )
+    left_cols = column_ring(
+        pack_left, 3, 2, far_p[:, L - 1 : L], far_p[:, L - 2 : L - 1], near_p[:, 0:1], far_up[:, L - 1 : L],
+        far_down[:, L - 1 : L], tw[0:R], packed[0:R],
+        lane_roll(shifted(old_left, 0, 1)[0:R], -64), lane_roll(shifted(old_left, 0, -1)[0:R], -64),
+    )
     sums = [jnp.zeros((R, L), jnp.float32) for _ in range(6)]
     for c in range(NC):
-        up, down = take(par, 0, gotx1, gotx2, pl.ds(c, 1))
-        ghosts = ghost_sum(trans, up, down, ghost_column(right, 0, L - 1, c), ghost_column(left, 0, 0, c))
-        two = remainder[c] - ghosts
+        two = -neighbour_sum(
+            products[c], trans, product_up[c : c + 1], product_down[c : c + 1],
+            ghost_column(right_cols, 0, L - 1, c), ghost_column(left_cols, 0, 0, c),
+        )
         zero, one = (rhs[c], vector[c])
         for k, (a, b) in enumerate(((zero, zero), (zero, one), (one, one), (zero, two), (one, two), (two, two))):
             sums[k] = sums[k] + a * b
-    lanes = iotas((1, L))[1]
+    lane = iotas((1, L))[1]
     row = jnp.zeros((1, L), jnp.float32)
     for k, total in enumerate(sums):
-        row = jnp.where(lanes == k, jnp.sum(total, keepdims=True), row)
-    out[...] = jnp.broadcast_to(row, out.shape)
+        row = jnp.where(lane == k, jnp.sum(total, keepdims=True), row)
+    dots[...] = jnp.broadcast_to(row, dots.shape)
 
 
 def finish_kernel(gathered, z_one, z_two, out, estimate):
@@ -563,15 +672,16 @@
     got_a1, got_a2 = swap(msg_a1, msg_a2, "gx")
 
     slab = pl.BlockSpec((NC, NC, 8, L), lambda i: (0, 0, i, 0))
-    inverse = pl.pallas_call(
+    strip = pl.BlockSpec((8, L), lambda i: (i, 0))
+    inverse, pack_left, pack_right, rows_up, rows_down = pl.pallas_call(
         inverse_kernel,
         grid=(R // 8,),
-        in_specs=[slab, pl.BlockSpec((8, L), lambda i: (i, 0))],
-        out_specs=slab,
-        out_shape=shape(NC, NC, R, L),
+        in_specs=[slab, slab, pl.BlockSpec((4, 8, L), lambda i: (0, i, 0)), strip],
+        out_specs=[slab, strip, strip, whole(RING_STATIC, L), whole(RING_STATIC, L)],
+        out_shape=[shape(NC, NC, R, L), shape(R, L), shape(R, L), shape(RING_STATIC, L), shape(RING_STATIC, L)],
         cost_estimate=pl.CostEstimate(flops=20_000_000, bytes_accessed=2_700_000, transcendentals=0),
         compiler_params=pltpu.CompilerParams(vmem_limit_bytes=30 * 1024 * 1024),
-    )(diag_blocks, well_mask)
+    )(diag_blocks, couple_blocks, transmissibility, well_mask)
 
     msg_y1, msg_y2, ext, ext_cols, edges = pl.pallas_call(
         setup_middle_kernel,
@@ -590,37 +700,36 @@
     fields = shape(NC, R, L)
     msg_b1, msg_b2, z_one, partial, product, coeffs, cols_right, cols_left, pressure_part, product_cols = call(
         first_step_kernel,
-        [SMEM()] + [VMEM()] * 12,
+        [SMEM()] + [VMEM()] * 14,
         [
             shape(BX_ROWS, L), shape(BX_ROWS, L), fields, fields, fields, shape(18, EX, EY),
             shape(EX, L), shape(EX, L), shape(R, L), shape(R, L),
         ],
     )(
         par, got_y1, got_y2, ext, ext_cols, edges, right_side, transmissibility, pressure_weights, well_mask,
-        diag_blocks, inverse, couple_blocks,
+        diag_blocks, inverse, couple_blocks, rows_up, rows_down,
     )
 
     got_b1, got_b2 = swap(msg_b1, msg_b2, "gx")
-    msg_c1, msg_c2, ext_b, ext_cols_b, rows_b = call(
+    msg_c1, msg_c2, ext_b, ext_cols_b, rows_b, vector_b = call(
         between_kernel,
-        [SMEM()] + [VMEM()] * 8,
-        [shape(EX, L), shape(EX, L), shape(EX, L), shape(EX, L), shape(2 * NC, L)],
-    )(par, got_b1, got_b2, pressure_part, product_cols, product, edges, transmissibility, pressure_weights)
+        [SMEM()] + [VMEM()] * 11,
+        [shape(EX + R, L), shape(EX + R, L), shape(EX, L), shape(EX, L), shape(2 * NC, L), fields],
+    )(
+        par, got_b1, got_b2, pressure_part, product_cols, product, edges, transmissibility, pressure_weights,
+        partial, pack_left, pack_right,
+    )
     got_c1, got_c2 = swap(msg_c1, msg_c2, "gy")
 
-    msg_x1, msg_x2, msg_z1, msg_z2, z_two, vector, remainder, _ = call(
+    devices = lax.axis_size("gx") * lax.axis_size("gy")
+    z_two, local = call(
         second_step_kernel,
-        [SMEM()] + [VMEM()] * 16,
-        [shape(16, L), shape(16, L), shape(R, L), shape(R, L), fields, fields, fields, fields],
+        [SMEM()] + [VMEM()] * 20,
+        [fields, shape(devices, L)],
+        [pltpu.VMEM((112, L), jnp.float32), pltpu.VMEM((112, L), jnp.float32)],
     )(
-        par, got_c1, got_c2, ext_b, ext_cols_b, rows_b, ext_cols, cols_right, cols_left, edges, coeffs, partial,
-        transmissibility, well_mask, diag_blocks, inverse, couple_blocks,
-    )
-    got_x1, got_x2 = swap(msg_x1, msg_x2, "gx")
-    got_z1, got_z2 = swap(msg_z1, msg_z2, "gy")
-    devices = lax.axis_size("gx") * lax.axis_size("gy")
-    (local,) = call(dots_kernel, [SMEM()] + [VMEM()] * 8, [shape(devices, L)])(
-        par, got_x1, got_x2, got_z1, got_z2, right_side, vector, remainder, transmissibility
+        par, got_c1, got_c2, got_b1, got_b2, ext_b, ext_cols_b, rows_b, ext_cols, cols_right, cols_left, edges, coeffs,
+        vector_b, product, right_side, transmissibility, well_mask, diag_blocks, inverse, couple_blocks,
     )
     gathered = lax.all_to_all(local, ("gx", "gy"), 0, 0, tiled=True)
     answer, estimate = call(finish_kernel, [VMEM()] * 3, [fields, shape(1, 1)])(gathered, z_one, z_two)

time: 83.8 us -> 73.4 us (0.88)
  starting transfers between devices: 26.9 us -> 17.7 us
  waiting for transfers between devices: 7.6 us -> 5.74 us
  Pallas kernels: 13.5 us -> 14.5 us
    ppermute x6 -> x4, starting transfers between devices: 16 us -> 9.78 us  [swap(): lax.ppermute(first, axis, pairs)]
    ppermute x6 -> x4, starting transfers between devices: 11 us -> 7.95 us  [swap(): lax.ppermute(second, axis, others)]
    ppermute x6 -> x4, waiting for transfers between devices: 4.82 us -> 2.74 us  [swap(): lax.ppermute(second, axis, others)]
    pallas_call x5 -> x4, Pallas kernels: 9.81 us -> 10.8 us  [the longest x1 3.55 us: on_device(): call(second_step_kernel, [SMEM()] + [VMEM()] * 20, [fields, shape(devices...]
    ppermute x6 -> x4, waiting for transfers between devices: 2.77 us -> 3 us  [swap(): lax.ppermute(first, axis, pairs)]
  transfers between devices with their start and end apart: 12 -> 8, of which waited for: 5 -> 4; matrix products, arithmetic and copies ran while one was open for 0% -> 0% of each run, Pallas kernels for 2% -> 4%
where the time goes in v3:
time: 73.4 us; the launch traced here: 73.1 us
  blocking collectives  34.3 us (47%)
  starting transfers between devices  17.7 us (24%)
  Pallas kernels  14.5 us (20%)
  waiting for transfers between devices  5.74 us (8%)
  between operations  0.79 us (1%)
    all_to_all x1, blocking collectives, on_device(): gathered = lax.all_to_all(local, ('gx', 'gy'), 0, 0, tiled=True)  34.3 us
    ppermute x4, starting transfers between devices, swap(): lax.ppermute(first, axis, pairs)  9.78 us
    ppermute x4, starting transfers between devices, swap(): lax.ppermute(second, axis, others)  7.95 us
    pallas_call x1, Pallas kernels, on_device(): call(second_step_kernel, [SMEM()] + [VMEM()] * 20, [fields, shape(devices...  3.55 us
    pallas_call x1, Pallas kernels, on_device(): call(first_step_kernel, [SMEM()] + [VMEM()] * 14, [shape(BX_ROWS, L), sha...  3.45 us
    pallas_call x1, Pallas kernels, on_device(): pl.pallas_call(inverse_kernel, grid=(R // 8,), in_specs=[slab, slab, pl.B...  3.09 us
    ppermute x4, waiting for transfers between devices, swap(): lax.ppermute(first, axis, pairs)  3 us
    ppermute x4, waiting for transfers between devices, swap(): lax.ppermute(second, axis, others)  2.74 us
  transfers between devices with their start and end apart: 8, of which 4 were waited for; matrix products, arithmetic and copies ran while one was open for 0% of the time, Pallas kernels for 4%

profile of v3, /device:TPU:1, one launch (start us, length us, event | category | flops | bytes accessed | tf_op | source)
XLA Modules:
  0.0 73.1 jit_solution(15857737512749528848)
XLA Ops:
  0.6 0.1 pad_add_fusion.par
  0.7 0.0 copy-start
  0.7 0.0 copy-start.2
  0.7 0.0 copy-start.3
  0.7 2.1 %shard_map.77 = (f32[248,128]{1,0:T(8,128)S(1)}, f32[248,128]{1,0:T(8,128)S(1)}, f32[192,128]{1,0:T(8,128)S(1)}, f32[32,128]{1,0:T(8,128)S(1)}) custom-call(s32[2]{0:T(128)S(1)} %pad_add_fusion.par, f32[9,32,128]{2,1,0:T(8,128)} %rhs.3, f32[9,9,32,128]{3,2,1,0:T(8,128)} %diag.5, f32[9,9,32,128]{3,2,1,0:T(8,128)} %couple.5, f32[4,32,128]{2,1,0:T(8,128)} %trans.9, ...), custom_call_target="tpu_custom_call" | custom-call | flops 20000000 | bytes 1000000 | tf_op jit(solution)/shard_map/pallas_call | solution.py:651
  2.8 0.0 copy-start.1
  2.8 0.0 copy-start.5
  2.8 2.1 %collective-permute-start = (f32[248,128]{1,0:T(8,128)S(1)}, f32[248,128]{1,0:T(8,128)S(1)}, u32[]{:S(2)}, u32[]{:S(2)}) collective-permute-start(f32[248,128]{1,0:T(8,128)S(1)} %get-tuple-element.36), channel_id=1, source_target_pairs={{0,16},{16,0},{32,48},{48,32},{64,80},{80,64},{96,112},{112,96},{1... | collective-permute-start | bytes 380936 | tf_op jit(solution)/shard_map/ppermute | solution.py:641
  4.9 0.7 collective-permute-start.1
  5.6 1.6 %collective-permute-done.got1 = f32[248,128]{1,0:T(8,128)S(1)} collective-permute-done((f32[248,128]{1,0:T(8,128)S(1)}, f32[248,128]{1,0:T(8,128)S(1)}, u32[]{:S(2)}, u32[]{:S(2)}) %collective-permute-start) | collective-permute-done | bytes 127008 | tf_op jit(solution)/shard_map/ppermute | solution.py:641
  7.2 0.0 collective-permute-done.1.got2
  7.2 0.0 copy-done
  7.2 0.0 copy-done.2
  7.2 0.0 copy-done.3
  7.3 0.8 %shard_map.78 = (f32[192,128]{1,0:T(8,128)S(1)}, f32[192,128]{1,0:T(8,128)S(1)}, f32[6,96,128]{2,1,0:T(8,128)S(1)}, f32[96,128]{1,0:T(8,128)S(1)}, f32[36,128]{1,0:T(8,128)S(1)}) custom-call(s32[2]{0:T(128)S(1)} %pad_add_fusion.par, f32[248,128]{1,0:T(8,128)S(1)} %collective-permute-done.got1, f32[248,128]{1,0:T(8,128)S(1)} %collective-permute-done.1.got2, ...), custom_call_target="tpu_custom_call" | custom-call | tf_op jit(solution)/shard_map/pallas_call | solution.py:686
  8.0 3.9 %collective-permute-start.2 = (f32[192,128]{1,0:T(8,128)S(1)}, f32[192,128]{1,0:T(8,128)S(1)}, u32[]{:S(2)}, u32[]{:S(2)}) collective-permute-start(f32[192,128]{1,0:T(8,128)S(1)} %get-tuple-element.40), channel_id=1, source_target_pairs={{0,1},{1,0},{2,3},{3,2},{4,5},{5,4},{6,7},{7,6},{8,9},{9,8},{10,11... | collective-permute-start | bytes 294920 | tf_op jit(solution)/shard_map/ppermute | solution.py:641
  11.9 0.0 copy-start.4
  11.9 2.1 %collective-permute-start.3 = (f32[192,128]{1,0:T(8,128)S(1)}, f32[192,128]{1,0:T(8,128)S(1)}, u32[]{:S(2)}, u32[]{:S(2)}) collective-permute-start(f32[192,128]{1,0:T(8,128)S(1)} %get-tuple-element.41), channel_id=1, source_target_pairs={{1,2},{2,1},{3,4},{4,3},{5,6},{6,5},{7,8},{8,7},{9,10},{10,9},{11,... | collective-permute-start | bytes 294920 | tf_op jit(solution)/shard_map/ppermute | solution.py:641
  14.0 0.0 copy-done.1
  14.0 0.0 copy-done.5
  14.0 3.1 %shard_map.79 = (f32[9,9,32,128]{3,2,1,0:T(8,128)S(1)}, f32[32,128]{1,0:T(8,128)S(1)}, f32[32,128]{1,0:T(8,128)S(1)}, f32[104,128]{1,0:T(8,128)S(1)}, f32[104,128]{1,0:T(8,128)S(1)}) custom-call(f32[9,9,32,128]{3,2,1,0:T(8,128)S(1)} %copy-done.1, f32[9,9,32,128]{3,2,1,0:T(8,128)S(1)} %copy-done, f32[4,32,128]{2,1,0:T(8,128)S(1)} %copy-done.2, ...), custom_call_target="tpu_custom_call" | custom-call | flops 20000000 | bytes 2700000 | tf_op jit(solution)/shard_map/pallas_call | solution.py:676
  17.1 0.0 collective-permute-done.2.got1
  17.2 0.8 %collective-permute-done.3.got2 = f32[192,128]{1,0:T(8,128)S(1)} collective-permute-done((f32[192,128]{1,0:T(8,128)S(1)}, f32[192,128]{1,0:T(8,128)S(1)}, u32[]{:S(2)}, u32[]{:S(2)}) %collective-permute-start.3) | collective-permute-done | bytes 98336 | tf_op jit(solution)/shard_map/ppermute | solution.py:641
  18.0 0.0 copy-done.4
  18.0 3.5 %shard_map.80 = (f32[192,128]{1,0:T(8,128)S(1)}, f32[192,128]{1,0:T(8,128)S(1)}, f32[9,32,128]{2,1,0:T(8,128)S(1)}, f32[9,32,128]{2,1,0:T(8,128)S(1)}, f32[9,32,...) custom-call(s32[2]{0:T(128)S(1)} %pad_add_fusion.par, ...), custom_call_target="tpu_custom_call" | custom-call | flops 20000000 | bytes 1000000 | tf_op jit(solution)/shard_map/pallas_call | solution.py:701
  21.4 3.7 %collective-permute-start.4 = (f32[192,128]{1,0:T(8,128)S(1)}, f32[192,128]{1,0:T(8,128)S(1)}, u32[]{:S(2)}, u32[]{:S(2)}) collective-permute-start(f32[192,128]{1,0:T(8,128)S(1)} %get-tuple-element.48), channel_id=1, source_target_pairs={{0,16},{16,0},{32,48},{48,32},{64,80},{80,64},{96,112},{112,96},{1... | collective-permute-start | bytes 294920 | tf_op jit(solution)/shard_map/ppermute | solution.py:641
  25.1 0.7 collective-permute-start.5
  25.8 1.3 %collective-permute-done.4.got1.gotx1 = f32[192,128]{1,0:T(8,128)S(1)} collective-permute-done((f32[192,128]{1,0:T(8,128)S(1)}, f32[192,128]{1,0:T(8,128)S(1)}, u32[]{:S(2)}, u32[]{:S(2)}) %collective-permute-start.4) | collective-permute-done | bytes 98336 | tf_op jit(solution)/shard_map/ppermute | solution.py:641
  27.1 0.0 collective-permute-done.5.got2.gotx2
  27.1 0.7 %shard_map.81 = (f32[128,128]{1,0:T(8,128)S(1)}, f32[128,128]{1,0:T(8,128)S(1)}, f32[96,128]{1,0:T(8,128)S(1)}, f32[96,128]{1,0:T(8,128)S(1)}, f32[18,128]{1,0:T(8,128)S(1)}, /*index=5*/f32[9,32,128]{2,1,0:T(8,128)S(1)}) custom-call(s32[2]{0:T(128)S(1)} %pad_add_fusion.par, f32[192,128]{1,0:T(8,128)S(1)} %collective-permute-done.4.got1.gotx1, ...), custom_call_target="tpu_custom_call" | custom-call | flops 20000000 | bytes 1000000 | tf_op jit(solution)/shard_map/pallas_call | solution.py:714
  27.9 0.1 collective-permute-start.6
  28.0 4.5 %collective-permute-start.7 = (f32[128,128]{1,0:T(8,128)S(1)}, f32[128,128]{1,0:T(8,128)S(1)}, u32[]{:S(2)}, u32[]{:S(2)}) collective-permute-start(f32[128,128]{1,0:T(8,128)S(1)} %get-tuple-element.57), channel_id=1, source_target_pairs={{1,2},{2,1},{3,4},{4,3},{5,6},{6,5},{7,8},{8,7},{9,10},{10,9},{11,... | collective-permute-start | bytes 196616 | tf_op jit(solution)/shard_map/ppermute | solution.py:641
  32.5 0.0 collective-permute-done.6.got1
  32.5 1.9 %collective-permute-done.7.got2 = f32[128,128]{1,0:T(8,128)S(1)} collective-permute-done((f32[128,128]{1,0:T(8,128)S(1)}, f32[128,128]{1,0:T(8,128)S(1)}, u32[]{:S(2)}, u32[]{:S(2)}) %collective-permute-start.7) | collective-permute-done | bytes 65568 | tf_op jit(solution)/shard_map/ppermute | solution.py:641
  34.5 3.5 %shard_map.82 = (f32[9,32,128]{2,1,0:T(8,128)S(1)}, f32[256,128]{1,0:T(8,128)S(1)}) custom-call(s32[2]{0:T(128)S(1)} %pad_add_fusion.par, f32[128,128]{1,0:T(8,128)S(1)} %collective-permute-done.6.got1, f32[128,128]{1,0:T(8,128)S(1)} %collective-permute-done.7.got2, f32[192,128]{1,0:T(8,128)S(1)} %collective-permute-done.4.got1.gotx1, ...), custom_call_target="tpu_custom_call" | custom-call | flops 20000000 | bytes 1000000 | tf_op jit(solution)/shard_map/pallas_call | solution.py:725
  38.0 34.3 %all_to_all.11 = f32[256,1,128]{2,1,0:T(1,128)S(1)} all-to-all(f32[256,1,128]{2,1,0:T(1,128)S(1)} %bitcast.8), channel_id=1, replica_groups=mesh['gx'=16,'gy'=16] {'gx','gy'}, dimensions={0} | all-to-all | bytes 262144 | tf_op jit(solution)/shard_map/all_to_all | solution.py:734
  72.3 0.9 %shard_map.83 = (f32[9,32,128]{2,1,0:T(8,128)}, f32[1,1]{1,0:T(1,128)}) custom-call(f32[256,128]{1,0:T(8,128)S(1)} %bitcast.7, f32[9,32,128]{2,1,0:T(8,128)S(1)} %get-tuple-element.66.z_one, f32[9,32,128]{2,1,0:T(8,128)S(1)} %get-tuple-element.67.z_two), custom_call_target="tpu_custom_call" | custom-call | flops 20000000 | bytes 1000000 | tf_op jit(solution)/shard_map/pallas_call | solution.py:735
Async XLA Ops:
  0.7 6.5 %copy-start = (f32[9,9,32,128]{3,2,1,0:T(8,128)S(1)}, f32[9,9,32,128]{3,2,1,0:T(8,128)}, u32[]{:S(2)}) copy-start(f32[9,9,32,128]{3,2,1,0:T(8,128)} %couple.5) | copy-start | bytes 3981316
  0.7 6.5 %copy-start.2 = (f32[4,32,128]{2,1,0:T(8,128)S(1)}, f32[4,32,128]{2,1,0:T(8,128)}, u32[]{:S(2)}) copy-start(f32[4,32,128]{2,1,0:T(8,128)} %trans.9) | copy-start | bytes 196612
  0.7 6.5 %copy-start.3 = (f32[9,32,128]{2,1,0:T(8,128)S(1)}, f32[9,32,128]{2,1,0:T(8,128)}, u32[]{:S(2)}) copy-start(f32[9,32,128]{2,1,0:T(8,128)} %weights.5) | copy-start | bytes 442372
  2.8 11.2 %copy-start.1 = (f32[9,9,32,128]{3,2,1,0:T(8,128)S(1)}, f32[9,9,32,128]{3,2,1,0:T(8,128)}, u32[]{:S(2)}) copy-start(f32[9,9,32,128]{3,2,1,0:T(8,128)} %diag.5) | copy-start | bytes 3981316
  2.8 11.2 %copy-start.5 = (s32[32,128]{1,0:T(8,128)S(1)}, s32[32,128]{1,0:T(8,128)}, u32[]{:S(2)}) copy-start(s32[32,128]{1,0:T(8,128)} %wells.5) | copy-start | bytes 49156
  2.8 4.4 %collective-permute-start = (f32[248,128]{1,0:T(8,128)S(1)}, f32[248,128]{1,0:T(8,128)S(1)}, u32[]{:S(2)}, u32[]{:S(2)}) collective-permute-start(f32[248,128]{1,0:T(8,128)S(1)} %get-tuple-element.36), channel_id=1, source_target_pairs={{0,16},{16,0},{32,48},{48,32},{64,80},{80,64},{96,112},{112,96},{1... | collective-permute-start | bytes 380936 | tf_op jit(solution)/shard_map/ppermute | solution.py:641
  4.9 2.3 %collective-permute-start.1 = (f32[248,128]{1,0:T(8,128)S(1)}, f32[248,128]{1,0:T(8,128)S(1)}, u32[]{:S(2)}, u32[]{:S(2)}) collective-permute-start(f32[248,128]{1,0:T(8,128)S(1)} %get-tuple-element.37), channel_id=1, source_target_pairs={{16,32},{32,16},{48,64},{64,48},{80,96},{96,80},{112,128},{128,112... | collective-permute-start | bytes 380936 | tf_op jit(solution)/shard_map/ppermute | solution.py:641
  8.0 9.1 %collective-permute-start.2 = (f32[192,128]{1,0:T(8,128)S(1)}, f32[192,128]{1,0:T(8,128)S(1)}, u32[]{:S(2)}, u32[]{:S(2)}) collective-permute-start(f32[192,128]{1,0:T(8,128)S(1)} %get-tuple-element.40), channel_id=1, source_target_pairs={{0,1},{1,0},{2,3},{3,2},{4,5},{5,4},{6,7},{7,6},{8,9},{9,8},{10,11... | collective-permute-start | bytes 294920 | tf_op jit(solution)/shard_map/ppermute | solution.py:641
  11.9 6.1 %copy-start.4 = (f32[9,32,128]{2,1,0:T(8,128)S(1)}, f32[9,32,128]{2,1,0:T(8,128)}, u32[]{:S(2)}) copy-start(f32[9,32,128]{2,1,0:T(8,128)} %rhs.3) | copy-start | bytes 442372
  11.9 6.1 %collective-permute-start.3 = (f32[192,128]{1,0:T(8,128)S(1)}, f32[192,128]{1,0:T(8,128)S(1)}, u32[]{:S(2)}, u32[]{:S(2)}) collective-permute-start(f32[192,128]{1,0:T(8,128)S(1)} %get-tuple-element.41), channel_id=1, source_target_pairs={{1,2},{2,1},{3,4},{4,3},{5,6},{6,5},{7,8},{8,7},{9,10},{10,9},{11,... | collective-permute-start | bytes 294920 | tf_op jit(solution)/shard_map/ppermute | solution.py:641
  21.4 5.7 %collective-permute-start.4 = (f32[192,128]{1,0:T(8,128)S(1)}, f32[192,128]{1,0:T(8,128)S(1)}, u32[]{:S(2)}, u32[]{:S(2)}) collective-permute-start(f32[192,128]{1,0:T(8,128)S(1)} %get-tuple-element.48), channel_id=1, source_target_pairs={{0,16},{16,0},{32,48},{48,32},{64,80},{80,64},{96,112},{112,96},{1... | collective-permute-start | bytes 294920 | tf_op jit(solution)/shard_map/ppermute | solution.py:641
  25.1 2.0 %collective-permute-start.5 = (f32[192,128]{1,0:T(8,128)S(1)}, f32[192,128]{1,0:T(8,128)S(1)}, u32[]{:S(2)}, u32[]{:S(2)}) collective-permute-start(f32[192,128]{1,0:T(8,128)S(1)} %get-tuple-element.49), channel_id=1, source_target_pairs={{16,32},{32,16},{48,64},{64,48},{80,96},{96,80},{112,128},{128,112... | collective-permute-start | bytes 294920 | tf_op jit(solution)/shard_map/ppermute | solution.py:641
  27.9 4.6 %collective-permute-start.6 = (f32[128,128]{1,0:T(8,128)S(1)}, f32[128,128]{1,0:T(8,128)S(1)}, u32[]{:S(2)}, u32[]{:S(2)}) collective-permute-start(f32[128,128]{1,0:T(8,128)S(1)} %get-tuple-element.56), channel_id=1, source_target_pairs={{0,1},{1,0},{2,3},{3,2},{4,5},{5,4},{6,7},{7,6},{8,9},{9,8},{10,11... | collective-permute-start | bytes 196616 | tf_op jit(solution)/shard_map/ppermute | solution.py:641
  28.0 6.5 %collective-permute-start.7 = (f32[128,128]{1,0:T(8,128)S(1)}, f32[128,128]{1,0:T(8,128)S(1)}, u32[]{:S(2)}, u32[]{:S(2)}) collective-permute-start(f32[128,128]{1,0:T(8,128)S(1)} %get-tuple-element.57), channel_id=1, source_target_pairs={{1,2},{2,1},{3,4},{4,3},{5,6},{6,5},{7,8},{8,7},{9,10},{10,9},{11,... | collective-permute-start | bytes 196616 | tf_op jit(solution)/shard_map/ppermute | solution.py:641

commit v4 on v3

--- a/solution.py
+++ b/solution.py
@@ -42,20 +42,20 @@
     return values if shift == 0 else pltpu.roll(values, shift, 1)
 
 
-def even_mask(par_ref, which, shape):
-    return jnp.full(shape, par_ref[which], jnp.int32) == 0
+def first_is_up(par_ref, which, shape):
+    return jnp.broadcast_to(par_ref[which : which + 1, :], shape) == 0
 
 
 def put(par_ref, which, first, second, rows, up, down):
-    even = even_mask(par_ref, which, up.shape)
-    first[rows, :] = jnp.where(even, up, down)
-    second[rows, :] = jnp.where(even, down, up)
+    mask = first_is_up(par_ref, which, up.shape)
+    first[rows, :] = jnp.where(mask, up, down)
+    second[rows, :] = jnp.where(mask, down, up)
 
 
 def take(par_ref, which, first, second, rows):
     one, two = (first[rows, :], second[rows, :])
-    even = even_mask(par_ref, which, one.shape)
-    return (jnp.where(even, one, two), jnp.where(even, two, one))
+    mask = first_is_up(par_ref, which, one.shape)
+    return (jnp.where(mask, one, two), jnp.where(mask, two, one))
 
 
 def pack_columns(parts):
@@ -122,7 +122,7 @@
     msg2[pl.ds(AX_COL, R), :] = packed
 
 
-def inverse_kernel(diag, couple, trans, wells, out, pack_left, pack_right, rows_up, rows_down):
+def inverse_kernel(diag, wells, out):
     boost = WELL_BOOST * wells[...].astype(jnp.float32)
     a = [[diag[i, j] + boost if i == j else diag[i, j] for j in range(NC)] for i in range(NC)]
     for k in range(NC):
@@ -135,12 +135,16 @@
     for i in range(NC):
         for j in range(NC):
             out[i, j] = a[i][j]
+
+
+def ring_kernel(inverse, diag, couple, trans, wells, pack_left, pack_right, rows_up, rows_down):
+    boost = WELL_BOOST * wells[...].astype(jnp.float32)
     entries = []
     for k in range(NC):
         for c in range(NC):
-            total = couple[c, 0] * a[0][k]
+            total = couple[c, 0] * inverse[0, k]
             for m in range(1, NC):
-                total = total + couple[c, m] * a[m][k]
+                total = total + couple[c, m] * inverse[m, k]
             entries.append((total, 0, NC * k + c))
     for c in range(NC):
         entries.append((diag[c, 0] + boost if c == 0 else diag[c, 0], 0, RING_EFF + c))
@@ -164,7 +168,7 @@
             rows_up[pl.ds(place, 1), :] = v[7 - inward : 8 - inward, :]
 
 
-def setup_middle_kernel(par, got1, got2, own, cols, couple0, trans, weights, msg1, msg2, ext, ext_cols, edges):
+def setup_middle_kernel(par, got1, got2, own, cols, couple0, trans, weights, _, msg1, msg2, ext, ext_cols, edges):
     rows, lanes = iotas((EX, L))
 
     def dots(span_of):
@@ -614,8 +618,8 @@
 
 
 VMEM = functools.partial(pl.BlockSpec, memory_space=pltpu.VMEM)
-SMEM = functools.partial(pl.BlockSpec, memory_space=pltpu.SMEM)
 HBM = functools.partial(pl.BlockSpec, memory_space=pltpu.HBM)
+ANY = functools.partial(pl.BlockSpec, memory_space=pl.ANY)
 
 
 def shape(*dims):
@@ -638,11 +642,12 @@
     peers = lax.axis_size(axis)
     pairs = [(i, i ^ 1) for i in range(peers) if i ^ 1 < peers]
     others = [(i, ((i + 1) ^ 1) - 1) for i in range(1, peers) if ((i + 1) ^ 1) - 1 < peers]
-    return (lax.ppermute(first, axis, pairs), lax.ppermute(second, axis, others))
+    return (lax.ppermute(first, axis, others), lax.ppermute(second, axis, pairs))
 
 
 def on_device(right_side, diag_blocks, couple_blocks, transmissibility, pressure_weights, well_mask):
-    par = jnp.stack([lax.axis_index("gx") & 1, lax.axis_index("gy") & 1]).astype(jnp.int32)
+    par = jnp.stack([1 - (lax.axis_index("gx") & 1), 1 - (lax.axis_index("gy") & 1)]).astype(jnp.int32)
+    par = jnp.broadcast_to(par[:, None], (2, L))
     column = pl.BlockSpec((NC, 1, R, L), lambda i: (0, 0, 0, 0))
 
     def whole(*dims):
@@ -650,7 +655,7 @@
 
     msg_a1, msg_a2, own, cols = call(
         setup_kernel,
-        [SMEM()] + [HBM()] * 6,
+        [VMEM()] + [HBM()] * 6,
         [shape(AX_ROWS, L), shape(AX_ROWS, L), shape(6 * R, L), shape(R, L)],
         [
             pltpu.VMEM((NC, R, L), jnp.float32),
@@ -673,34 +678,43 @@
 
     slab = pl.BlockSpec((NC, NC, 8, L), lambda i: (0, 0, i, 0))
     strip = pl.BlockSpec((8, L), lambda i: (i, 0))
-    inverse, pack_left, pack_right, rows_up, rows_down = pl.pallas_call(
+    inverse = pl.pallas_call(
         inverse_kernel,
         grid=(R // 8,),
-        in_specs=[slab, slab, pl.BlockSpec((4, 8, L), lambda i: (0, i, 0)), strip],
-        out_specs=[slab, strip, strip, whole(RING_STATIC, L), whole(RING_STATIC, L)],
-        out_shape=[shape(NC, NC, R, L), shape(R, L), shape(R, L), shape(RING_STATIC, L), shape(RING_STATIC, L)],
+        in_specs=[slab, strip],
+        out_specs=slab,
+        out_shape=shape(NC, NC, R, L),
         cost_estimate=pl.CostEstimate(flops=20_000_000, bytes_accessed=2_700_000, transcendentals=0),
         compiler_params=pltpu.CompilerParams(vmem_limit_bytes=30 * 1024 * 1024),
-    )(diag_blocks, couple_blocks, transmissibility, well_mask)
+    )(diag_blocks, well_mask)
+    pack_left, pack_right, rows_up, rows_down = pl.pallas_call(
+        ring_kernel,
+        grid=(R // 8,),
+        in_specs=[slab, slab, slab, pl.BlockSpec((4, 8, L), lambda i: (0, i, 0)), strip],
+        out_specs=[strip, strip, whole(RING_STATIC, L), whole(RING_STATIC, L)],
+        out_shape=[shape(R, L), shape(R, L), shape(RING_STATIC, L), shape(RING_STATIC, L)],
+        cost_estimate=pl.CostEstimate(flops=20_000_000, bytes_accessed=2_700_000, transcendentals=0),
+        compiler_params=pltpu.CompilerParams(vmem_limit_bytes=30 * 1024 * 1024),
+    )(inverse, diag_blocks, couple_blocks, transmissibility, well_mask)
 
     msg_y1, msg_y2, ext, ext_cols, edges = pl.pallas_call(
         setup_middle_kernel,
         grid=(1,),
         in_specs=[
-            SMEM(), whole(AX_ROWS, L), whole(AX_ROWS, L), whole(6 * R, L), whole(R, L), column,
-            whole(4, R, L), whole(NC, R, L),
+            VMEM(), whole(AX_ROWS, L), whole(AX_ROWS, L), whole(6 * R, L), whole(R, L), column,
+            whole(4, R, L), whole(NC, R, L), ANY(),
         ],
         out_specs=[whole(AY_ROWS, L), whole(AY_ROWS, L), whole(6, EX, L), whole(EX, L), whole(4 * NC, L)],
         out_shape=[shape(AY_ROWS, L), shape(AY_ROWS, L), shape(6, EX, L), shape(EX, L), shape(4 * NC, L)],
         compiler_params=pltpu.CompilerParams(vmem_limit_bytes=30 * 1024 * 1024),
-    )(par, got_a1, got_a2, own, cols, couple_blocks, transmissibility, pressure_weights)
+    )(par, got_a1, got_a2, own, cols, couple_blocks, transmissibility, pressure_weights, inverse)
 
     got_y1, got_y2 = swap(msg_y1, msg_y2, "gy")
 
     fields = shape(NC, R, L)
     msg_b1, msg_b2, z_one, partial, product, coeffs, cols_right, cols_left, pressure_part, product_cols = call(
         first_step_kernel,
-        [SMEM()] + [VMEM()] * 14,
+        [VMEM()] + [VMEM()] * 14,
         [
             shape(BX_ROWS, L), shape(BX_ROWS, L), fields, fields, fields, shape(18, EX, EY),
             shape(EX, L), shape(EX, L), shape(R, L), shape(R, L),
@@ -713,7 +727,7 @@
     got_b1, got_b2 = swap(msg_b1, msg_b2, "gx")
     msg_c1, msg_c2, ext_b, ext_cols_b, rows_b, vector_b = call(
         between_kernel,
-        [SMEM()] + [VMEM()] * 11,
+        [VMEM()] + [VMEM()] * 11,
         [shape(EX + R, L), shape(EX + R, L), shape(EX, L), shape(EX, L), shape(2 * NC, L), fields],
     )(
         par, got_b1, got_b2, pressure_part, product_cols, product, edges, transmissibility, pressure_weights,
@@ -724,7 +738,7 @@
     devices = lax.axis_size("gx") * lax.axis_size("gy")
     z_two, local = call(
         second_step_kernel,
-        [SMEM()] + [VMEM()] * 20,
+        [VMEM()] + [VMEM()] * 20,
         [fields, shape(devices, L)],
         [pltpu.VMEM((112, L), jnp.float32), pltpu.VMEM((112, L), jnp.float32)],
     )(

time: 73.4 us -> 69.7 us (0.950)
  blocking collectives: 34.3 us -> 31 us
  Pallas kernels: 14.5 us -> 12.3 us
  starting transfers between devices: 17.7 us -> 19.3 us
    all_to_all x1, blocking collectives: 34.3 us -> 31 us  [on_device(): gathered = lax.all_to_all(local, ('gx', 'gy'), 0, 0, tiled=True)]
    pallas_call x6 -> x7, Pallas kernels: 13.7 us -> 11.5 us  [the longest x1 2.98 us: on_device(): call(second_step_kernel, [VMEM()] + [VMEM()] * 20, [fields, shape(devices...]
    ppermute x8, starting transfers between devices: 17.7 us -> 19.3 us  [the longest x4 11.1 us: swap(): lax.ppermute(first, axis, others)]
  transfers between devices with their start and end apart: 8 -> 8, of which waited for: 4 -> 3; matrix products, arithmetic and copies ran while one was open for 0% -> 0% of each run, Pallas kernels for 4% -> 5%
where the time goes in v4:
time: 69.7 us; the launch traced here: 69.4 us
  blocking collectives  31 us (44%)
  starting transfers between devices  19.3 us (28%)
  Pallas kernels  12.3 us (18%)
  waiting for transfers between devices  5.81 us (8%)
  between operations  0.81 us (1%)
    all_to_all x1, blocking collectives, on_device(): gathered = lax.all_to_all(local, ('gx', 'gy'), 0, 0, tiled=True)  31 us
    ppermute x4, starting transfers between devices, swap(): lax.ppermute(first, axis, others)  11.1 us
    ppermute x4, starting transfers between devices, swap(): lax.ppermute(second, axis, pairs)  8.21 us
    ppermute x4, waiting for transfers between devices, swap(): lax.ppermute(second, axis, pairs)  3.97 us
    pallas_call x1, Pallas kernels, on_device(): call(second_step_kernel, [VMEM()] + [VMEM()] * 20, [fields, shape(devices...  2.98 us
    pallas_call x1, Pallas kernels, on_device(): call(first_step_kernel, [VMEM()] + [VMEM()] * 14, [shape(BX_ROWS, L), sha...  2.9 us
    pallas_call x1, Pallas kernels, on_device(): pl.pallas_call(ring_kernel, grid=(R // 8,), in_specs=[slab, slab, slab, p...  2.3 us
    ppermute x4, waiting for transfers between devices, swap(): lax.ppermute(first, axis, others)  1.84 us
  transfers between devices with their start and end apart: 8, of which 3 were waited for; matrix products, arithmetic and copies ran while one was open for 0% of the time, Pallas kernels for 5%

profile of v4, /device:TPU:1, one launch (start us, length us, event | category | flops | bytes accessed | tf_op | source)
XLA Modules:
  0.0 69.4 jit_solution(15220292330233213740)
XLA Ops:
  0.6 0.1 pad_add_fusion
  0.7 0.1 broadcast_in_dim.2.par
  0.8 0.0 copy-start
  0.8 0.0 copy-start.5
  0.8 1.6 %shard_map.77 = (f32[248,128]{1,0:T(8,128)S(1)}, f32[248,128]{1,0:T(8,128)S(1)}, f32[192,128]{1,0:T(8,128)S(1)}, f32[32,128]{1,0:T(8,128)S(1)}) custom-call(s32[2,128]{1,0:T(2,128)S(1)} %broadcast_in_dim.2.par, f32[9,32,128]{2,1,0:T(8,128)} %rhs.3, f32[9,9,32,128]{3,2,1,0:T(8,128)} %diag.7, f32[9,9,32,128]{3,2,1,0:T(8,128)} %couple.5, f32[4,32,128]{2,1,0:T(8,128)} %trans.9, ...), custom_call_target="tpu_custom_call" | custom-call | flops 20000000 | bytes 1000000 | tf_op jit(solution)/shard_map/pallas_call | solution.py:656
  2.4 0.7 collective-permute-start
  3.1 0.0 copy-start.1
  3.1 0.0 copy-start.2
  3.1 0.0 copy-start.3
  3.1 4.6 %collective-permute-start.1 = (f32[248,128]{1,0:T(8,128)S(1)}, f32[248,128]{1,0:T(8,128)S(1)}, u32[]{:S(2)}, u32[]{:S(2)}) collective-permute-start(f32[248,128]{1,0:T(8,128)S(1)} %get-tuple-element.36), channel_id=1, source_target_pairs={{0,16},{16,0},{32,48},{48,32},{64,80},{80,64},{96,112},{112,96},{1... | collective-permute-start | bytes 380936 | tf_op jit(solution)/shard_map/ppermute | solution.py:645
  7.7 0.0 copy-done
  7.7 0.0 copy-done.5
  7.7 1.3 %shard_map.78._.inverse = f32[9,9,32,128]{3,2,1,0:T(8,128)S(1)} custom-call(f32[9,9,32,128]{3,2,1,0:T(8,128)S(1)} %copy-done, s32[32,128]{1,0:T(8,128)S(1)} %copy-done.5), custom_call_target="tpu_custom_call" | custom-call | flops 20000000 | bytes 2700000 | tf_op jit(solution)/shard_map/pallas_call | solution.py:681
  9.0 0.0 collective-permute-done.got1
  9.0 1.6 %collective-permute-done.1.got2 = f32[248,128]{1,0:T(8,128)S(1)} collective-permute-done((f32[248,128]{1,0:T(8,128)S(1)}, f32[248,128]{1,0:T(8,128)S(1)}, u32[]{:S(2)}, u32[]{:S(2)}) %collective-permute-start.1) | collective-permute-done | bytes 127008 | tf_op jit(solution)/shard_map/ppermute | solution.py:645
  10.5 0.0 copy-done.1
  10.5 0.0 copy-done.2
  10.5 0.0 copy-done.3
  10.5 0.2 shard_map.79
  10.8 5.0 %collective-permute-start.2 = (f32[192,128]{1,0:T(8,128)S(1)}, f32[192,128]{1,0:T(8,128)S(1)}, u32[]{:S(2)}, u32[]{:S(2)}) collective-permute-start(f32[192,128]{1,0:T(8,128)S(1)} %get-tuple-element.39), channel_id=1, source_target_pairs={{1,2},{2,1},{3,4},{4,3},{5,6},{6,5},{7,8},{8,7},{9,10},{10,9},{11,... | collective-permute-start | bytes 294920 | tf_op jit(solution)/shard_map/ppermute | solution.py:645
  15.8 0.0 copy-start.4
  15.8 0.1 collective-permute-start.3
  15.9 2.3 %shard_map.80 = (f32[32,128]{1,0:T(8,128)S(1)}, f32[32,128]{1,0:T(8,128)S(1)}, f32[104,128]{1,0:T(8,128)S(1)}, f32[104,128]{1,0:T(8,128)S(1)}) custom-call(f32[9,9,32,128]{3,2,1,0:T(8,128)S(1)} %shard_map.78._.inverse, f32[9,9,32,128]{3,2,1,0:T(8,128)S(1)} %copy-done, f32[9,9,32,128]{3,2,1,0:T(8,128)S(1)} %copy-done.1, f32[4,32,128]{2,1,0:T(8,128)S(1)} %copy-done.2, ...), custom_call_target="tpu_custom_call" | custom-call | flops 20000000 | bytes 2700000 | tf_op jit(solution)/shard_map/pallas_call | solution.py:690
  18.2 0.0 collective-permute-done.2.got1
  18.2 0.0 collective-permute-done.3.got2
  18.2 0.0 copy-done.4
  18.2 2.9 %shard_map.81 = (f32[192,128]{1,0:T(8,128)S(1)}, f32[192,128]{1,0:T(8,128)S(1)}, f32[9,32,128]{2,1,0:T(8,128)S(1)}, f32[9,32,128]{2,1,0:T(8,128)S(1)}, f32[9,32,...) custom-call(s32[2,128]{1,0:T(2,128)S(1)} %broadcast_in_dim.2.par, ...), custom_call_target="tpu_custom_call" | custom-call | flops 20000000 | bytes 1000000 | tf_op jit(solution)/shard_map/pallas_call | solution.py:715
  21.1 0.7 collective-permute-start.4
  21.8 3.5 %collective-permute-start.5 = (f32[192,128]{1,0:T(8,128)S(1)}, f32[192,128]{1,0:T(8,128)S(1)}, u32[]{:S(2)}, u32[]{:S(2)}) collective-permute-start(f32[192,128]{1,0:T(8,128)S(1)} %get-tuple-element.47), channel_id=1, source_target_pairs={{0,16},{16,0},{32,48},{48,32},{64,80},{80,64},{96,112},{112,96},{1... | collective-permute-start | bytes 294920 | tf_op jit(solution)/shard_map/ppermute | solution.py:645
  25.2 0.0 collective-permute-done.4.got1.gotx1
  25.2 2.4 %collective-permute-done.5.got2.gotx2 = f32[192,128]{1,0:T(8,128)S(1)} collective-permute-done((f32[192,128]{1,0:T(8,128)S(1)}, f32[192,128]{1,0:T(8,128)S(1)}, u32[]{:S(2)}, u32[]{:S(2)}) %collective-permute-start.5) | collective-permute-done | bytes 98336 | tf_op jit(solution)/shard_map/ppermute | solution.py:645
  27.7 0.2 shard_map.82
  27.9 4.8 %collective-permute-start.6 = (f32[128,128]{1,0:T(8,128)S(1)}, f32[128,128]{1,0:T(8,128)S(1)}, u32[]{:S(2)}, u32[]{:S(2)}) collective-permute-start(f32[128,128]{1,0:T(8,128)S(1)} %get-tuple-element.54), channel_id=1, source_target_pairs={{1,2},{2,1},{3,4},{4,3},{5,6},{6,5},{7,8},{8,7},{9,10},{10,9},{11,... | collective-permute-start | bytes 196616 | tf_op jit(solution)/shard_map/ppermute | solution.py:645
  32.6 0.1 collective-permute-start.7
  32.7 1.8 %collective-permute-done.6.got1 = f32[128,128]{1,0:T(8,128)S(1)} collective-permute-done((f32[128,128]{1,0:T(8,128)S(1)}, f32[128,128]{1,0:T(8,128)S(1)}, u32[]{:S(2)}, u32[]{:S(2)}) %collective-permute-start.6) | collective-permute-done | bytes 65568 | tf_op jit(solution)/shard_map/ppermute | solution.py:645
  34.6 0.0 collective-permute-done.7.got2
  34.6 3.0 %shard_map.83 = (f32[9,32,128]{2,1,0:T(8,128)S(1)}, f32[256,128]{1,0:T(8,128)S(1)}) custom-call(s32[2,128]{1,0:T(2,128)S(1)} %broadcast_in_dim.2.par, f32[128,128]{1,0:T(8,128)S(1)} %collective-permute-done.6.got1, f32[128,128]{1,0:T(8,128)S(1)} %collective-permute-done.7.got2, f32[192,128]{1,0:T(8,128)S(1)} %collective-permute-done.4.got1.gotx1, ...), custom_call_target="tpu_custom_call" | custom-call | flops 20000000 | bytes 1000000 | tf_op jit(solution)/shard_map/pallas_call | solution.py:739
  37.6 31.0 %all_to_all.11 = f32[256,1,128]{2,1,0:T(1,128)S(1)} all-to-all(f32[256,1,128]{2,1,0:T(1,128)S(1)} %bitcast.8), channel_id=1, replica_groups=mesh['gx'=16,'gy'=16] {'gx','gy'}, dimensions={0} | all-to-all | bytes 262144 | tf_op jit(solution)/shard_map/all_to_all | solution.py:748
  68.6 0.9 %shard_map.84 = (f32[9,32,128]{2,1,0:T(8,128)}, f32[1,1]{1,0:T(1,128)}) custom-call(f32[256,128]{1,0:T(8,128)S(1)} %bitcast.7, f32[9,32,128]{2,1,0:T(8,128)S(1)} %get-tuple-element.64.z_one, f32[9,32,128]{2,1,0:T(8,128)S(1)} %get-tuple-element.65.z_two), custom_call_target="tpu_custom_call" | custom-call | flops 20000000 | bytes 1000000 | tf_op jit(solution)/shard_map/pallas_call | solution.py:749
Async XLA Ops:
  0.8 6.9 %copy-start = (f32[9,9,32,128]{3,2,1,0:T(8,128)S(1)}, f32[9,9,32,128]{3,2,1,0:T(8,128)}, u32[]{:S(2)}) copy-start(f32[9,9,32,128]{3,2,1,0:T(8,128)} %diag.7) | copy-start | bytes 3981316
  0.8 6.9 %copy-start.5 = (s32[32,128]{1,0:T(8,128)S(1)}, s32[32,128]{1,0:T(8,128)}, u32[]{:S(2)}) copy-start(s32[32,128]{1,0:T(8,128)} %wells.7) | copy-start | bytes 49156
  2.4 6.5 %collective-permute-start = (f32[248,128]{1,0:T(8,128)S(1)}, f32[248,128]{1,0:T(8,128)S(1)}, u32[]{:S(2)}, u32[]{:S(2)}) collective-permute-start(f32[248,128]{1,0:T(8,128)S(1)} %get-tuple-element.35), channel_id=1, source_target_pairs={{16,32},{32,16},{48,64},{64,48},{80,96},{96,80},{112,128},{128,112... | collective-permute-start | bytes 380936 | tf_op jit(solution)/shard_map/ppermute | solution.py:645
  3.1 7.4 %copy-start.1 = (f32[9,9,32,128]{3,2,1,0:T(8,128)S(1)}, f32[9,9,32,128]{3,2,1,0:T(8,128)}, u32[]{:S(2)}) copy-start(f32[9,9,32,128]{3,2,1,0:T(8,128)} %couple.5) | copy-start | bytes 3981316
  3.1 7.4 %copy-start.2 = (f32[4,32,128]{2,1,0:T(8,128)S(1)}, f32[4,32,128]{2,1,0:T(8,128)}, u32[]{:S(2)}) copy-start(f32[4,32,128]{2,1,0:T(8,128)} %trans.9) | copy-start | bytes 196612
  3.1 7.4 %copy-start.3 = (f32[9,32,128]{2,1,0:T(8,128)S(1)}, f32[9,32,128]{2,1,0:T(8,128)}, u32[]{:S(2)}) copy-start(f32[9,32,128]{2,1,0:T(8,128)} %weights.5) | copy-start | bytes 442372
  3.1 7.4 %collective-permute-start.1 = (f32[248,128]{1,0:T(8,128)S(1)}, f32[248,128]{1,0:T(8,128)S(1)}, u32[]{:S(2)}, u32[]{:S(2)}) collective-permute-start(f32[248,128]{1,0:T(8,128)S(1)} %get-tuple-element.36), channel_id=1, source_target_pairs={{0,16},{16,0},{32,48},{48,32},{64,80},{80,64},{96,112},{112,96},{1... | collective-permute-start | bytes 380936 | tf_op jit(solution)/shard_map/ppermute | solution.py:645
  10.8 7.4 %collective-permute-start.2 = (f32[192,128]{1,0:T(8,128)S(1)}, f32[192,128]{1,0:T(8,128)S(1)}, u32[]{:S(2)}, u32[]{:S(2)}) collective-permute-start(f32[192,128]{1,0:T(8,128)S(1)} %get-tuple-element.39), channel_id=1, source_target_pairs={{1,2},{2,1},{3,4},{4,3},{5,6},{6,5},{7,8},{8,7},{9,10},{10,9},{11,... | collective-permute-start | bytes 294920 | tf_op jit(solution)/shard_map/ppermute | solution.py:645
  15.8 2.4 %copy-start.4 = (f32[9,32,128]{2,1,0:T(8,128)S(1)}, f32[9,32,128]{2,1,0:T(8,128)}, u32[]{:S(2)}) copy-start(f32[9,32,128]{2,1,0:T(8,128)} %rhs.3) | copy-start | bytes 442372
  15.8 2.4 %collective-permute-start.3 = (f32[192,128]{1,0:T(8,128)S(1)}, f32[192,128]{1,0:T(8,128)S(1)}, u32[]{:S(2)}, u32[]{:S(2)}) collective-permute-start(f32[192,128]{1,0:T(8,128)S(1)} %get-tuple-element.40), channel_id=1, source_target_pairs={{0,1},{1,0},{2,3},{3,2},{4,5},{5,4},{6,7},{7,6},{8,9},{9,8},{10,11... | collective-permute-start | bytes 294920 | tf_op jit(solution)/shard_map/ppermute | solution.py:645
  21.1 4.1 %collective-permute-start.4 = (f32[192,128]{1,0:T(8,128)S(1)}, f32[192,128]{1,0:T(8,128)S(1)}, u32[]{:S(2)}, u32[]{:S(2)}) collective-permute-start(f32[192,128]{1,0:T(8,128)S(1)} %get-tuple-element.46), channel_id=1, source_target_pairs={{16,32},{32,16},{48,64},{64,48},{80,96},{96,80},{112,128},{128,112... | collective-permute-start | bytes 294920 | tf_op jit(solution)/shard_map/ppermute | solution.py:645
  21.8 5.9 %collective-permute-start.5 = (f32[192,128]{1,0:T(8,128)S(1)}, f32[192,128]{1,0:T(8,128)S(1)}, u32[]{:S(2)}, u32[]{:S(2)}) collective-permute-start(f32[192,128]{1,0:T(8,128)S(1)} %get-tuple-element.47), channel_id=1, source_target_pairs={{0,16},{16,0},{32,48},{48,32},{64,80},{80,64},{96,112},{112,96},{1... | collective-permute-start | bytes 294920 | tf_op jit(solution)/shard_map/ppermute | solution.py:645
  27.9 6.7 %collective-permute-start.6 = (f32[128,128]{1,0:T(8,128)S(1)}, f32[128,128]{1,0:T(8,128)S(1)}, u32[]{:S(2)}, u32[]{:S(2)}) collective-permute-start(f32[128,128]{1,0:T(8,128)S(1)} %get-tuple-element.54), channel_id=1, source_target_pairs={{1,2},{2,1},{3,4},{4,3},{5,6},{6,5},{7,8},{8,7},{9,10},{10,9},{11,... | collective-permute-start | bytes 196616 | tf_op jit(solution)/shard_map/ppermute | solution.py:645
  32.6 1.9 %collective-permute-start.7 = (f32[128,128]{1,0:T(8,128)S(1)}, f32[128,128]{1,0:T(8,128)S(1)}, u32[]{:S(2)}, u32[]{:S(2)}) collective-permute-start(f32[128,128]{1,0:T(8,128)S(1)} %get-tuple-element.55), channel_id=1, source_target_pairs={{0,1},{1,0},{2,3},{3,2},{4,5},{5,4},{6,7},{7,6},{8,9},{9,8},{10,11... | collective-permute-start | bytes 196616 | tf_op jit(solution)/shard_map/ppermute | solution.py:645

commit v5 on v4

--- a/solution.py
+++ b/solution.py
@@ -237,67 +237,122 @@
     return jnp.sum(jnp.where(keep, product, 0.0), axis=1, keepdims=True)
 
 
-def pair_sums(values, step):
-    rows, lanes = iotas(values.shape)
-    values = values + jnp.where((rows // step) % 2 == 0, shifted(values, 0, step), shifted(values, 0, -step))
-    return values + jnp.where((lanes // step) % 2 == 0, shifted(values, 1, step), shifted(values, 1, -step))
-
-
-def coarsen_into(coeffs, level):
+def lane_pairs(values, step):
+    lanes = iotas(values.shape)[1]
+    return values + jnp.where((lanes // step) % 2 == 0, lane_roll(values, -step), lane_roll(values, step))
+
+
+def even_rows(ref, half):
+    return ref.at[half][pl.ds(0, ref.shape[1] // 2, stride=2), :]
+
+
+def odd_rows(ref, half):
+    return ref.at[half][pl.ds(1, ref.shape[1] // 2, stride=2), :]
+
+
+def restrict(values, temp, step):
+    result = []
+    for half in range(2):
+        temp[half] = values[half]
+        result.append(lane_pairs(even_rows(temp, half) + odd_rows(temp, half), step))
+    return result
+
+
+def prolong(values, temp):
+    result = []
+    for half in range(2):
+        count = values[half].shape[0]
+        temp.at[half][pl.ds(0, count, stride=2), :] = values[half]
+        temp.at[half][pl.ds(1, count, stride=2), :] = values[half]
+        result.append(temp[half])
+    return result
+
+
+def coarsen_into(fine, coarse, temp, level):
     step = 2**level
-    base, out = (6 * level, 6 * level + 6)
-    rows, lanes = iotas((EX, EY))
-    row_even = (rows // step) % 2 == 0
-    lane_even = (lanes // step) % 2 == 0
-    east, west, north, south = (coeffs[base + d] for d in (EAST, WEST, NORTH, SOUTH))
-    center = coeffs[base] + (jnp.where(row_even, east, west) + jnp.where(lane_even, north, south))
-    center = pair_sums(center, step)
-    coeffs[out + CENTER] = center
-    coeffs[out + SCALE] = RELAX / center
-    coeffs[out + EAST] = pair_sums(jnp.where(row_even, 0.0, east), step)
-    coeffs[out + WEST] = pair_sums(jnp.where(row_even, west, 0.0), step)
-    coeffs[out + NORTH] = pair_sums(jnp.where(lane_even, 0.0, north), step)
-    coeffs[out + SOUTH] = pair_sums(jnp.where(lane_even, south, 0.0), step)
-
-
-def level_apply(values, coeffs, level):
+    for half in range(2):
+        lane_even = (iotas(fine.shape[2:])[1] // step) % 2 == 0
+        center, east, west, north, south = (fine[d, half] for d in range(5))
+        temp[half] = center + jnp.where(lane_even, north, south)
+        total = even_rows(temp, half) + odd_rows(temp, half)
+        temp[half] = east
+        total = total + even_rows(temp, half)
+        coarse[EAST, half] = lane_pairs(odd_rows(temp, half), step)
+        temp[half] = west
+        total = total + odd_rows(temp, half)
+        coarse[WEST, half] = lane_pairs(even_rows(temp, half), step)
+        total = lane_pairs(total, step)
+        coarse[CENTER, half] = total
+        coarse[SCALE, half] = RELAX / total
+        temp[half] = jnp.where(lane_even, 0.0, north)
+        coarse[NORTH, half] = lane_pairs(even_rows(temp, half) + odd_rows(temp, half), step)
+        temp[half] = jnp.where(lane_even, south, 0.0)
+        coarse[SOUTH, half] = lane_pairs(even_rows(temp, half) + odd_rows(temp, half), step)
+
+
+def level_apply(values, coeffs, guarded, level):
     step = 2**level
-    base = 6 * level
-    return coeffs[base + CENTER] * values + (
-        coeffs[base + EAST] * shifted(values, 0, step)
-        + coeffs[base + WEST] * shifted(values, 0, -step)
-        + coeffs[base + NORTH] * shifted(values, 1, step)
-        + coeffs[base + SOUTH] * shifted(values, 1, -step)
-    )
-
-
-def sweep(values, source, coeffs, level):
-    return values + coeffs[6 * level + SCALE] * (source - level_apply(values, coeffs, level))
-
-
-def vcycle(source, coeffs):
-    values0 = coeffs[SCALE] * source
-    source1 = pair_sums(source - level_apply(values0, coeffs, 0), 1)
-    values1 = coeffs[6 + SCALE] * source1
-    source2 = pair_sums(source1 - level_apply(values1, coeffs, 1), 2)
-    values2 = coeffs[12 + SCALE] * source2
+    count = values[0].shape[0]
+    lanes = iotas(values[0].shape)[1]
+    right = [lane_roll(v, -step) for v in values]
+    left = [lane_roll(v, step) for v in values]
+    result = []
+    for half in range(2):
+        v = values[half]
+        guarded[half, pl.ds(8, count), :] = v
+        guarded[half, pl.ds(7, 1), :] = v[count - 1 : count]
+        guarded[half, pl.ds(8 + count, 1), :] = v[0:1]
+        result.append(
+            coeffs[CENTER, half] * v
+            + (
+                coeffs[EAST, half] * guarded[half, pl.ds(9, count), :]
+                + coeffs[WEST, half] * guarded[half, pl.ds(7, count), :]
+                + coeffs[NORTH, half] * jnp.where(lanes >= L - step, right[1 - half], right[half])
+                + coeffs[SOUTH, half] * jnp.where(lanes < step, left[1 - half], left[half])
+            )
+        )
+    return result
+
+
+def sweep(values, source, coeffs, guarded, level):
+    applied = level_apply(values, coeffs, guarded, level)
+    return [v + coeffs[SCALE, h] * (f - a) for h, (v, f, a) in enumerate(zip(values, source, applied))]
+
+
+def difference(source, applied):
+    return [f - a for f, a in zip(source, applied)]
+
+
+def scaled(source, coeffs):
+    return [coeffs[SCALE, h] * f for h, f in enumerate(source)]
+
+
+def vcycle(source, levels, guards, temps):
+    values0 = scaled(source, levels[0])
+    source1 = restrict(difference(source, level_apply(values0, levels[0], guards[0], 0)), temps[0], 1)
+    values1 = scaled(source1, levels[1])
+    source2 = restrict(difference(source1, level_apply(values1, levels[1], guards[1], 1)), temps[1], 2)
+    values2 = scaled(source2, levels[2])
     for _ in range(COARSE_SWEEPS - 1):
-        values2 = sweep(values2, source2, coeffs, 2)
-    values1 = sweep(values1 + values2, source1, coeffs, 1)
-    return sweep(values0 + values1, source, coeffs, 0)
+        values2 = sweep(values2, source2, levels[2], guards[2], 2)
+    values1 = [v + e for v, e in zip(values1, prolong(values2, temps[1]))]
+    values1 = sweep(values1, source1, levels[1], guards[1], 1)
+    values0 = [v + e for v, e in zip(values0, prolong(values1, temps[0]))]
+    return sweep(values0, source, levels[0], guards[0], 0)
 
 
 def ghost_column(packed, start, to_lane, lane):
     return lane_roll(packed, to_lane - (start + lane))
 
 
-def neighbour_sum(values, trans, up_row, down_row, right_col, left_col):
-    rows, lanes = iotas((R, L))
-    east = jnp.where(rows == R - 1, up_row, shifted(values, 0, 1))
-    west = jnp.where(rows == 0, down_row, shifted(values, 0, -1))
+def neighbour_sum(values, trans, guarded, up_row, down_row, right_col, left_col):
+    lanes = iotas((R, L))[1]
+    guarded[pl.ds(8, R), :] = values
+    guarded[pl.ds(7, 1), :] = down_row
+    guarded[pl.ds(8 + R, 1), :] = up_row
     north = jnp.where(lanes == L - 1, right_col, shifted(values, 1, 1))
     south = jnp.where(lanes == 0, left_col, shifted(values, 1, -1))
-    return trans[0] * east + trans[1] * west + trans[2] * north + trans[3] * south
+    return trans[0] * guarded[pl.ds(9, R), :] + trans[1] * guarded[pl.ds(7, R), :] + trans[2] * north + trans[3] * south
 
 
 def ghost_rows(trans, up_row, down_row):
@@ -310,10 +365,10 @@
     return jnp.where(lanes == L - 1, trans[2] * right_col, 0.0) + jnp.where(lanes == 0, trans[3] * left_col, 0.0)
 
 
-def one_step(pressure, vector, edges, col_right, col_left, diag, inverse, couple, trans, boost, z_out):
-    p = pressure[0:R, 0:L]
-    up_row, down_row = (pressure[R : R + 1, 0:L], pressure[EX - 1 : EX, 0:L])
-    far = pressure[0:R, L:EY]
+def one_step(pressure, vector, edges, col_right, col_left, diag, inverse, couple, trans, boost, z_out, around_rows):
+    p = pressure[0][0:R]
+    up_row, down_row = (pressure[0][R : R + 1], pressure[0][EX - 1 : EX])
+    far = pressure[1][0:R]
     right_p, left_p = (lane_roll(far, L - 1), lane_roll(far, 1))
     second = []
     for c in range(NC):
@@ -323,6 +378,7 @@
         around = neighbour_sum(
             couple[c, 0] * p,
             trans,
+            around_rows.at[c],
             edges[pl.ds(c, 1), :] * up_row,
             edges[pl.ds(NC + c, 1), :] * down_row,
             ghost_column(col_right, 64, L - 1, c) * right_p,
@@ -347,7 +403,8 @@
 
 def first_step_kernel(
     par, got1, got2, ext, ext_cols, edges, rhs, trans, weights, wells, diag, inverse, couple, rows_up, rows_down,
-    msg1, msg2, z_out, partial, product, coeffs, cols_right, cols_left, pressure_part, product_cols,
+    msg1, msg2, z_out, partial, product, level0, level1, level2, cols_right, cols_left, pressure_part, product_cols,
+    guard0, guard1, guard2, temp0, temp1, around_rows,
 ):
     rows, lanes = iotas((EX, L))
     right, left = take(par, 1, got1, got2, pl.ds(EX, EX))
@@ -373,19 +430,23 @@
         if k == SOUTH:
             near = jnp.where(lanes == 0, south_own, near)
             far = jnp.where(lanes == 0, south_right, far)
-        field = jnp.concatenate([near, far], axis=1)
         if k == 5:
-            source = field
+            source = [near, far]
         else:
-            coeffs[k] = field
-    coeffs[SCALE] = RELAX / coeffs[CENTER]
-    coarsen_into(coeffs, 0)
-    coarsen_into(coeffs, 1)
-    pressure = vcycle(source, coeffs)
+            level0[k, 0] = near
+            level0[k, 1] = far
+        if k == CENTER:
+            level0[SCALE, 0] = RELAX / near
+            level0[SCALE, 1] = RELAX / far
+    levels = (level0, level1, level2)
+    coarsen_into(level0, level1, temp0, 0)
+    coarsen_into(level1, level2, temp1, 1)
+    pressure = vcycle(source, levels, (guard0, guard1, guard2), (temp0, temp1))
     boost = WELL_BOOST * wells[...].astype(jnp.float32)
     vector = [rhs[c] for c in range(NC)]
     products = one_step(
-        pressure, vector, edges, right[0:R], left[0:R], diag, inverse, couple, trans, boost, z_out
+        pressure, vector, edges, right[0:R], left[0:R], diag, inverse, couple, trans, boost, z_out,
+        around_rows,
     )
     put(par, 0, msg1, msg2, pl.ds(BX_RING, RING_STATIC), rows_up[...], rows_down[...])
     weighed = jnp.zeros((R, L), jnp.float32)
@@ -393,7 +454,7 @@
     parts = []
     for c in range(NC):
         product[c] = products[c]
-        value = -neighbour_sum(products[c], trans, zero, zero, 0.0, 0.0)
+        value = -neighbour_sum(products[c], trans, around_rows.at[c], zero, zero, 0.0, 0.0)
         partial[c] = value
         weighed = weighed + weights[c] * value
         last, first = (slice(R - 1, R), slice(0, 1))
@@ -455,10 +516,10 @@
 
 def row_ring(ring, outward, inward, pressure, row, out_row, own_row, edge_cols, product_row, couple_row, corners, old_corners):
     lanes = iotas((1, L))[1]
-    line = pressure[row : row + 1, :]
-    p = line[:, 0:L]
-    p_right, p_left = (line[:, L : L + 1], line[:, EY - 1 : EY])
-    p_out, p_own = (pressure[out_row : out_row + 1, 0:L], pressure[own_row : own_row + 1, 0:L])
+    near, far = pressure
+    p, beyond = (near[row : row + 1], far[row : row + 1])
+    p_right, p_left = (beyond[:, 0:1], beyond[:, L - 1 : L])
+    p_out, p_own = (near[out_row : out_row + 1], near[own_row : own_row + 1])
     t_out, t_in = (ring(RING_TRANS + outward), ring(RING_TRANS + inward))
     t_right, t_left = (ring(RING_TRANS + 2), ring(RING_TRANS + 3))
     second = []
@@ -509,9 +570,10 @@
 
 
 def second_step_kernel(
-    par, got1, got2, gotx1, gotx2, ext, ext_cols, rows_in, setup_cols, cols_right, cols_left, edges, coeffs, partial,
+    par, got1, got2, gotx1, gotx2, ext, ext_cols, rows_in, setup_cols, cols_right, cols_left, edges,
+    level0, level1, level2, partial,
     product, rhs, trans, wells, diag, inverse, couple,
-    z_out, dots, ring_up, ring_down,
+    z_out, dots, ring_up, ring_down, guard0, guard1, guard2, temp0, temp1, around_rows,
 ):
     rows, lanes = iotas((EX, L))
     right, left = take(par, 1, got1, got2, pl.ds(0, EX))
@@ -526,7 +588,7 @@
         lanes < HALO, right, jnp.where(lanes >= L - HALO, lane_roll(left, L - HALO), 0.0)
     )
     far = far - jnp.where(lanes == 0, far_right, 0.0) - jnp.where(lanes == L - 1, far_left, 0.0)
-    pressure = vcycle(jnp.concatenate([near, far], axis=1), coeffs)
+    pressure = vcycle([near, far], (level0, level1, level2), (guard0, guard1, guard2), (temp0, temp1))
     vector = []
     for c in range(NC):
         columns = ghost_columns(
@@ -535,7 +597,8 @@
         vector.append(partial[c] - columns)
     boost = WELL_BOOST * wells[...].astype(jnp.float32)
     products = one_step(
-        pressure, vector, edges, old_right[0:R], old_left[0:R], diag, inverse, couple, trans, boost, z_out
+        pressure, vector, edges, old_right[0:R], old_left[0:R], diag, inverse, couple, trans, boost, z_out,
+        around_rows,
     )
     up, down = take(par, 0, gotx1, gotx2, pl.ds(BX_RING, 112))
     ring_up[...] = up
@@ -556,9 +619,9 @@
         product_up = product_up + ring_up[pl.ds(NC * k, NC), :] * second_up[k]
         product_down = product_down + ring_down[pl.ds(NC * k, NC), :] * second_down[k]
     pack_right, pack_left = take(par, 1, got1, got2, pl.ds(EX, R))
-    far_p = pressure[:, L:EY]
+    far_p = pressure[1]
     far_up, far_down = (shifted(far_p, 0, 1)[0:R], shifted(far_p, 0, -1)[0:R])
-    far_p, near_p = (far_p[0:R], pressure[0:R, 0:L])
+    far_p, near_p = (far_p[0:R], pressure[0][0:R])
     right_cols = column_ring(
         pack_right, 2, 3, far_p[:, 0:1], far_p[:, 1:2], near_p[:, L - 1 : L], far_up[:, 0:1], far_down[:, 0:1],
         lane_roll(tw[0:R], -2 * NC), lane_roll(packed[0:R], -NC),
@@ -572,7 +635,7 @@
     sums = [jnp.zeros((R, L), jnp.float32) for _ in range(6)]
     for c in range(NC):
         two = -neighbour_sum(
-            products[c], trans, product_up[c : c + 1], product_down[c : c + 1],
+            products[c], trans, around_rows.at[c], product_up[c : c + 1], product_down[c : c + 1],
             ghost_column(right_cols, 0, L - 1, c), ghost_column(left_cols, 0, 0, c),
         )
         zero, one = (rhs[c], vector[c])
@@ -712,13 +775,21 @@
     got_y1, got_y2 = swap(msg_y1, msg_y2, "gy")
 
     fields = shape(NC, R, L)
-    msg_b1, msg_b2, z_one, partial, product, coeffs, cols_right, cols_left, pressure_part, product_cols = call(
+    work = [
+        pltpu.VMEM(dims, jnp.float32)
+        for dims in (
+            (2, EX + 16, L), (2, EX // 2 + 16, L), (2, EX // 4 + 16, L), (2, EX, L), (2, EX // 2, L), (NC, R + 16, L),
+        )
+    ]
+    msg_b1, msg_b2, z_one, partial, product, level0, level1, level2, cols_right, cols_left, pressure_part, product_cols = call(
         first_step_kernel,
         [VMEM()] + [VMEM()] * 14,
         [
-            shape(BX_ROWS, L), shape(BX_ROWS, L), fields, fields, fields, shape(18, EX, EY),
+            shape(BX_ROWS, L), shape(BX_ROWS, L), fields, fields, fields, shape(6, 2, EX, L),
+            shape(6, 2, EX // 2, L), shape(6, 2, EX // 4, L),
             shape(EX, L), shape(EX, L), shape(R, L), shape(R, L),
         ],
+        work,
     )(
         par, got_y1, got_y2, ext, ext_cols, edges, right_side, transmissibility, pressure_weights, well_mask,
         diag_blocks, inverse, couple_blocks, rows_up, rows_down,
@@ -738,12 +809,12 @@
     devices = lax.axis_size("gx") * lax.axis_size("gy")
     z_two, local = call(
         second_step_kernel,
-        [VMEM()] + [VMEM()] * 20,
+        [VMEM()] * 23,
         [fields, shape(devices, L)],
-        [pltpu.VMEM((112, L), jnp.float32), pltpu.VMEM((112, L), jnp.float32)],
+        [pltpu.VMEM((112, L), jnp.float32), pltpu.VMEM((112, L), jnp.float32)] + work,
     )(
-        par, got_c1, got_c2, got_b1, got_b2, ext_b, ext_cols_b, rows_b, ext_cols, cols_right, cols_left, edges, coeffs,
-        vector_b, product, right_side, transmissibility, well_mask, diag_blocks, inverse, couple_blocks,
+        par, got_c1, got_c2, got_b1, got_b2, ext_b, ext_cols_b, rows_b, ext_cols, cols_right, cols_left, edges,
+        level0, level1, level2, vector_b, product, right_side, transmissibility, well_mask, diag_blocks, inverse, couple_blocks,
     )
     gathered = lax.all_to_all(local, ("gx", "gy"), 0, 0, tiled=True)
     answer, estimate = call(finish_kernel, [VMEM()] * 3, [fields, shape(1, 1)])(gathered, z_one, z_two)

time: 69.7 us -> 68.3 us (0.980)
  Pallas kernels: 12.3 us -> 10.9 us
    pallas_call x1, Pallas kernels: 2.9 us -> 2.11 us  [on_device(): call(first_step_kernel, [VMEM()] + [VMEM()] * 14, [shape(BX_ROWS, L), sha...]
where the time goes in v5:
time: 68.3 us; the launch traced here: 68 us
  blocking collectives  31 us (45%)
  starting transfers between devices  19.3 us (28%)
  Pallas kernels  10.9 us (16%)
  waiting for transfers between devices  5.81 us (9%)
  between operations  0.81 us (1%)
    all_to_all x1, blocking collectives, on_device(): gathered = lax.all_to_all(local, ('gx', 'gy'), 0, 0, tiled=True)  31 us
    ppermute x4, starting transfers between devices, swap(): lax.ppermute(first, axis, others)  11.1 us
    ppermute x4, starting transfers between devices, swap(): lax.ppermute(second, axis, pairs)  8.21 us
    ppermute x4, waiting for transfers between devices, swap(): lax.ppermute(second, axis, pairs)  3.97 us
    pallas_call x1, Pallas kernels, on_device(): call(second_step_kernel, [VMEM()] * 23, [fields, shape(devices, L)], [plt...  2.36 us
    pallas_call x1, Pallas kernels, on_device(): pl.pallas_call(ring_kernel, grid=(R // 8,), in_specs=[slab, slab, slab, p...  2.3 us
    pallas_call x1, Pallas kernels, on_device(): call(first_step_kernel, [VMEM()] + [VMEM()] * 14, [shape(BX_ROWS, L), sha...  2.11 us
    ppermute x4, waiting for transfers between devices, swap(): lax.ppermute(first, axis, others)  1.84 us
  transfers between devices with their start and end apart: 8, of which 3 were waited for; matrix products, arithmetic and copies ran while one was open for 0% of the time, Pallas kernels for 5%

profile of v5, /device:TPU:1, one launch (start us, length us, event | category | flops | bytes accessed | tf_op | source)
XLA Modules:
  0.0 68.0 jit_solution(11171524310256714154)
XLA Ops:
  0.6 0.1 pad_add_fusion
  0.7 0.1 broadcast_in_dim.2.par
  0.8 0.0 copy-start
  0.8 0.0 copy-start.5
  0.8 1.6 %shard_map.77 = (f32[248,128]{1,0:T(8,128)S(1)}, f32[248,128]{1,0:T(8,128)S(1)}, f32[192,128]{1,0:T(8,128)S(1)}, f32[32,128]{1,0:T(8,128)S(1)}) custom-call(s32[2,128]{1,0:T(2,128)S(1)} %broadcast_in_dim.2.par, f32[9,32,128]{2,1,0:T(8,128)} %rhs.3, f32[9,9,32,128]{3,2,1,0:T(8,128)} %diag.7, f32[9,9,32,128]{3,2,1,0:T(8,128)} %couple.5, f32[4,32,128]{2,1,0:T(8,128)} %trans.9, ...), custom_call_target="tpu_custom_call" | custom-call | flops 20000000 | bytes 1000000 | tf_op jit(solution)/shard_map/pallas_call | solution.py:719
  2.4 0.7 collective-permute-start
  3.1 0.0 copy-start.1
  3.1 0.0 copy-start.2
  3.1 0.0 copy-start.3
  3.1 4.6 %collective-permute-start.1 = (f32[248,128]{1,0:T(8,128)S(1)}, f32[248,128]{1,0:T(8,128)S(1)}, u32[]{:S(2)}, u32[]{:S(2)}) collective-permute-start(f32[248,128]{1,0:T(8,128)S(1)} %get-tuple-element.38), channel_id=1, source_target_pairs={{0,16},{16,0},{32,48},{48,32},{64,80},{80,64},{96,112},{112,96},{1... | collective-permute-start | bytes 380936 | tf_op jit(solution)/shard_map/ppermute | solution.py:708
  7.7 0.0 copy-done
  7.7 0.0 copy-done.5
  7.7 1.3 %shard_map.78._.inverse = f32[9,9,32,128]{3,2,1,0:T(8,128)S(1)} custom-call(f32[9,9,32,128]{3,2,1,0:T(8,128)S(1)} %copy-done, s32[32,128]{1,0:T(8,128)S(1)} %copy-done.5), custom_call_target="tpu_custom_call" | custom-call | flops 20000000 | bytes 2700000 | tf_op jit(solution)/shard_map/pallas_call | solution.py:744
  9.0 0.0 collective-permute-done.got1
  9.0 1.6 %collective-permute-done.1.got2 = f32[248,128]{1,0:T(8,128)S(1)} collective-permute-done((f32[248,128]{1,0:T(8,128)S(1)}, f32[248,128]{1,0:T(8,128)S(1)}, u32[]{:S(2)}, u32[]{:S(2)}) %collective-permute-start.1) | collective-permute-done | bytes 127008 | tf_op jit(solution)/shard_map/ppermute | solution.py:708
  10.5 0.0 copy-done.1
  10.5 0.0 copy-done.2
  10.5 0.0 copy-done.3
  10.5 0.2 shard_map.79
  10.8 5.0 %collective-permute-start.2 = (f32[192,128]{1,0:T(8,128)S(1)}, f32[192,128]{1,0:T(8,128)S(1)}, u32[]{:S(2)}, u32[]{:S(2)}) collective-permute-start(f32[192,128]{1,0:T(8,128)S(1)} %get-tuple-element.41), channel_id=1, source_target_pairs={{1,2},{2,1},{3,4},{4,3},{5,6},{6,5},{7,8},{8,7},{9,10},{10,9},{11,... | collective-permute-start | bytes 294920 | tf_op jit(solution)/shard_map/ppermute | solution.py:708
  15.8 0.0 copy-start.4
  15.8 0.1 collective-permute-start.3
  15.9 2.3 %shard_map.80 = (f32[32,128]{1,0:T(8,128)S(1)}, f32[32,128]{1,0:T(8,128)S(1)}, f32[104,128]{1,0:T(8,128)S(1)}, f32[104,128]{1,0:T(8,128)S(1)}) custom-call(f32[9,9,32,128]{3,2,1,0:T(8,128)S(1)} %shard_map.78._.inverse, f32[9,9,32,128]{3,2,1,0:T(8,128)S(1)} %copy-done, f32[9,9,32,128]{3,2,1,0:T(8,128)S(1)} %copy-done.1, f32[4,32,128]{2,1,0:T(8,128)S(1)} %copy-done.2, ...), custom_call_target="tpu_custom_call" | custom-call | flops 20000000 | bytes 2700000 | tf_op jit(solution)/shard_map/pallas_call | solution.py:753
  18.2 0.0 collective-permute-done.2.got1
  18.2 0.0 collective-permute-done.3.got2
  18.2 0.0 copy-done.4
  18.2 2.1 %shard_map.81 = (f32[192,128]{1,0:T(8,128)S(1)}, f32[192,128]{1,0:T(8,128)S(1)}, f32[9,32,128]{2,1,0:T(8,128)S(1)}, f32[9,32,128]{2,1,0:T(8,128)S(1)}, f32[9,32,...) custom-call(s32[2,128]{1,0:T(2,128)S(1)} %broadcast_in_dim.2.par, ...), custom_call_target="tpu_custom_call" | custom-call | flops 20000000 | bytes 1000000 | tf_op jit(solution)/shard_map/pallas_call | solution.py:784
  20.3 0.7 collective-permute-start.4
  21.0 3.5 %collective-permute-start.5 = (f32[192,128]{1,0:T(8,128)S(1)}, f32[192,128]{1,0:T(8,128)S(1)}, u32[]{:S(2)}, u32[]{:S(2)}) collective-permute-start(f32[192,128]{1,0:T(8,128)S(1)} %get-tuple-element.49), channel_id=1, source_target_pairs={{0,16},{16,0},{32,48},{48,32},{64,80},{80,64},{96,112},{112,96},{1... | collective-permute-start | bytes 294920 | tf_op jit(solution)/shard_map/ppermute | solution.py:708
  24.5 0.0 collective-permute-done.4.got1.gotx1
  24.5 2.4 %collective-permute-done.5.got2.gotx2 = f32[192,128]{1,0:T(8,128)S(1)} collective-permute-done((f32[192,128]{1,0:T(8,128)S(1)}, f32[192,128]{1,0:T(8,128)S(1)}, u32[]{:S(2)}, u32[]{:S(2)}) %collective-permute-start.5) | collective-permute-done | bytes 98336 | tf_op jit(solution)/shard_map/ppermute | solution.py:708
  26.9 0.2 shard_map.82
  27.1 4.8 %collective-permute-start.6 = (f32[128,128]{1,0:T(8,128)S(1)}, f32[128,128]{1,0:T(8,128)S(1)}, u32[]{:S(2)}, u32[]{:S(2)}) collective-permute-start(f32[128,128]{1,0:T(8,128)S(1)} %get-tuple-element.56), channel_id=1, source_target_pairs={{1,2},{2,1},{3,4},{4,3},{5,6},{6,5},{7,8},{8,7},{9,10},{10,9},{11,... | collective-permute-start | bytes 196616 | tf_op jit(solution)/shard_map/ppermute | solution.py:708
  31.8 0.1 collective-permute-start.7
  31.9 1.8 %collective-permute-done.6.got1 = f32[128,128]{1,0:T(8,128)S(1)} collective-permute-done((f32[128,128]{1,0:T(8,128)S(1)}, f32[128,128]{1,0:T(8,128)S(1)}, u32[]{:S(2)}, u32[]{:S(2)}) %collective-permute-start.6) | collective-permute-done | bytes 65568 | tf_op jit(solution)/shard_map/ppermute | solution.py:708
  33.8 0.0 collective-permute-done.7.got2
  33.8 2.4 %shard_map.83 = (f32[9,32,128]{2,1,0:T(8,128)S(1)}, f32[256,128]{1,0:T(8,128)S(1)}) custom-call(s32[2,128]{1,0:T(2,128)S(1)} %broadcast_in_dim.2.par, f32[128,128]{1,0:T(8,128)S(1)} %collective-permute-done.6.got1, f32[128,128]{1,0:T(8,128)S(1)} %collective-permute-done.7.got2, f32[192,128]{1,0:T(8,128)S(1)} %collective-permute-done.4.got1.gotx1, ...), custom_call_target="tpu_custom_call" | custom-call | flops 20000000 | bytes 1000000 | tf_op jit(solution)/shard_map/pallas_call | solution.py:810
  36.2 31.0 %all_to_all.11 = f32[256,1,128]{2,1,0:T(1,128)S(1)} all-to-all(f32[256,1,128]{2,1,0:T(1,128)S(1)} %bitcast.8), channel_id=1, replica_groups=mesh['gx'=16,'gy'=16] {'gx','gy'}, dimensions={0} | all-to-all | bytes 262144 | tf_op jit(solution)/shard_map/all_to_all | solution.py:819
  67.2 0.9 %shard_map.84 = (f32[9,32,128]{2,1,0:T(8,128)}, f32[1,1]{1,0:T(1,128)}) custom-call(f32[256,128]{1,0:T(8,128)S(1)} %bitcast.7, f32[9,32,128]{2,1,0:T(8,128)S(1)} %get-tuple-element.68.z_one, f32[9,32,128]{2,1,0:T(8,128)S(1)} %get-tuple-element.69.z_two), custom_call_target="tpu_custom_call" | custom-call | flops 20000000 | bytes 1000000 | tf_op jit(solution)/shard_map/pallas_call | solution.py:820
Async XLA Ops:
  0.8 6.9 %copy-start = (f32[9,9,32,128]{3,2,1,0:T(8,128)S(1)}, f32[9,9,32,128]{3,2,1,0:T(8,128)}, u32[]{:S(2)}) copy-start(f32[9,9,32,128]{3,2,1,0:T(8,128)} %diag.7) | copy-start | bytes 3981316
  0.8 6.9 %copy-start.5 = (s32[32,128]{1,0:T(8,128)S(1)}, s32[32,128]{1,0:T(8,128)}, u32[]{:S(2)}) copy-start(s32[32,128]{1,0:T(8,128)} %wells.7) | copy-start | bytes 49156
  2.4 6.5 %collective-permute-start = (f32[248,128]{1,0:T(8,128)S(1)}, f32[248,128]{1,0:T(8,128)S(1)}, u32[]{:S(2)}, u32[]{:S(2)}) collective-permute-start(f32[248,128]{1,0:T(8,128)S(1)} %get-tuple-element.37), channel_id=1, source_target_pairs={{16,32},{32,16},{48,64},{64,48},{80,96},{96,80},{112,128},{128,112... | collective-permute-start | bytes 380936 | tf_op jit(solution)/shard_map/ppermute | solution.py:708
  3.1 7.4 %copy-start.1 = (f32[9,9,32,128]{3,2,1,0:T(8,128)S(1)}, f32[9,9,32,128]{3,2,1,0:T(8,128)}, u32[]{:S(2)}) copy-start(f32[9,9,32,128]{3,2,1,0:T(8,128)} %couple.5) | copy-start | bytes 3981316
  3.1 7.4 %copy-start.2 = (f32[4,32,128]{2,1,0:T(8,128)S(1)}, f32[4,32,128]{2,1,0:T(8,128)}, u32[]{:S(2)}) copy-start(f32[4,32,128]{2,1,0:T(8,128)} %trans.9) | copy-start | bytes 196612
  3.1 7.4 %copy-start.3 = (f32[9,32,128]{2,1,0:T(8,128)S(1)}, f32[9,32,128]{2,1,0:T(8,128)}, u32[]{:S(2)}) copy-start(f32[9,32,128]{2,1,0:T(8,128)} %weights.5) | copy-start | bytes 442372
  3.1 7.4 %collective-permute-start.1 = (f32[248,128]{1,0:T(8,128)S(1)}, f32[248,128]{1,0:T(8,128)S(1)}, u32[]{:S(2)}, u32[]{:S(2)}) collective-permute-start(f32[248,128]{1,0:T(8,128)S(1)} %get-tuple-element.38), channel_id=1, source_target_pairs={{0,16},{16,0},{32,48},{48,32},{64,80},{80,64},{96,112},{112,96},{1... | collective-permute-start | bytes 380936 | tf_op jit(solution)/shard_map/ppermute | solution.py:708
  10.8 7.4 %collective-permute-start.2 = (f32[192,128]{1,0:T(8,128)S(1)}, f32[192,128]{1,0:T(8,128)S(1)}, u32[]{:S(2)}, u32[]{:S(2)}) collective-permute-start(f32[192,128]{1,0:T(8,128)S(1)} %get-tuple-element.41), channel_id=1, source_target_pairs={{1,2},{2,1},{3,4},{4,3},{5,6},{6,5},{7,8},{8,7},{9,10},{10,9},{11,... | collective-permute-start | bytes 294920 | tf_op jit(solution)/shard_map/ppermute | solution.py:708
  15.8 2.4 %copy-start.4 = (f32[9,32,128]{2,1,0:T(8,128)S(1)}, f32[9,32,128]{2,1,0:T(8,128)}, u32[]{:S(2)}) copy-start(f32[9,32,128]{2,1,0:T(8,128)} %rhs.3) | copy-start | bytes 442372
  15.8 2.4 %collective-permute-start.3 = (f32[192,128]{1,0:T(8,128)S(1)}, f32[192,128]{1,0:T(8,128)S(1)}, u32[]{:S(2)}, u32[]{:S(2)}) collective-permute-start(f32[192,128]{1,0:T(8,128)S(1)} %get-tuple-element.42), channel_id=1, source_target_pairs={{0,1},{1,0},{2,3},{3,2},{4,5},{5,4},{6,7},{7,6},{8,9},{9,8},{10,11... | collective-permute-start | bytes 294920 | tf_op jit(solution)/shard_map/ppermute | solution.py:708
  20.3 4.1 %collective-permute-start.4 = (f32[192,128]{1,0:T(8,128)S(1)}, f32[192,128]{1,0:T(8,128)S(1)}, u32[]{:S(2)}, u32[]{:S(2)}) collective-permute-start(f32[192,128]{1,0:T(8,128)S(1)} %get-tuple-element.48), channel_id=1, source_target_pairs={{16,32},{32,16},{48,64},{64,48},{80,96},{96,80},{112,128},{128,112... | collective-permute-start | bytes 294920 | tf_op jit(solution)/shard_map/ppermute | solution.py:708
  21.0 5.9 %collective-permute-start.5 = (f32[192,128]{1,0:T(8,128)S(1)}, f32[192,128]{1,0:T(8,128)S(1)}, u32[]{:S(2)}, u32[]{:S(2)}) collective-permute-start(f32[192,128]{1,0:T(8,128)S(1)} %get-tuple-element.49), channel_id=1, source_target_pairs={{0,16},{16,0},{32,48},{48,32},{64,80},{80,64},{96,112},{112,96},{1... | collective-permute-start | bytes 294920 | tf_op jit(solution)/shard_map/ppermute | solution.py:708
  27.1 6.7 %collective-permute-start.6 = (f32[128,128]{1,0:T(8,128)S(1)}, f32[128,128]{1,0:T(8,128)S(1)}, u32[]{:S(2)}, u32[]{:S(2)}) collective-permute-start(f32[128,128]{1,0:T(8,128)S(1)} %get-tuple-element.56), channel_id=1, source_target_pairs={{1,2},{2,1},{3,4},{4,3},{5,6},{6,5},{7,8},{8,7},{9,10},{10,9},{11,... | collective-permute-start | bytes 196616 | tf_op jit(solution)/shard_map/ppermute | solution.py:708
  31.8 1.9 %collective-permute-start.7 = (f32[128,128]{1,0:T(8,128)S(1)}, f32[128,128]{1,0:T(8,128)S(1)}, u32[]{:S(2)}, u32[]{:S(2)}) collective-permute-start(f32[128,128]{1,0:T(8,128)S(1)} %get-tuple-element.57), channel_id=1, source_target_pairs={{0,1},{1,0},{2,3},{3,2},{4,5},{5,4},{6,7},{7,6},{8,9},{9,8},{10,11... | collective-permute-start | bytes 196616 | tf_op jit(solution)/shard_map/ppermute | solution.py:708

commit v6 on v5

--- a/solution.py
+++ b/solution.py
@@ -18,11 +18,11 @@
 
 AX_EDGE = 6 * R
 AX_COL = AX_EDGE + 24
-AX_ROWS = AX_COL + R
+AX_ROWS = AX_COL + 16
 AY_ROWS = 2 * EX
 BX_EDGE = R
 BX_COL = BX_EDGE + 16
-BX_RING = BX_COL + R
+BX_RING = BX_COL + 8
 BX_ROWS = BX_RING + 112
 RING_EFF, RING_NEXT, RING_TRANS, RING_VECTOR, RING_STATIC = 81, 90, 99, 103, 104
 
@@ -67,6 +67,27 @@
     return packed
 
 
+def fold(values, width, rows, per_group):
+    lanes = iotas((rows, L))[1]
+    blocks = []
+    for start in range(0, values.shape[0], rows * per_group):
+        block = values[start : start + rows]
+        for g in range(1, per_group):
+            first = start + g * rows
+            if first < values.shape[0]:
+                block = jnp.where(lanes >= g * width, lane_roll(values[first : first + rows], g * width), block)
+        blocks.append(block)
+    return blocks[0] if len(blocks) == 1 else jnp.concatenate(blocks, axis=0)
+
+
+def unfold(folded, width, rows, per_group, total):
+    parts = []
+    for g in range(total // rows):
+        block = folded[g // per_group * rows : (g // per_group + 1) * rows]
+        parts.append(lane_roll(block, -(g % per_group) * width))
+    return jnp.concatenate(parts, axis=0)
+
+
 def setup_kernel(
     par, rhs_hbm, diag_hbm, couple_hbm, trans_hbm, weights_hbm, wells_hbm, msg1, msg2, own, cols,
     rhs, diag0, couple0, trans, weights, wells, sems,
@@ -74,36 +95,24 @@
     pairs = (
         (weights_hbm, weights),
         (couple_hbm.at[:, 0:1], couple0),
+        (trans_hbm, trans),
         (diag_hbm.at[:, 0:1], diag0),
-        (trans_hbm, trans),
         (rhs_hbm, rhs),
         (wells_hbm, wells),
     )
     copies = [pltpu.make_async_copy(a, b, sems.at[i]) for i, (a, b) in enumerate(pairs)]
     for copy in copies:
         copy.start()
-    for copy in copies:
+    for copy in copies[:3]:
         copy.wait()
     rows, lanes = iotas((R, L))
-    center = WELL_BOOST * wells[...].astype(jnp.float32) * weights[0]
-    pressure = jnp.zeros((R, L), jnp.float32)
     links = [jnp.zeros((R, L), jnp.float32) for _ in range(4)]
     for c in range(NC):
         w, col = (weights[c], couple0[c, 0])
-        center = center + w * diag0[c, 0]
-        pressure = pressure + w * rhs[c]
         for d, (axis, step) in enumerate(((0, 1), (0, -1), (1, 1), (1, -1))):
             links[d] = links[d] + w * shifted(col, axis, step)
     inside = (rows != R - 1, rows != 0, lanes != L - 1, lanes != 0)
-    fields = [center]
-    for d in range(4):
-        fields.append(jnp.where(inside[d], -trans[d] * links[d], 0.0))
-    fields.append(pressure)
-    for k, field in enumerate(fields):
-        span = pl.ds(k * R, R)
-        own[span, :] = field
-        msg1[span, :] = field
-        msg2[span, :] = field
+    fields = [None] + [jnp.where(inside[d], -trans[d] * links[d], 0.0) for d in range(4)] + [None]
     t_up, t_down = (trans[0, R - 1 : R, :], trans[1, 0:1, :])
     t_right, t_left = (trans[2], trans[3])
     for c in range(NC):
@@ -118,8 +127,22 @@
         parts += [(col, 0, c), (t_left * w, 0, NC + c), (col, L - 1, 2 * NC + c), (t_right * w, L - 1, 3 * NC + c)]
     packed = pack_columns(parts)
     cols[...] = packed
-    msg1[pl.ds(AX_COL, R), :] = packed
-    msg2[pl.ds(AX_COL, R), :] = packed
+    folded = fold(packed, 4 * NC, 8, 3)
+    msg1[pl.ds(AX_COL, 16), :] = folded
+    msg2[pl.ds(AX_COL, 16), :] = folded
+    for copy in copies[3:]:
+        copy.wait()
+    center = WELL_BOOST * wells[...].astype(jnp.float32) * weights[0]
+    pressure = jnp.zeros((R, L), jnp.float32)
+    for c in range(NC):
+        center = center + weights[c] * diag0[c, 0]
+        pressure = pressure + weights[c] * rhs[c]
+    fields[0], fields[5] = (center, pressure)
+    for k, field in enumerate(fields):
+        span = pl.ds(k * R, R)
+        own[span, :] = field
+        msg1[span, :] = field
+        msg2[span, :] = field
 
 
 def inverse_kernel(diag, wells, out):
@@ -206,7 +229,7 @@
             field = jnp.where(rows == 0, west_own, jnp.where(rows == R, west_up, field))
         ext[k] = field
         fields.append(field)
-    up, down = take(par, 0, got1, got2, pl.ds(AX_COL, R))
+    up, down = (unfold(v, 4 * NC, 8, 3, R) for v in take(par, 0, got1, got2, pl.ds(AX_COL, 16)))
     packed = jnp.concatenate([cols[...], up, down], axis=0)
     ext_cols[...] = packed
     to_right = [lane_roll(f, HALO * (k % 4) + HALO) for k, f in enumerate(fields)]
@@ -468,7 +491,7 @@
     for msg in (msg1, msg2):
         msg[pl.ds(0, R), :] = weighed
         msg[pl.ds(BX_EDGE + NC, 16 - NC), :] = blank
-        msg[pl.ds(BX_COL, R), :] = columns
+        msg[pl.ds(BX_COL, 8), :] = fold(columns, 2 * NC, 8, 4)
 
 
 def between_kernel(
@@ -497,18 +520,18 @@
     edge = edge + jnp.where(rows == R, far_up, 0.0) + jnp.where(rows == EX - 1, far_down, 0.0)
     field = field - edge
     ext[...] = field
-    up, down = take(par, 0, got1, got2, pl.ds(BX_COL, R))
+    up, down = (unfold(v, 2 * NC, 8, 4, R) for v in take(par, 0, got1, got2, pl.ds(BX_COL, 8)))
     packed = jnp.concatenate([product_cols[...], up, down], axis=0)
     ext_cols[...] = packed
     near = lanes < HALO
     put(
-        par, 1, msg1, msg2, pl.ds(0, EX),
-        jnp.where(near, lane_roll(field, HALO), lane_roll(packed, HALO - NC)),
-        jnp.where(near, field, lane_roll(packed, HALO)),
+        par, 1, msg1, msg2, pl.ds(0, R),
+        fold(jnp.where(near, lane_roll(field, HALO), lane_roll(packed, HALO - NC)), HALO + NC, R, 3),
+        fold(jnp.where(near, field, lane_roll(packed, HALO)), HALO + NC, R, 3),
     )
     fixed = iotas((R, L))[1] < RING_VECTOR
     put(
-        par, 1, msg1, msg2, pl.ds(EX, R),
+        par, 1, msg1, msg2, pl.ds(R, R),
         jnp.where(fixed, pack_right[...], pack_columns(to_right)),
         jnp.where(fixed, pack_left[...], pack_columns(to_left)),
     )
@@ -576,7 +599,7 @@
     z_out, dots, ring_up, ring_down, guard0, guard1, guard2, temp0, temp1, around_rows,
 ):
     rows, lanes = iotas((EX, L))
-    right, left = take(par, 1, got1, got2, pl.ds(0, EX))
+    right, left = (unfold(v, HALO + NC, R, 3, EX) for v in take(par, 1, got1, got2, pl.ds(0, R)))
     packed, tw = (ext_cols[...], setup_cols[...])
     old_right, old_left = (cols_right[...], cols_left[...])
     own_right = lane_sum(lane_roll(tw, HALO - 3 * NC) * right, HALO)
@@ -618,7 +641,7 @@
     for k in range(1, NC):
         product_up = product_up + ring_up[pl.ds(NC * k, NC), :] * second_up[k]
         product_down = product_down + ring_down[pl.ds(NC * k, NC), :] * second_down[k]
-    pack_right, pack_left = take(par, 1, got1, got2, pl.ds(EX, R))
+    pack_right, pack_left = take(par, 1, got1, got2, pl.ds(R, R))
     far_p = pressure[1]
     far_up, far_down = (shifted(far_p, 0, 1)[0:R], shifted(far_p, 0, -1)[0:R])
     far_p, near_p = (far_p[0:R], pressure[0][0:R])
@@ -799,7 +822,7 @@
     msg_c1, msg_c2, ext_b, ext_cols_b, rows_b, vector_b = call(
         between_kernel,
         [VMEM()] + [VMEM()] * 11,
-        [shape(EX + R, L), shape(EX + R, L), shape(EX, L), shape(EX, L), shape(2 * NC, L), fields],
+        [shape(2 * R, L), shape(2 * R, L), shape(EX, L), shape(EX, L), shape(2 * NC, L), fields],
     )(
         par, got_b1, got_b2, pressure_part, product_cols, product, edges, transmissibility, pressure_weights,
         partial, pack_left, pack_right,

time: 68.3 us -> 67.6 us (0.990)
  waiting for transfers between devices: 5.81 us -> 4.75 us
    ppermute x4, waiting for transfers between devices: 3.97 us -> 3.26 us  [swap(): lax.ppermute(second, axis, pairs)]
where the time goes in v6:
time: 67.6 us; the launch traced here: 67.4 us
  blocking collectives  31.1 us (46%)
  starting transfers between devices  19.6 us (29%)
  Pallas kernels  11 us (16%)
  waiting for transfers between devices  4.75 us (7%)
  between operations  0.8 us (1%)
    all_to_all x1, blocking collectives, on_device(): gathered = lax.all_to_all(local, ('gx', 'gy'), 0, 0, tiled=True)  31.1 us
    ppermute x4, starting transfers between devices, swap(): lax.ppermute(first, axis, others)  11.4 us
    ppermute x4, starting transfers between devices, swap(): lax.ppermute(second, axis, pairs)  8.21 us
    ppermute x4, waiting for transfers between devices, swap(): lax.ppermute(second, axis, pairs)  3.26 us
    pallas_call x1, Pallas kernels, on_device(): call(second_step_kernel, [VMEM()] * 23, [fields, shape(devices, L)], [plt...  2.4 us
    pallas_call x1, Pallas kernels, on_device(): pl.pallas_call(ring_kernel, grid=(R // 8,), in_specs=[slab, slab, slab, p...  2.31 us
    pallas_call x1, Pallas kernels, on_device(): call(first_step_kernel, [VMEM()] + [VMEM()] * 14, [shape(BX_ROWS, L), sha...  2.14 us
    pallas_call x1, Pallas kernels, on_device(): call(setup_kernel, [VMEM()] + [HBM()] * 6, [shape(AX_ROWS, L), shape(AX_R...  1.52 us
  transfers between devices with their start and end apart: 8, of which 3 were waited for; matrix products, arithmetic and copies ran while one was open for 0% of the time, Pallas kernels for 5%

profile of v6, /device:TPU:1, one launch (start us, length us, event | category | flops | bytes accessed | tf_op | source)
XLA Modules:
  0.0 67.4 jit_solution(10380775384720708977)
XLA Ops:
  0.6 0.1 pad_add_fusion
  0.7 0.1 broadcast_in_dim.2.par
  0.8 0.0 copy-start
  0.8 0.0 copy-start.5
  0.8 1.5 %shard_map.77 = (f32[232,128]{1,0:T(8,128)S(1)}, f32[232,128]{1,0:T(8,128)S(1)}, f32[192,128]{1,0:T(8,128)S(1)}, f32[32,128]{1,0:T(8,128)S(1)}) custom-call(s32[2,128]{1,0:T(2,128)S(1)} %broadcast_in_dim.2.par, f32[9,32,128]{2,1,0:T(8,128)} %rhs.3, f32[9,9,32,128]{3,2,1,0:T(8,128)} %diag.7, f32[9,9,32,128]{3,2,1,0:T(8,128)} %couple.5, f32[4,32,128]{2,1,0:T(8,128)} %trans.9, ...), custom_call_target="tpu_custom_call" | custom-call | flops 20000000 | bytes 1000000 | tf_op jit(solution)/shard_map/pallas_call | solution.py:742
  2.3 0.7 collective-permute-start
  3.0 0.0 copy-start.1
  3.0 0.0 copy-start.2
  3.0 0.0 copy-start.3
  3.0 4.6 %collective-permute-start.1 = (f32[232,128]{1,0:T(8,128)S(1)}, f32[232,128]{1,0:T(8,128)S(1)}, u32[]{:S(2)}, u32[]{:S(2)}) collective-permute-start(f32[232,128]{1,0:T(8,128)S(1)} %get-tuple-element.38), channel_id=1, source_target_pairs={{0,16},{16,0},{32,48},{48,32},{64,80},{80,64},{96,112},{112,96},{1... | collective-permute-start | bytes 356360 | tf_op jit(solution)/shard_map/ppermute | solution.py:731
  7.6 0.0 copy-done
  7.6 0.0 copy-done.5
  7.6 1.3 %shard_map.78._.inverse = f32[9,9,32,128]{3,2,1,0:T(8,128)S(1)} custom-call(f32[9,9,32,128]{3,2,1,0:T(8,128)S(1)} %copy-done, s32[32,128]{1,0:T(8,128)S(1)} %copy-done.5), custom_call_target="tpu_custom_call" | custom-call | flops 20000000 | bytes 2700000 | tf_op jit(solution)/shard_map/pallas_call | solution.py:767
  8.9 0.0 collective-permute-done.got1
  8.9 1.4 %collective-permute-done.1.got2 = f32[232,128]{1,0:T(8,128)S(1)} collective-permute-done((f32[232,128]{1,0:T(8,128)S(1)}, f32[232,128]{1,0:T(8,128)S(1)}, u32[]{:S(2)}, u32[]{:S(2)}) %collective-permute-start.1) | collective-permute-done | bytes 118816 | tf_op jit(solution)/shard_map/ppermute | solution.py:731
  10.3 0.0 copy-done.1
  10.3 0.0 copy-done.2
  10.3 0.0 copy-done.3
  10.3 0.2 shard_map.79
  10.5 5.0 %collective-permute-start.2 = (f32[192,128]{1,0:T(8,128)S(1)}, f32[192,128]{1,0:T(8,128)S(1)}, u32[]{:S(2)}, u32[]{:S(2)}) collective-permute-start(f32[192,128]{1,0:T(8,128)S(1)} %get-tuple-element.41), channel_id=1, source_target_pairs={{1,2},{2,1},{3,4},{4,3},{5,6},{6,5},{7,8},{8,7},{9,10},{10,9},{11,... | collective-permute-start | bytes 294920 | tf_op jit(solution)/shard_map/ppermute | solution.py:731
  15.5 0.0 copy-start.4
  15.5 0.1 collective-permute-start.3
  15.6 2.3 %shard_map.80 = (f32[32,128]{1,0:T(8,128)S(1)}, f32[32,128]{1,0:T(8,128)S(1)}, f32[104,128]{1,0:T(8,128)S(1)}, f32[104,128]{1,0:T(8,128)S(1)}) custom-call(f32[9,9,32,128]{3,2,1,0:T(8,128)S(1)} %shard_map.78._.inverse, f32[9,9,32,128]{3,2,1,0:T(8,128)S(1)} %copy-done, f32[9,9,32,128]{3,2,1,0:T(8,128)S(1)} %copy-done.1, f32[4,32,128]{2,1,0:T(8,128)S(1)} %copy-done.2, ...), custom_call_target="tpu_custom_call" | custom-call | flops 20000000 | bytes 2700000 | tf_op jit(solution)/shard_map/pallas_call | solution.py:776
  17.9 0.0 collective-permute-done.2.got1
  17.9 0.0 collective-permute-done.3.got2
  17.9 0.0 copy-done.4
  17.9 2.1 %shard_map.81 = (f32[168,128]{1,0:T(8,128)S(1)}, f32[168,128]{1,0:T(8,128)S(1)}, f32[9,32,128]{2,1,0:T(8,128)S(1)}, f32[9,32,128]{2,1,0:T(8,128)S(1)}, f32[9,32,...) custom-call(s32[2,128]{1,0:T(2,128)S(1)} %broadcast_in_dim.2.par, ...), custom_call_target="tpu_custom_call" | custom-call | flops 20000000 | bytes 1000000 | tf_op jit(solution)/shard_map/pallas_call | solution.py:807
  20.1 0.7 collective-permute-start.4
  20.7 3.5 %collective-permute-start.5 = (f32[168,128]{1,0:T(8,128)S(1)}, f32[168,128]{1,0:T(8,128)S(1)}, u32[]{:S(2)}, u32[]{:S(2)}) collective-permute-start(f32[168,128]{1,0:T(8,128)S(1)} %get-tuple-element.49), channel_id=1, source_target_pairs={{0,16},{16,0},{32,48},{48,32},{64,80},{80,64},{96,112},{112,96},{1... | collective-permute-start | bytes 258056 | tf_op jit(solution)/shard_map/ppermute | solution.py:731
  24.2 0.0 collective-permute-done.4.got1.gotx1
  24.2 1.9 %collective-permute-done.5.got2.gotx2 = f32[168,128]{1,0:T(8,128)S(1)} collective-permute-done((f32[168,128]{1,0:T(8,128)S(1)}, f32[168,128]{1,0:T(8,128)S(1)}, u32[]{:S(2)}, u32[]{:S(2)}) %collective-permute-start.5) | collective-permute-done | bytes 86048 | tf_op jit(solution)/shard_map/ppermute | solution.py:731
  26.1 0.2 shard_map.82
  26.3 5.1 %collective-permute-start.6 = (f32[64,128]{1,0:T(8,128)S(1)}, f32[64,128]{1,0:T(8,128)S(1)}, u32[]{:S(2)}, u32[]{:S(2)}) collective-permute-start(f32[64,128]{1,0:T(8,128)S(1)} %get-tuple-element.56), channel_id=1, source_target_pairs={{1,2},{2,1},{3,4},{4,3},{5,6},{6,5},{7,8},{8,7},{9,10},{10,9},{11,... | collective-permute-start | bytes 98312 | tf_op jit(solution)/shard_map/ppermute | solution.py:731
  31.4 0.1 collective-permute-start.7
  31.5 1.5 %collective-permute-done.6.got1 = f32[64,128]{1,0:T(8,128)S(1)} collective-permute-done((f32[64,128]{1,0:T(8,128)S(1)}, f32[64,128]{1,0:T(8,128)S(1)}, u32[]{:S(2)}, u32[]{:S(2)}) %collective-permute-start.6) | collective-permute-done | bytes 32800 | tf_op jit(solution)/shard_map/ppermute | solution.py:731
  33.0 0.0 collective-permute-done.7.got2
  33.0 2.4 %shard_map.83 = (f32[9,32,128]{2,1,0:T(8,128)S(1)}, f32[256,128]{1,0:T(8,128)S(1)}) custom-call(s32[2,128]{1,0:T(2,128)S(1)} %broadcast_in_dim.2.par, f32[64,128]{1,0:T(8,128)S(1)} %collective-permute-done.6.got1, f32[64,128]{1,0:T(8,128)S(1)} %collective-permute-done.7.got2, f32[168,128]{1,0:T(8,128)S(1)} %collective-permute-done.4.got1.gotx1, ...), custom_call_target="tpu_custom_call" | custom-call | flops 20000000 | bytes 1000000 | tf_op jit(solution)/shard_map/pallas_call | solution.py:833
  35.4 31.1 %all_to_all.11 = f32[256,1,128]{2,1,0:T(1,128)S(1)} all-to-all(f32[256,1,128]{2,1,0:T(1,128)S(1)} %bitcast.8), channel_id=1, replica_groups=mesh['gx'=16,'gy'=16] {'gx','gy'}, dimensions={0} | all-to-all | bytes 262144 | tf_op jit(solution)/shard_map/all_to_all | solution.py:842
  66.5 0.9 %shard_map.84 = (f32[9,32,128]{2,1,0:T(8,128)}, f32[1,1]{1,0:T(1,128)}) custom-call(f32[256,128]{1,0:T(8,128)S(1)} %bitcast.7, f32[9,32,128]{2,1,0:T(8,128)S(1)} %get-tuple-element.68.z_one, f32[9,32,128]{2,1,0:T(8,128)S(1)} %get-tuple-element.69.z_two), custom_call_target="tpu_custom_call" | custom-call | flops 20000000 | bytes 1000000 | tf_op jit(solution)/shard_map/pallas_call | solution.py:843
Async XLA Ops:
  0.8 6.8 %copy-start = (f32[9,9,32,128]{3,2,1,0:T(8,128)S(1)}, f32[9,9,32,128]{3,2,1,0:T(8,128)}, u32[]{:S(2)}) copy-start(f32[9,9,32,128]{3,2,1,0:T(8,128)} %diag.7) | copy-start | bytes 3981316
  0.8 6.8 %copy-start.5 = (s32[32,128]{1,0:T(8,128)S(1)}, s32[32,128]{1,0:T(8,128)}, u32[]{:S(2)}) copy-start(s32[32,128]{1,0:T(8,128)} %wells.7) | copy-start | bytes 49156
  2.3 6.5 %collective-permute-start = (f32[232,128]{1,0:T(8,128)S(1)}, f32[232,128]{1,0:T(8,128)S(1)}, u32[]{:S(2)}, u32[]{:S(2)}) collective-permute-start(f32[232,128]{1,0:T(8,128)S(1)} %get-tuple-element.37), channel_id=1, source_target_pairs={{16,32},{32,16},{48,64},{64,48},{80,96},{96,80},{112,128},{128,112... | collective-permute-start | bytes 356360 | tf_op jit(solution)/shard_map/ppermute | solution.py:731
  3.0 7.3 %copy-start.1 = (f32[9,9,32,128]{3,2,1,0:T(8,128)S(1)}, f32[9,9,32,128]{3,2,1,0:T(8,128)}, u32[]{:S(2)}) copy-start(f32[9,9,32,128]{3,2,1,0:T(8,128)} %couple.5) | copy-start | bytes 3981316
  3.0 7.3 %copy-start.2 = (f32[4,32,128]{2,1,0:T(8,128)S(1)}, f32[4,32,128]{2,1,0:T(8,128)}, u32[]{:S(2)}) copy-start(f32[4,32,128]{2,1,0:T(8,128)} %trans.9) | copy-start | bytes 196612
  3.0 7.2 %copy-start.3 = (f32[9,32,128]{2,1,0:T(8,128)S(1)}, f32[9,32,128]{2,1,0:T(8,128)}, u32[]{:S(2)}) copy-start(f32[9,32,128]{2,1,0:T(8,128)} %weights.5) | copy-start | bytes 442372
  3.0 7.2 %collective-permute-start.1 = (f32[232,128]{1,0:T(8,128)S(1)}, f32[232,128]{1,0:T(8,128)S(1)}, u32[]{:S(2)}, u32[]{:S(2)}) collective-permute-start(f32[232,128]{1,0:T(8,128)S(1)} %get-tuple-element.38), channel_id=1, source_target_pairs={{0,16},{16,0},{32,48},{48,32},{64,80},{80,64},{96,112},{112,96},{1... | collective-permute-start | bytes 356360 | tf_op jit(solution)/shard_map/ppermute | solution.py:731
  10.5 7.4 %collective-permute-start.2 = (f32[192,128]{1,0:T(8,128)S(1)}, f32[192,128]{1,0:T(8,128)S(1)}, u32[]{:S(2)}, u32[]{:S(2)}) collective-permute-start(f32[192,128]{1,0:T(8,128)S(1)} %get-tuple-element.41), channel_id=1, source_target_pairs={{1,2},{2,1},{3,4},{4,3},{5,6},{6,5},{7,8},{8,7},{9,10},{10,9},{11,... | collective-permute-start | bytes 294920 | tf_op jit(solution)/shard_map/ppermute | solution.py:731
  15.5 2.4 %copy-start.4 = (f32[9,32,128]{2,1,0:T(8,128)S(1)}, f32[9,32,128]{2,1,0:T(8,128)}, u32[]{:S(2)}) copy-start(f32[9,32,128]{2,1,0:T(8,128)} %rhs.3) | copy-start | bytes 442372
  15.5 2.4 %collective-permute-start.3 = (f32[192,128]{1,0:T(8,128)S(1)}, f32[192,128]{1,0:T(8,128)S(1)}, u32[]{:S(2)}, u32[]{:S(2)}) collective-permute-start(f32[192,128]{1,0:T(8,128)S(1)} %get-tuple-element.42), channel_id=1, source_target_pairs={{0,1},{1,0},{2,3},{3,2},{4,5},{5,4},{6,7},{7,6},{8,9},{9,8},{10,11... | collective-permute-start | bytes 294920 | tf_op jit(solution)/shard_map/ppermute | solution.py:731
  20.1 4.1 %collective-permute-start.4 = (f32[168,128]{1,0:T(8,128)S(1)}, f32[168,128]{1,0:T(8,128)S(1)}, u32[]{:S(2)}, u32[]{:S(2)}) collective-permute-start(f32[168,128]{1,0:T(8,128)S(1)} %get-tuple-element.48), channel_id=1, source_target_pairs={{16,32},{32,16},{48,64},{64,48},{80,96},{96,80},{112,128},{128,112... | collective-permute-start | bytes 258056 | tf_op jit(solution)/shard_map/ppermute | solution.py:731
  20.7 5.3 %collective-permute-start.5 = (f32[168,128]{1,0:T(8,128)S(1)}, f32[168,128]{1,0:T(8,128)S(1)}, u32[]{:S(2)}, u32[]{:S(2)}) collective-permute-start(f32[168,128]{1,0:T(8,128)S(1)} %get-tuple-element.49), channel_id=1, source_target_pairs={{0,16},{16,0},{32,48},{48,32},{64,80},{80,64},{96,112},{112,96},{1... | collective-permute-start | bytes 258056 | tf_op jit(solution)/shard_map/ppermute | solution.py:731
  26.3 6.7 %collective-permute-start.6 = (f32[64,128]{1,0:T(8,128)S(1)}, f32[64,128]{1,0:T(8,128)S(1)}, u32[]{:S(2)}, u32[]{:S(2)}) collective-permute-start(f32[64,128]{1,0:T(8,128)S(1)} %get-tuple-element.56), channel_id=1, source_target_pairs={{1,2},{2,1},{3,4},{4,3},{5,6},{6,5},{7,8},{8,7},{9,10},{10,9},{11,... | collective-permute-start | bytes 98312 | tf_op jit(solution)/shard_map/ppermute | solution.py:731
  31.4 1.6 %collective-permute-start.7 = (f32[64,128]{1,0:T(8,128)S(1)}, f32[64,128]{1,0:T(8,128)S(1)}, u32[]{:S(2)}, u32[]{:S(2)}) collective-permute-start(f32[64,128]{1,0:T(8,128)S(1)} %get-tuple-element.57), channel_id=1, source_target_pairs={{0,1},{1,0},{2,3},{3,2},{4,5},{5,4},{6,7},{7,6},{8,9},{9,8},{10,11... | collective-permute-start | bytes 98312 | tf_op jit(solution)/shard_map/ppermute | solution.py:731

commit v7 on v6

--- a/solution.py
+++ b/solution.py
@@ -89,8 +89,8 @@
 
 
 def setup_kernel(
-    par, rhs_hbm, diag_hbm, couple_hbm, trans_hbm, weights_hbm, wells_hbm, msg1, msg2, own, cols,
-    rhs, diag0, couple0, trans, weights, wells, sems,
+    par, rhs_hbm, diag_hbm, couple_hbm, trans_hbm, weights_hbm, wells_hbm, msg1, msg2, own, cols, diag0, couple0,
+    rhs, trans, weights, wells, sems,
 ):
     pairs = (
         (weights_hbm, weights),
@@ -734,19 +734,19 @@
 def on_device(right_side, diag_blocks, couple_blocks, transmissibility, pressure_weights, well_mask):
     par = jnp.stack([1 - (lax.axis_index("gx") & 1), 1 - (lax.axis_index("gy") & 1)]).astype(jnp.int32)
     par = jnp.broadcast_to(par[:, None], (2, L))
-    column = pl.BlockSpec((NC, 1, R, L), lambda i: (0, 0, 0, 0))
 
     def whole(*dims):
         return pl.BlockSpec(dims, lambda i: (0,) * len(dims))
 
-    msg_a1, msg_a2, own, cols = call(
+    msg_a1, msg_a2, own, cols, diag0, couple0 = call(
         setup_kernel,
         [VMEM()] + [HBM()] * 6,
-        [shape(AX_ROWS, L), shape(AX_ROWS, L), shape(6 * R, L), shape(R, L)],
+        [
+            shape(AX_ROWS, L), shape(AX_ROWS, L), shape(6 * R, L), shape(R, L), shape(NC, 1, R, L),
+            shape(NC, 1, R, L),
+        ],
         [
             pltpu.VMEM((NC, R, L), jnp.float32),
-            pltpu.VMEM((NC, 1, R, L), jnp.float32),
-            pltpu.VMEM((NC, 1, R, L), jnp.float32),
             pltpu.VMEM((4, R, L), jnp.float32),
             pltpu.VMEM((NC, R, L), jnp.float32),
             pltpu.VMEM((R, L), jnp.int32),
@@ -772,28 +772,31 @@
         out_shape=shape(NC, NC, R, L),
         cost_estimate=pl.CostEstimate(flops=20_000_000, bytes_accessed=2_700_000, transcendentals=0),
         compiler_params=pltpu.CompilerParams(vmem_limit_bytes=30 * 1024 * 1024),
-    )(diag_blocks, well_mask)
+    )(pltpu.with_memory_space_constraint(diag_blocks, pltpu.HBM), well_mask)
     pack_left, pack_right, rows_up, rows_down = pl.pallas_call(
         ring_kernel,
         grid=(R // 8,),
-        in_specs=[slab, slab, slab, pl.BlockSpec((4, 8, L), lambda i: (0, i, 0)), strip],
+        in_specs=[
+            slab, pl.BlockSpec((NC, 1, 8, L), lambda i: (0, 0, i, 0)), slab,
+            pl.BlockSpec((4, 8, L), lambda i: (0, i, 0)), strip,
+        ],
         out_specs=[strip, strip, whole(RING_STATIC, L), whole(RING_STATIC, L)],
         out_shape=[shape(R, L), shape(R, L), shape(RING_STATIC, L), shape(RING_STATIC, L)],
         cost_estimate=pl.CostEstimate(flops=20_000_000, bytes_accessed=2_700_000, transcendentals=0),
         compiler_params=pltpu.CompilerParams(vmem_limit_bytes=30 * 1024 * 1024),
-    )(inverse, diag_blocks, couple_blocks, transmissibility, well_mask)
+    )(inverse, diag0, couple_blocks, transmissibility, well_mask)
 
     msg_y1, msg_y2, ext, ext_cols, edges = pl.pallas_call(
         setup_middle_kernel,
         grid=(1,),
         in_specs=[
-            VMEM(), whole(AX_ROWS, L), whole(AX_ROWS, L), whole(6 * R, L), whole(R, L), column,
+            VMEM(), whole(AX_ROWS, L), whole(AX_ROWS, L), whole(6 * R, L), whole(R, L), whole(NC, 1, R, L),
             whole(4, R, L), whole(NC, R, L), ANY(),
         ],
         out_specs=[whole(AY_ROWS, L), whole(AY_ROWS, L), whole(6, EX, L), whole(EX, L), whole(4 * NC, L)],
         out_shape=[shape(AY_ROWS, L), shape(AY_ROWS, L), shape(6, EX, L), shape(EX, L), shape(4 * NC, L)],
         compiler_params=pltpu.CompilerParams(vmem_limit_bytes=30 * 1024 * 1024),
-    )(par, got_a1, got_a2, own, cols, couple_blocks, transmissibility, pressure_weights, inverse)
+    )(par, got_a1, got_a2, own, cols, couple0, transmissibility, pressure_weights, inverse)
 
     got_y1, got_y2 = swap(msg_y1, msg_y2, "gy")
 
@@ -815,7 +818,7 @@
         work,
     )(
         par, got_y1, got_y2, ext, ext_cols, edges, right_side, transmissibility, pressure_weights, well_mask,
-        diag_blocks, inverse, couple_blocks, rows_up, rows_down,
+        diag0, inverse, couple_blocks, rows_up, rows_down,
     )
 
     got_b1, got_b2 = swap(msg_b1, msg_b2, "gx")
@@ -837,7 +840,7 @@
         [pltpu.VMEM((112, L), jnp.float32), pltpu.VMEM((112, L), jnp.float32)] + work,
     )(
         par, got_c1, got_c2, got_b1, got_b2, ext_b, ext_cols_b, rows_b, ext_cols, cols_right, cols_left, edges,
-        level0, level1, level2, vector_b, product, right_side, transmissibility, well_mask, diag_blocks, inverse, couple_blocks,
+        level0, level1, level2, vector_b, product, right_side, transmissibility, well_mask, diag0, inverse, couple_blocks,
     )
     gathered = lax.all_to_all(local, ("gx", "gy"), 0, 0, tiled=True)
     answer, estimate = call(finish_kernel, [VMEM()] * 3, [fields, shape(1, 1)])(gathered, z_one, z_two)

time: 67.6 us -> 67.6 us (level)
  waiting for transfers between devices: 4.75 us -> 3.37 us
  Pallas kernels: 11 us -> 12.3 us
    pallas_call x1, Pallas kernels: 1.25 us -> 2.78 us  [on_device(): pl.pallas_call(inverse_kernel, grid=(R // 8,), in_specs=[slab, strip], ou...]
    ppermute x4, waiting for transfers between devices: 3.26 us -> 1.88 us  [swap(): lax.ppermute(second, axis, pairs)]
  transfers between devices with their start and end apart: 8 -> 8, of which waited for: 3 -> 2; matrix products, arithmetic and copies ran while one was open for 0% -> 0% of each run, Pallas kernels for 5% -> 7%
where the time goes in v7:
time: 67.6 us; the launch traced here: 67.3 us
  blocking collectives  31.3 us (46%)
  starting transfers between devices  19.4 us (29%)
  Pallas kernels  12.3 us (18%)
  waiting for transfers between devices  3.37 us (5%)
  between operations  0.83 us (1%)
    all_to_all x1, blocking collectives, on_device(): gathered = lax.all_to_all(local, ('gx', 'gy'), 0, 0, tiled=True)  31.3 us
    ppermute x4, starting transfers between devices, swap(): lax.ppermute(first, axis, others)  11.2 us
    ppermute x4, starting transfers between devices, swap(): lax.ppermute(second, axis, pairs)  8.21 us
    pallas_call x1, Pallas kernels, on_device(): pl.pallas_call(inverse_kernel, grid=(R // 8,), in_specs=[slab, strip], ou...  2.78 us
    pallas_call x1, Pallas kernels, on_device(): call(second_step_kernel, [VMEM()] * 23, [fields, shape(devices, L)], [plt...  2.41 us
    pallas_call x1, Pallas kernels, on_device(): call(first_step_kernel, [VMEM()] + [VMEM()] * 14, [shape(BX_ROWS, L), sha...  2.16 us
    pallas_call x1, Pallas kernels, on_device(): pl.pallas_call(ring_kernel, grid=(R // 8,), in_specs=[slab, pl.BlockSpec(...  2.15 us
    ppermute x4, waiting for transfers between devices, swap(): lax.ppermute(second, axis, pairs)  1.88 us
  transfers between devices with their start and end apart: 8, of which 2 were waited for; matrix products, arithmetic and copies ran while one was open for 0% of the time, Pallas kernels for 7%

profile of v7, /device:TPU:1, one launch (start us, length us, event | category | flops | bytes accessed | tf_op | source)
XLA Modules:
  0.0 67.3 jit_solution(6284623548810705220)
XLA Ops:
  0.6 0.1 pad_add_fusion
  0.7 0.1 broadcast_in_dim.2.par
  0.8 0.0 copy-start.4
  0.8 1.4 %shard_map.77 = (f32[232,128]{1,0:T(8,128)S(1)}, f32[232,128]{1,0:T(8,128)S(1)}, f32[192,128]{1,0:T(8,128)S(1)}, f32[32,128]{1,0:T(8,128)S(1)}, f32[9,1,32,128]{...) custom-call(s32[2,128]{1,0:T(2,128)S(1)} %broadcast_in_dim.2.par, f32[9,32,128]{2,1,0:T(8,128)} %rhs.3, ...), custom_call_target="tpu_custom_call" | custom-call | flops 20000000 | bytes 1000000 | tf_op jit(solution)/shard_map/pallas_call | solution.py:741
  2.2 0.7 collective-permute-start
  2.9 0.0 copy-start.1
  2.9 0.0 copy-start.2
  2.9 4.6 %collective-permute-start.1 = (f32[232,128]{1,0:T(8,128)S(1)}, f32[232,128]{1,0:T(8,128)S(1)}, u32[]{:S(2)}, u32[]{:S(2)}) collective-permute-start(f32[232,128]{1,0:T(8,128)S(1)} %get-tuple-element.40), channel_id=1, source_target_pairs={{0,16},{16,0},{32,48},{48,32},{64,80},{80,64},{96,112},{112,96},{1... | collective-permute-start | bytes 356360 | tf_op jit(solution)/shard_map/ppermute | solution.py:731
  7.5 0.0 copy-done.4
  7.5 2.8 %shard_map.78._.inverse = f32[9,9,32,128]{3,2,1,0:T(8,128)S(1)} custom-call(f32[9,9,32,128]{3,2,1,0:T(8,128)} %diag.1, s32[32,128]{1,0:T(8,128)S(1)} %copy-done.4), custom_call_target="tpu_custom_call" | custom-call | flops 20000000 | bytes 2700000 | tf_op jit(solution)/shard_map/pallas_call | solution.py:767
  10.3 0.0 copy-start
  10.3 0.0 collective-permute-done.got1
  10.3 0.0 collective-permute-done.1.got2
  10.3 0.0 copy-done.1
  10.3 0.0 copy-done.2
  10.3 0.2 shard_map.79
  10.6 4.8 %collective-permute-start.2 = (f32[192,128]{1,0:T(8,128)S(1)}, f32[192,128]{1,0:T(8,128)S(1)}, u32[]{:S(2)}, u32[]{:S(2)}) collective-permute-start(f32[192,128]{1,0:T(8,128)S(1)} %get-tuple-element.44), channel_id=1, source_target_pairs={{1,2},{2,1},{3,4},{4,3},{5,6},{6,5},{7,8},{8,7},{9,10},{10,9},{11,... | collective-permute-start | bytes 294920 | tf_op jit(solution)/shard_map/ppermute | solution.py:731
  15.4 0.1 collective-permute-start.3
  15.5 0.0 copy-done
  15.5 0.0 copy-start.3
  15.5 2.2 %shard_map.80 = (f32[32,128]{1,0:T(8,128)S(1)}, f32[32,128]{1,0:T(8,128)S(1)}, f32[104,128]{1,0:T(8,128)S(1)}, f32[104,128]{1,0:T(8,128)S(1)}) custom-call(f32[9,9,32,128]{3,2,1,0:T(8,128)S(1)} %shard_map.78._.inverse, f32[9,1,32,128]{3,2,1,0:T(8,128)S(1)} %get-tuple-element.49.diag, f32[9,9,32,128]{3,2,1,0:T(8,128)S(1)} %copy-done, ...), custom_call_target="tpu_custom_call" | custom-call | flops 20000000 | bytes 2700000 | tf_op jit(solution)/shard_map/pallas_call | solution.py:776
  17.6 0.0 collective-permute-done.2.got1
  17.7 0.0 collective-permute-done.3.got2
  17.7 0.0 copy-done.3
  17.7 2.2 %shard_map.81 = (f32[168,128]{1,0:T(8,128)S(1)}, f32[168,128]{1,0:T(8,128)S(1)}, f32[9,32,128]{2,1,0:T(8,128)S(1)}, f32[9,32,128]{2,1,0:T(8,128)S(1)}, f32[9,32,...) custom-call(s32[2,128]{1,0:T(2,128)S(1)} %broadcast_in_dim.2.par, ...), custom_call_target="tpu_custom_call" | custom-call | flops 20000000 | bytes 1000000 | tf_op jit(solution)/shard_map/pallas_call | solution.py:810
  19.8 0.7 collective-permute-start.4
  20.5 3.5 %collective-permute-start.5 = (f32[168,128]{1,0:T(8,128)S(1)}, f32[168,128]{1,0:T(8,128)S(1)}, u32[]{:S(2)}, u32[]{:S(2)}) collective-permute-start(f32[168,128]{1,0:T(8,128)S(1)} %get-tuple-element.53), channel_id=1, source_target_pairs={{0,16},{16,0},{32,48},{48,32},{64,80},{80,64},{96,112},{112,96},{1... | collective-permute-start | bytes 258056 | tf_op jit(solution)/shard_map/ppermute | solution.py:731
  24.0 0.0 collective-permute-done.4.got1.gotx1
  24.0 1.9 %collective-permute-done.5.got2.gotx2 = f32[168,128]{1,0:T(8,128)S(1)} collective-permute-done((f32[168,128]{1,0:T(8,128)S(1)}, f32[168,128]{1,0:T(8,128)S(1)}, u32[]{:S(2)}, u32[]{:S(2)}) %collective-permute-start.5) | collective-permute-done | bytes 86048 | tf_op jit(solution)/shard_map/ppermute | solution.py:731
  25.8 0.2 shard_map.82
  26.1 5.0 %collective-permute-start.6 = (f32[64,128]{1,0:T(8,128)S(1)}, f32[64,128]{1,0:T(8,128)S(1)}, u32[]{:S(2)}, u32[]{:S(2)}) collective-permute-start(f32[64,128]{1,0:T(8,128)S(1)} %get-tuple-element.60), channel_id=1, source_target_pairs={{1,2},{2,1},{3,4},{4,3},{5,6},{6,5},{7,8},{8,7},{9,10},{10,9},{11,... | collective-permute-start | bytes 98312 | tf_op jit(solution)/shard_map/ppermute | solution.py:731
  31.1 0.1 collective-permute-start.7
  31.2 1.5 %collective-permute-done.6.got1 = f32[64,128]{1,0:T(8,128)S(1)} collective-permute-done((f32[64,128]{1,0:T(8,128)S(1)}, f32[64,128]{1,0:T(8,128)S(1)}, u32[]{:S(2)}, u32[]{:S(2)}) %collective-permute-start.6) | collective-permute-done | bytes 32800 | tf_op jit(solution)/shard_map/ppermute | solution.py:731
  32.7 0.0 collective-permute-done.7.got2
  32.7 2.4 %shard_map.83 = (f32[9,32,128]{2,1,0:T(8,128)S(1)}, f32[256,128]{1,0:T(8,128)S(1)}) custom-call(s32[2,128]{1,0:T(2,128)S(1)} %broadcast_in_dim.2.par, f32[64,128]{1,0:T(8,128)S(1)} %collective-permute-done.6.got1, f32[64,128]{1,0:T(8,128)S(1)} %collective-permute-done.7.got2, f32[168,128]{1,0:T(8,128)S(1)} %collective-permute-done.4.got1.gotx1, ...), custom_call_target="tpu_custom_call" | custom-call | flops 20000000 | bytes 1000000 | tf_op jit(solution)/shard_map/pallas_call | solution.py:836
  35.1 31.3 %all_to_all.11 = f32[256,1,128]{2,1,0:T(1,128)S(1)} all-to-all(f32[256,1,128]{2,1,0:T(1,128)S(1)} %bitcast.8), channel_id=1, replica_groups=mesh['gx'=16,'gy'=16] {'gx','gy'}, dimensions={0} | all-to-all | bytes 262144 | tf_op jit(solution)/shard_map/all_to_all | solution.py:845
  66.4 0.9 %shard_map.84 = (f32[9,32,128]{2,1,0:T(8,128)}, f32[1,1]{1,0:T(1,128)}) custom-call(f32[256,128]{1,0:T(8,128)S(1)} %bitcast.7, f32[9,32,128]{2,1,0:T(8,128)S(1)} %get-tuple-element.72.z_one, f32[9,32,128]{2,1,0:T(8,128)S(1)} %get-tuple-element.73.z_two), custom_call_target="tpu_custom_call" | custom-call | flops 20000000 | bytes 1000000 | tf_op jit(solution)/shard_map/pallas_call | solution.py:846
Async XLA Ops:
  0.8 6.7 %copy-start.4 = (s32[32,128]{1,0:T(8,128)S(1)}, s32[32,128]{1,0:T(8,128)}, u32[]{:S(2)}) copy-start(s32[32,128]{1,0:T(8,128)} %wells.7) | copy-start | bytes 49156
  2.2 8.1 %collective-permute-start = (f32[232,128]{1,0:T(8,128)S(1)}, f32[232,128]{1,0:T(8,128)S(1)}, u32[]{:S(2)}, u32[]{:S(2)}) collective-permute-start(f32[232,128]{1,0:T(8,128)S(1)} %get-tuple-element.39), channel_id=1, source_target_pairs={{16,32},{32,16},{48,64},{64,48},{80,96},{96,80},{112,128},{128,112... | collective-permute-start | bytes 356360 | tf_op jit(solution)/shard_map/ppermute | solution.py:731
  2.9 7.4 %copy-start.1 = (f32[4,32,128]{2,1,0:T(8,128)S(1)}, f32[4,32,128]{2,1,0:T(8,128)}, u32[]{:S(2)}) copy-start(f32[4,32,128]{2,1,0:T(8,128)} %trans.9) | copy-start | bytes 196612
  2.9 7.4 %copy-start.2 = (f32[9,32,128]{2,1,0:T(8,128)S(1)}, f32[9,32,128]{2,1,0:T(8,128)}, u32[]{:S(2)}) copy-start(f32[9,32,128]{2,1,0:T(8,128)} %weights.5) | copy-start | bytes 442372
  2.9 7.4 %collective-permute-start.1 = (f32[232,128]{1,0:T(8,128)S(1)}, f32[232,128]{1,0:T(8,128)S(1)}, u32[]{:S(2)}, u32[]{:S(2)}) collective-permute-start(f32[232,128]{1,0:T(8,128)S(1)} %get-tuple-element.40), channel_id=1, source_target_pairs={{0,16},{16,0},{32,48},{48,32},{64,80},{80,64},{96,112},{112,96},{1... | collective-permute-start | bytes 356360 | tf_op jit(solution)/shard_map/ppermute | solution.py:731
  10.3 5.2 %copy-start = (f32[9,9,32,128]{3,2,1,0:T(8,128)S(1)}, f32[9,9,32,128]{3,2,1,0:T(8,128)}, u32[]{:S(2)}) copy-start(f32[9,9,32,128]{3,2,1,0:T(8,128)} %couple.5) | copy-start | bytes 3981316
  10.6 7.1 %collective-permute-start.2 = (f32[192,128]{1,0:T(8,128)S(1)}, f32[192,128]{1,0:T(8,128)S(1)}, u32[]{:S(2)}, u32[]{:S(2)}) collective-permute-start(f32[192,128]{1,0:T(8,128)S(1)} %get-tuple-element.44), channel_id=1, source_target_pairs={{1,2},{2,1},{3,4},{4,3},{5,6},{6,5},{7,8},{8,7},{9,10},{10,9},{11,... | collective-permute-start | bytes 294920 | tf_op jit(solution)/shard_map/ppermute | solution.py:731
  15.4 2.3 %collective-permute-start.3 = (f32[192,128]{1,0:T(8,128)S(1)}, f32[192,128]{1,0:T(8,128)S(1)}, u32[]{:S(2)}, u32[]{:S(2)}) collective-permute-start(f32[192,128]{1,0:T(8,128)S(1)} %get-tuple-element.45), channel_id=1, source_target_pairs={{0,1},{1,0},{2,3},{3,2},{4,5},{5,4},{6,7},{7,6},{8,9},{9,8},{10,11... | collective-permute-start | bytes 294920 | tf_op jit(solution)/shard_map/ppermute | solution.py:731
  15.5 2.2 %copy-start.3 = (f32[9,32,128]{2,1,0:T(8,128)S(1)}, f32[9,32,128]{2,1,0:T(8,128)}, u32[]{:S(2)}) copy-start(f32[9,32,128]{2,1,0:T(8,128)} %rhs.3) | copy-start | bytes 442372
  19.8 4.1 %collective-permute-start.4 = (f32[168,128]{1,0:T(8,128)S(1)}, f32[168,128]{1,0:T(8,128)S(1)}, u32[]{:S(2)}, u32[]{:S(2)}) collective-permute-start(f32[168,128]{1,0:T(8,128)S(1)} %get-tuple-element.52), channel_id=1, source_target_pairs={{16,32},{32,16},{48,64},{64,48},{80,96},{96,80},{112,128},{128,112... | collective-permute-start | bytes 258056 | tf_op jit(solution)/shard_map/ppermute | solution.py:731
  20.5 5.3 %collective-permute-start.5 = (f32[168,128]{1,0:T(8,128)S(1)}, f32[168,128]{1,0:T(8,128)S(1)}, u32[]{:S(2)}, u32[]{:S(2)}) collective-permute-start(f32[168,128]{1,0:T(8,128)S(1)} %get-tuple-element.53), channel_id=1, source_target_pairs={{0,16},{16,0},{32,48},{48,32},{64,80},{80,64},{96,112},{112,96},{1... | collective-permute-start | bytes 258056 | tf_op jit(solution)/shard_map/ppermute | solution.py:731
  26.1 6.6 %collective-permute-start.6 = (f32[64,128]{1,0:T(8,128)S(1)}, f32[64,128]{1,0:T(8,128)S(1)}, u32[]{:S(2)}, u32[]{:S(2)}) collective-permute-start(f32[64,128]{1,0:T(8,128)S(1)} %get-tuple-element.60), channel_id=1, source_target_pairs={{1,2},{2,1},{3,4},{4,3},{5,6},{6,5},{7,8},{8,7},{9,10},{10,9},{11,... | collective-permute-start | bytes 98312 | tf_op jit(solution)/shard_map/ppermute | solution.py:731
  31.1 1.6 %collective-permute-start.7 = (f32[64,128]{1,0:T(8,128)S(1)}, f32[64,128]{1,0:T(8,128)S(1)}, u32[]{:S(2)}, u32[]{:S(2)}) collective-permute-start(f32[64,128]{1,0:T(8,128)S(1)} %get-tuple-element.61), channel_id=1, source_target_pairs={{0,1},{1,0},{2,3},{3,2},{4,5},{5,4},{6,7},{7,6},{8,9},{9,8},{10,11... | collective-permute-start | bytes 98312 | tf_op jit(solution)/shard_map/ppermute | solution.py:731

commit v8 on v6

--- a/solution.py
+++ b/solution.py
@@ -728,11 +728,13 @@
     peers = lax.axis_size(axis)
     pairs = [(i, i ^ 1) for i in range(peers) if i ^ 1 < peers]
     others = [(i, ((i + 1) ^ 1) - 1) for i in range(1, peers) if ((i + 1) ^ 1) - 1 < peers]
+    if axis == "gy":
+        pairs, others = (others, pairs)
     return (lax.ppermute(first, axis, others), lax.ppermute(second, axis, pairs))
 
 
 def on_device(right_side, diag_blocks, couple_blocks, transmissibility, pressure_weights, well_mask):
-    par = jnp.stack([1 - (lax.axis_index("gx") & 1), 1 - (lax.axis_index("gy") & 1)]).astype(jnp.int32)
+    par = jnp.stack([1 - (lax.axis_index("gx") & 1), lax.axis_index("gy") & 1]).astype(jnp.int32)
     par = jnp.broadcast_to(par[:, None], (2, L))
     column = pl.BlockSpec((NC, 1, R, L), lambda i: (0, 0, 0, 0))
 

time: 67.6 us -> 68 us (level)
    ppermute x4, starting transfers between devices: 8.21 us -> 16.7 us  [swap(): lax.ppermute(second, axis, pairs)]
    ppermute x4, starting transfers between devices: 11.4 us -> 3.04 us  [swap(): lax.ppermute(first, axis, others)]
    ppermute x4, waiting for transfers between devices: 3.26 us -> 4.97 us  [swap(): lax.ppermute(second, axis, pairs)]
    ppermute x4, waiting for transfers between devices: 1.49 us -> 0.01 us  [swap(): lax.ppermute(first, axis, others)]
  transfers between devices with their start and end apart: 8 -> 8, of which waited for: 3 -> 4; matrix products, arithmetic and copies ran while one was open for 0% -> 0% of each run, Pallas kernels for 5% -> 5%
where the time goes in v8:
time: 68 us; the launch traced here: 67.7 us
  blocking collectives  31.2 us (46%)
  starting transfers between devices  19.7 us (29%)
  Pallas kernels  10.9 us (16%)
  waiting for transfers between devices  4.98 us (7%)
  between operations  0.78 us (1%)
    all_to_all x1, blocking collectives, on_device(): gathered = lax.all_to_all(local, ('gx', 'gy'), 0, 0, tiled=True)  31.2 us
    ppermute x4, starting transfers between devices, swap(): lax.ppermute(second, axis, pairs)  16.7 us
    ppermute x4, waiting for transfers between devices, swap(): lax.ppermute(second, axis, pairs)  4.97 us
    ppermute x4, starting transfers between devices, swap(): lax.ppermute(first, axis, others)  3.04 us
    pallas_call x1, Pallas kernels, on_device(): call(second_step_kernel, [VMEM()] * 23, [fields, shape(devices, L)], [plt...  2.4 us
    pallas_call x1, Pallas kernels, on_device(): pl.pallas_call(ring_kernel, grid=(R // 8,), in_specs=[slab, slab, slab, p...  2.3 us
    pallas_call x1, Pallas kernels, on_device(): call(first_step_kernel, [VMEM()] + [VMEM()] * 14, [shape(BX_ROWS, L), sha...  2.13 us
    pallas_call x1, Pallas kernels, on_device(): call(setup_kernel, [VMEM()] + [HBM()] * 6, [shape(AX_ROWS, L), shape(AX_R...  1.52 us
  transfers between devices with their start and end apart: 8, of which 4 were waited for; matrix products, arithmetic and copies ran while one was open for 0% of the time, Pallas kernels for 5%

profile of v8, /device:TPU:1, one launch (start us, length us, event | category | flops | bytes accessed | tf_op | source)
XLA Modules:
  0.0 67.7 jit_solution(10774647795490755855)
XLA Ops:
  0.6 0.1 pad_add_fusion
  0.7 0.1 broadcast_in_dim.2.par
  0.8 0.0 copy-start
  0.8 0.0 copy-start.5
  0.8 1.5 %shard_map.77 = (f32[232,128]{1,0:T(8,128)S(1)}, f32[232,128]{1,0:T(8,128)S(1)}, f32[192,128]{1,0:T(8,128)S(1)}, f32[32,128]{1,0:T(8,128)S(1)}) custom-call(s32[2,128]{1,0:T(2,128)S(1)} %broadcast_in_dim.2.par, f32[9,32,128]{2,1,0:T(8,128)} %rhs.3, f32[9,9,32,128]{3,2,1,0:T(8,128)} %diag.7, f32[9,9,32,128]{3,2,1,0:T(8,128)} %couple.5, f32[4,32,128]{2,1,0:T(8,128)} %trans.9, ...), custom_call_target="tpu_custom_call" | custom-call | flops 20000000 | bytes 1000000 | tf_op jit(solution)/shard_map/pallas_call | solution.py:744
  2.3 0.7 collective-permute-start
  3.0 0.0 copy-start.1
  3.0 0.0 copy-start.2
  3.0 0.0 copy-start.3
  3.0 4.6 %collective-permute-start.1 = (f32[232,128]{1,0:T(8,128)S(1)}, f32[232,128]{1,0:T(8,128)S(1)}, u32[]{:S(2)}, u32[]{:S(2)}) collective-permute-start(f32[232,128]{1,0:T(8,128)S(1)} %get-tuple-element.38), channel_id=1, source_target_pairs={{0,16},{16,0},{32,48},{48,32},{64,80},{80,64},{96,112},{112,96},{1... | collective-permute-start | bytes 356360 | tf_op jit(solution)/shard_map/ppermute | solution.py:733
  7.6 0.0 copy-done
  7.6 0.0 copy-done.5
  7.6 1.3 %shard_map.78._.inverse = f32[9,9,32,128]{3,2,1,0:T(8,128)S(1)} custom-call(f32[9,9,32,128]{3,2,1,0:T(8,128)S(1)} %copy-done, s32[32,128]{1,0:T(8,128)S(1)} %copy-done.5), custom_call_target="tpu_custom_call" | custom-call | flops 20000000 | bytes 2700000 | tf_op jit(solution)/shard_map/pallas_call | solution.py:769
  8.9 0.0 collective-permute-done.got1
  8.9 1.4 %collective-permute-done.1.got2 = f32[232,128]{1,0:T(8,128)S(1)} collective-permute-done((f32[232,128]{1,0:T(8,128)S(1)}, f32[232,128]{1,0:T(8,128)S(1)}, u32[]{:S(2)}, u32[]{:S(2)}) %collective-permute-start.1) | collective-permute-done | bytes 118816 | tf_op jit(solution)/shard_map/ppermute | solution.py:733
  10.3 0.0 copy-done.1
  10.3 0.0 copy-done.2
  10.3 0.0 copy-done.3
  10.3 0.2 shard_map.79
  10.5 1.6 %collective-permute-start.2 = (f32[192,128]{1,0:T(8,128)S(1)}, f32[192,128]{1,0:T(8,128)S(1)}, u32[]{:S(2)}, u32[]{:S(2)}) collective-permute-start(f32[192,128]{1,0:T(8,128)S(1)} %get-tuple-element.41), channel_id=1, source_target_pairs={{0,1},{1,0},{2,3},{3,2},{4,5},{5,4},{6,7},{7,6},{8,9},{9,8},{10,11... | collective-permute-start | bytes 294920 | tf_op jit(solution)/shard_map/ppermute | solution.py:733
  12.1 0.0 copy-start.4
  12.1 3.6 %collective-permute-start.3 = (f32[192,128]{1,0:T(8,128)S(1)}, f32[192,128]{1,0:T(8,128)S(1)}, u32[]{:S(2)}, u32[]{:S(2)}) collective-permute-start(f32[192,128]{1,0:T(8,128)S(1)} %get-tuple-element.42), channel_id=1, source_target_pairs={{1,2},{2,1},{3,4},{4,3},{5,6},{6,5},{7,8},{8,7},{9,10},{10,9},{11,... | collective-permute-start | bytes 294920 | tf_op jit(solution)/shard_map/ppermute | solution.py:733
  15.7 2.3 %shard_map.80 = (f32[32,128]{1,0:T(8,128)S(1)}, f32[32,128]{1,0:T(8,128)S(1)}, f32[104,128]{1,0:T(8,128)S(1)}, f32[104,128]{1,0:T(8,128)S(1)}) custom-call(f32[9,9,32,128]{3,2,1,0:T(8,128)S(1)} %shard_map.78._.inverse, f32[9,9,32,128]{3,2,1,0:T(8,128)S(1)} %copy-done, f32[9,9,32,128]{3,2,1,0:T(8,128)S(1)} %copy-done.1, f32[4,32,128]{2,1,0:T(8,128)S(1)} %copy-done.2, ...), custom_call_target="tpu_custom_call" | custom-call | flops 20000000 | bytes 2700000 | tf_op jit(solution)/shard_map/pallas_call | solution.py:778
  18.0 0.0 collective-permute-done.2.got1
  18.0 0.1 collective-permute-done.3.got2
  18.2 0.0 copy-done.4
  18.2 2.1 %shard_map.81 = (f32[168,128]{1,0:T(8,128)S(1)}, f32[168,128]{1,0:T(8,128)S(1)}, f32[9,32,128]{2,1,0:T(8,128)S(1)}, f32[9,32,128]{2,1,0:T(8,128)S(1)}, f32[9,32,...) custom-call(s32[2,128]{1,0:T(2,128)S(1)} %broadcast_in_dim.2.par, ...), custom_call_target="tpu_custom_call" | custom-call | flops 20000000 | bytes 1000000 | tf_op jit(solution)/shard_map/pallas_call | solution.py:809
  20.3 0.7 collective-permute-start.4
  21.0 3.5 %collective-permute-start.5 = (f32[168,128]{1,0:T(8,128)S(1)}, f32[168,128]{1,0:T(8,128)S(1)}, u32[]{:S(2)}, u32[]{:S(2)}) collective-permute-start(f32[168,128]{1,0:T(8,128)S(1)} %get-tuple-element.49), channel_id=1, source_target_pairs={{0,16},{16,0},{32,48},{48,32},{64,80},{80,64},{96,112},{112,96},{1... | collective-permute-start | bytes 258056 | tf_op jit(solution)/shard_map/ppermute | solution.py:733
  24.4 0.0 collective-permute-done.4.got1.gotx1
  24.4 1.9 %collective-permute-done.5.got2.gotx2 = f32[168,128]{1,0:T(8,128)S(1)} collective-permute-done((f32[168,128]{1,0:T(8,128)S(1)}, f32[168,128]{1,0:T(8,128)S(1)}, u32[]{:S(2)}, u32[]{:S(2)}) %collective-permute-start.5) | collective-permute-done | bytes 86048 | tf_op jit(solution)/shard_map/ppermute | solution.py:733
  26.3 0.2 shard_map.82
  26.6 0.1 collective-permute-start.6
  26.7 5.0 %collective-permute-start.7 = (f32[64,128]{1,0:T(8,128)S(1)}, f32[64,128]{1,0:T(8,128)S(1)}, u32[]{:S(2)}, u32[]{:S(2)}) collective-permute-start(f32[64,128]{1,0:T(8,128)S(1)} %get-tuple-element.57), channel_id=1, source_target_pairs={{1,2},{2,1},{3,4},{4,3},{5,6},{6,5},{7,8},{8,7},{9,10},{10,9},{11,... | collective-permute-start | bytes 98312 | tf_op jit(solution)/shard_map/ppermute | solution.py:733
  31.7 0.0 collective-permute-done.6.got1
  31.7 1.6 %collective-permute-done.7.got2 = f32[64,128]{1,0:T(8,128)S(1)} collective-permute-done((f32[64,128]{1,0:T(8,128)S(1)}, f32[64,128]{1,0:T(8,128)S(1)}, u32[]{:S(2)}, u32[]{:S(2)}) %collective-permute-start.7) | collective-permute-done | bytes 32800 | tf_op jit(solution)/shard_map/ppermute | solution.py:733
  33.3 2.4 %shard_map.83 = (f32[9,32,128]{2,1,0:T(8,128)S(1)}, f32[256,128]{1,0:T(8,128)S(1)}) custom-call(s32[2,128]{1,0:T(2,128)S(1)} %broadcast_in_dim.2.par, f32[64,128]{1,0:T(8,128)S(1)} %collective-permute-done.6.got1, f32[64,128]{1,0:T(8,128)S(1)} %collective-permute-done.7.got2, f32[168,128]{1,0:T(8,128)S(1)} %collective-permute-done.4.got1.gotx1, ...), custom_call_target="tpu_custom_call" | custom-call | flops 20000000 | bytes 1000000 | tf_op jit(solution)/shard_map/pallas_call | solution.py:835
  35.7 31.2 %all_to_all.11 = f32[256,1,128]{2,1,0:T(1,128)S(1)} all-to-all(f32[256,1,128]{2,1,0:T(1,128)S(1)} %bitcast.8), channel_id=1, replica_groups=mesh['gx'=16,'gy'=16] {'gx','gy'}, dimensions={0} | all-to-all | bytes 262144 | tf_op jit(solution)/shard_map/all_to_all | solution.py:844
  66.9 0.9 %shard_map.84 = (f32[9,32,128]{2,1,0:T(8,128)}, f32[1,1]{1,0:T(1,128)}) custom-call(f32[256,128]{1,0:T(8,128)S(1)} %bitcast.7, f32[9,32,128]{2,1,0:T(8,128)S(1)} %get-tuple-element.68.z_one, f32[9,32,128]{2,1,0:T(8,128)S(1)} %get-tuple-element.69.z_two), custom_call_target="tpu_custom_call" | custom-call | flops 20000000 | bytes 1000000 | tf_op jit(solution)/shard_map/pallas_call | solution.py:845
Async XLA Ops:
  0.8 6.8 %copy-start = (f32[9,9,32,128]{3,2,1,0:T(8,128)S(1)}, f32[9,9,32,128]{3,2,1,0:T(8,128)}, u32[]{:S(2)}) copy-start(f32[9,9,32,128]{3,2,1,0:T(8,128)} %diag.7) | copy-start | bytes 3981316
  0.8 6.8 %copy-start.5 = (s32[32,128]{1,0:T(8,128)S(1)}, s32[32,128]{1,0:T(8,128)}, u32[]{:S(2)}) copy-start(s32[32,128]{1,0:T(8,128)} %wells.7) | copy-start | bytes 49156
  2.3 6.5 %collective-permute-start = (f32[232,128]{1,0:T(8,128)S(1)}, f32[232,128]{1,0:T(8,128)S(1)}, u32[]{:S(2)}, u32[]{:S(2)}) collective-permute-start(f32[232,128]{1,0:T(8,128)S(1)} %get-tuple-element.37), channel_id=1, source_target_pairs={{16,32},{32,16},{48,64},{64,48},{80,96},{96,80},{112,128},{128,112... | collective-permute-start | bytes 356360 | tf_op jit(solution)/shard_map/ppermute | solution.py:733
  3.0 7.3 %copy-start.1 = (f32[9,9,32,128]{3,2,1,0:T(8,128)S(1)}, f32[9,9,32,128]{3,2,1,0:T(8,128)}, u32[]{:S(2)}) copy-start(f32[9,9,32,128]{3,2,1,0:T(8,128)} %couple.5) | copy-start | bytes 3981316
  3.0 7.3 %copy-start.2 = (f32[4,32,128]{2,1,0:T(8,128)S(1)}, f32[4,32,128]{2,1,0:T(8,128)}, u32[]{:S(2)}) copy-start(f32[4,32,128]{2,1,0:T(8,128)} %trans.9) | copy-start | bytes 196612
  3.0 7.2 %copy-start.3 = (f32[9,32,128]{2,1,0:T(8,128)S(1)}, f32[9,32,128]{2,1,0:T(8,128)}, u32[]{:S(2)}) copy-start(f32[9,32,128]{2,1,0:T(8,128)} %weights.5) | copy-start | bytes 442372
  3.0 7.2 %collective-permute-start.1 = (f32[232,128]{1,0:T(8,128)S(1)}, f32[232,128]{1,0:T(8,128)S(1)}, u32[]{:S(2)}, u32[]{:S(2)}) collective-permute-start(f32[232,128]{1,0:T(8,128)S(1)} %get-tuple-element.38), channel_id=1, source_target_pairs={{0,16},{16,0},{32,48},{48,32},{64,80},{80,64},{96,112},{112,96},{1... | collective-permute-start | bytes 356360 | tf_op jit(solution)/shard_map/ppermute | solution.py:733
  10.5 7.5 %collective-permute-start.2 = (f32[192,128]{1,0:T(8,128)S(1)}, f32[192,128]{1,0:T(8,128)S(1)}, u32[]{:S(2)}, u32[]{:S(2)}) collective-permute-start(f32[192,128]{1,0:T(8,128)S(1)} %get-tuple-element.41), channel_id=1, source_target_pairs={{0,1},{1,0},{2,3},{3,2},{4,5},{5,4},{6,7},{7,6},{8,9},{9,8},{10,11... | collective-permute-start | bytes 294920 | tf_op jit(solution)/shard_map/ppermute | solution.py:733
  12.1 6.1 %copy-start.4 = (f32[9,32,128]{2,1,0:T(8,128)S(1)}, f32[9,32,128]{2,1,0:T(8,128)}, u32[]{:S(2)}) copy-start(f32[9,32,128]{2,1,0:T(8,128)} %rhs.3) | copy-start | bytes 442372
  12.1 6.1 %collective-permute-start.3 = (f32[192,128]{1,0:T(8,128)S(1)}, f32[192,128]{1,0:T(8,128)S(1)}, u32[]{:S(2)}, u32[]{:S(2)}) collective-permute-start(f32[192,128]{1,0:T(8,128)S(1)} %get-tuple-element.42), channel_id=1, source_target_pairs={{1,2},{2,1},{3,4},{4,3},{5,6},{6,5},{7,8},{8,7},{9,10},{10,9},{11,... | collective-permute-start | bytes 294920 | tf_op jit(solution)/shard_map/ppermute | solution.py:733
  20.3 4.1 %collective-permute-start.4 = (f32[168,128]{1,0:T(8,128)S(1)}, f32[168,128]{1,0:T(8,128)S(1)}, u32[]{:S(2)}, u32[]{:S(2)}) collective-permute-start(f32[168,128]{1,0:T(8,128)S(1)} %get-tuple-element.48), channel_id=1, source_target_pairs={{16,32},{32,16},{48,64},{64,48},{80,96},{96,80},{112,128},{128,112... | collective-permute-start | bytes 258056 | tf_op jit(solution)/shard_map/ppermute | solution.py:733
  21.0 5.3 %collective-permute-start.5 = (f32[168,128]{1,0:T(8,128)S(1)}, f32[168,128]{1,0:T(8,128)S(1)}, u32[]{:S(2)}, u32[]{:S(2)}) collective-permute-start(f32[168,128]{1,0:T(8,128)S(1)} %get-tuple-element.49), channel_id=1, source_target_pairs={{0,16},{16,0},{32,48},{48,32},{64,80},{80,64},{96,112},{112,96},{1... | collective-permute-start | bytes 258056 | tf_op jit(solution)/shard_map/ppermute | solution.py:733
  26.6 5.2 %collective-permute-start.6 = (f32[64,128]{1,0:T(8,128)S(1)}, f32[64,128]{1,0:T(8,128)S(1)}, u32[]{:S(2)}, u32[]{:S(2)}) collective-permute-start(f32[64,128]{1,0:T(8,128)S(1)} %get-tuple-element.56), channel_id=1, source_target_pairs={{0,1},{1,0},{2,3},{3,2},{4,5},{5,4},{6,7},{7,6},{8,9},{9,8},{10,11... | collective-permute-start | bytes 98312 | tf_op jit(solution)/shard_map/ppermute | solution.py:733
  26.7 6.6 %collective-permute-start.7 = (f32[64,128]{1,0:T(8,128)S(1)}, f32[64,128]{1,0:T(8,128)S(1)}, u32[]{:S(2)}, u32[]{:S(2)}) collective-permute-start(f32[64,128]{1,0:T(8,128)S(1)} %get-tuple-element.57), channel_id=1, source_target_pairs={{1,2},{2,1},{3,4},{4,3},{5,6},{6,5},{7,8},{8,7},{9,10},{10,9},{11,... | collective-permute-start | bytes 98312 | tf_op jit(solution)/shard_map/ppermute | solution.py:733
